TPU v7x, 32 devices: a whole 2x2x4 slice. The times are simulated.
32 devices in a mesh: grp: 4 (over y, x), tile: 8 (over z, core).
Axes of the slice: x: 2, y: 2, z: 4, core: 2. Of those that a mesh axis runs over, the one named last changes fastest.
Arguments:
- latents: bfloat16 [4, 1024, 1152], P('grp', 'tile'), may hold values from -6 to 6
- condition: bfloat16 [4, 1152], replicated, may hold values from -6 to 6
- w_modulate: bfloat16 [1152, 3456], P(None, 'grp'), may hold values from -1 to 1
- w_project: bfloat16 [1152, 3456], replicated, may hold values from -0.1875 to 0.1875
- w_output: bfloat16 [1152, 1152], replicated, may hold values from -0.1875 to 0.1875
- detail: int32 [4, 8], P('grp'), may hold values from 0 to 1, as said below
Outputs:
- updated: bfloat16 [4, 1024, 1152], P('grp', 'tile')
Inputs may be any that keep to these rules, and one draw needn't show every extreme that they name: `detail`: at most 2 strips of an image are marked, and at least one.
All inputs are finite; a program needn't handle non-finite values.
Results may differ from a plain program's by a relative error of at most 0.012.
Values may be sent and summed in bfloat16 or wider, within the bound.
No kernel may reach another device: no remote copies, remote signals or barrier semaphores. Data moves between devices by JAX's collectives and lax.ppermute only.
A program may use at most 192 MiB of HBM per device.

v0:
```python
import jax
import jax.numpy as jnp
from jax import lax
from jax.sharding import PartitionSpec as P

HEADS = 16
ROW_TOKENS = 64


def with_halo(cells, sides, width):
    for axis, dim in sides:
        count = lax.axis_size(axis)
        ends = count - 1
        head = lax.slice_in_dim(cells, 0, width, axis=dim)
        tail = lax.slice_in_dim(cells, cells.shape[dim] - width, cells.shape[dim], axis=dim)
        cells = jnp.concatenate(
            [
                lax.ppermute(tail, axis, [(i, (i + 1) % count) for i in range(ends)]),
                cells,
                lax.ppermute(head, axis, [((i + 1) % count, i) for i in range(ends)]),
            ],
            axis=dim,
        )
    return cells


def partial_attend(query, keys, values, valid):
    count = query.shape[0]
    width = query.shape[1]
    heads_q = query.reshape(count, HEADS, width // HEADS)
    heads_k = keys.reshape(keys.shape[0], HEADS, width // HEADS)
    heads_v = values.reshape(values.shape[0], HEADS, width // HEADS)
    scores = jnp.einsum("qhd,khd->hqk", heads_q, heads_k, preferred_element_type=jnp.float32)
    scores = scores / jnp.sqrt(jnp.float32(width // HEADS))
    if valid is not None:
        scores = jnp.where(valid[None, None, :], scores, jnp.float32(-1e30))
    top = jnp.max(scores, axis=2)
    probs = jnp.exp(scores - top[:, :, None])
    total = jnp.sum(probs, axis=2)
    result = jnp.einsum(
        "hqk,khd->qhd", probs.astype(jnp.bfloat16), heads_v, preferred_element_type=jnp.float32
    )
    return (result.reshape(count, width), top, total)


def finish(result, total):
    count = result.shape[0]
    heads = total.shape[0]
    return (result.reshape(count, heads, -1) / jnp.transpose(total)[:, :, None]).reshape(count, -1)


def blend(first, second):
    sum_first, top_first, total_first = first
    sum_second, top_second, total_second = second
    merged = jnp.maximum(top_first, top_second)
    old_factor = jnp.exp(top_first - merged)
    new_factor = jnp.exp(top_second - merged)
    rows = sum_first.shape[0]
    heads = top_first.shape[0]
    scaled = sum_first.reshape(rows, heads, -1) * jnp.transpose(old_factor)[:, :, None]
    scaled = sum_second.reshape(rows, heads, -1) * jnp.transpose(new_factor)[:, :, None]
    return (scaled.reshape(sum_first.shape), merged, total_second * new_factor)


def on_device(latents, condition, w_modulate, w_project, w_output, detail):
    width = w_output.shape[0]
    columns = jnp.dot(condition, w_modulate, preferred_element_type=jnp.float32)
    modulation = lax.all_to_all(columns, "grp", split_axis=0, concat_axis=1, tiled=True)
    shift = modulation[:, :width]
    scale = modulation[:, width : 2 * width]
    gate = modulation[:, 2 * width :]
    tokens = latents[0]
    count = tokens.shape[0]
    values32 = tokens.astype(jnp.float32)
    mean = jnp.mean(values32, axis=1, keepdims=True)
    centered = values32 - mean
    variance = jnp.mean(centered * centered, axis=1, keepdims=True)
    normed = (centered / jnp.sqrt(variance + 1e-06) * (1.0 + scale) + shift).astype(jnp.bfloat16)
    projected = jnp.dot(normed, w_project, preferred_element_type=jnp.float32).astype(jnp.bfloat16)
    query = projected[:, :width]
    pairs = projected[:, width:]
    extended = with_halo(pairs, (("tile", 0),), ROW_TOKENS)
    position = lax.axis_index("tile")
    strips = lax.axis_size("tile")
    valid = jnp.concatenate(
        [
            jnp.broadcast_to(position > 0, (ROW_TOKENS,)),
            jnp.ones((count,), dtype=bool),
            jnp.broadcast_to(position < strips - 1, (ROW_TOKENS,)),
        ]
    )
    near_sum, near_top, near_total = partial_attend(
        query, extended[:, :width], extended[:, width:], valid
    )
    near = finish(near_sum, near_total)
    marks = detail[0]
    mark = lax.dynamic_index_in_dim(marks, position, keepdims=False)
    start_state = (
        jnp.zeros((count, width), jnp.float32),
        jnp.full((HEADS, count), -1e30, jnp.float32),
        jnp.zeros((HEADS, count), jnp.float32),
    )
    piece = lax.all_gather(pairs, "tile", axis=0, tiled=True)

    def update(state):
        return blend(state, partial_attend(query, piece[:, :width], piece[:, width:], None))

    def keep_state(state):
        return state

    whole_sum, whole_top, whole_total = lax.cond(mark > 0, update, keep_state, start_state)
    whole = finish(whole_sum, jnp.where(whole_total > 0, whole_total, 1.0))
    mixed = (near + jnp.where(mark > 0, whole, 0.0)).astype(jnp.bfloat16)
    branch = jnp.dot(mixed, w_output, preferred_element_type=jnp.float32)
    updated = (values32 + gate * branch).astype(jnp.bfloat16)
    return updated[None]


def solution(mesh):
    in_specs = (P("grp", "tile", None), P(), P(None, "grp"), P(), P(), P("grp", None))
    out_specs = P("grp", "tile", None)
    return jax.shard_map(
        on_device, mesh=mesh, in_specs=in_specs, out_specs=out_specs, check_vma=False
    )
```

profile of v0, /device:TPU:5, one launch (start us, length us, event | category | flops | bytes accessed | tf_op | source)
XLA Modules:
  0.0 109.0 jit_solution(16125089351170501005)
XLA Ops:
  6.5 0.0 copy-start
  6.5 0.0 copy-start.3
  6.5 2.3 %convolution_bitcast_fusion.1 = f32[4,1,864]{2,0,1:T(4,128)S(1)} fusion(bf16[4,1152]{1,0:T(4,128)(2,1)} %param.9, bf16[1152,864]{0,1:T(8,128)(2,1)} %param.10), kind=kOutput, calls=%fused_computation.28 | convolution fusion | flops 7962624 | bytes 2013696 | tf_op jit(solution)/shard_map/dot_general | solution.py:67
  8.9 0.6 copy.17
  9.5 3.7 %all-to-all-start = ((f32[4,1,864]{2,1,0:T(1,128)}), f32[4,1,864]{2,1,0:T(1,128)S(1)}, u32[]{:S(2)}, u32[]{:S(2)}) async-start(f32[4,1,864]{2,1,0:T(1,128)} %copy.17), calls=%async_computation | async-start | bytes 28672 | tf_op jit(solution)/shard_map/all_to_all | solution.py:68
  13.2 0.0 all-gather.2.cloned.1.call-start
  13.2 1.1 convert_reduce_fusion
  14.3 0.0 copy-done.3
  14.3 0.2 fusion.31
  14.5 1.3 %all-to-all-done = f32[4,1,864]{2,1,0:T(1,128)S(1)} async-done(((f32[4,1,864]{2,1,0:T(1,128)}), f32[4,1,864]{2,1,0:T(1,128)S(1)}, u32[]{:S(2)}, u32[]{:S(2)}) %all-to-all-start) | async-done | bytes 13856 | tf_op jit(solution)/shard_map/all_to_all | solution.py:68
  15.9 0.1 all_to_all.14
  16.0 4.7 %convolution_convert_fusion = bf16[128,3456]{1,0:T(8,128)(2,1)S(1)} fusion(bf16[1152,3456]{1,0:T(8,128)(2,1)} %param.11, bf16[1,128,1152]{2,1,0:T(8,128)(2,1)S(1)} %copy-done.3, f32[1152]{0:T(1024)S(1)} %get-tuple-element.22, f32[1152]{0:T(1024)S(1)} %get-tuple-element.23, f32[128]{0:T(128)S(1)} %add_sqrt_fusion, f32[128]{0:T(128)S(1)} %broadcast_multiply_fusion), kind=kOutput, calls=%fused_computation.15 | convolution fusion | flops 1020542976 | bytes 9152512 | tf_op jit(solution)/shard_map/dot_general | solution.py:79
  20.8 0.0 copy-start.5
  20.8 0.9 copy-done.5
  21.7 0.0 copy-start.7
  21.7 0.9 slice.50
  22.5 0.0 copy-start.2
  22.5 0.0 all-gather.2.cloned.1.call-update
  22.6 2.0 %fusion.49 = (bf16[64,2304]{1,0:T(8,128)(2,1)}, bf16[64,2304]{1,0:T(8,128)(2,1)}) fusion(bf16[128,3456]{1,0:T(8,128)(2,1)} %copy-done.5), kind=kLoop, calls=%fused_computation.64 | loop fusion | bytes 1179648 | tf_op jit(solution)/shard_map/slice | solution.py:15
  24.5 5.0 %collective-permute-start = (bf16[64,2304]{1,0:T(8,128)(2,1)}, bf16[64,2304]{1,0:T(8,128)(2,1)}, u32[]{:S(2)}, u32[]{:S(2)}) collective-permute-start(bf16[64,2304]{1,0:T(8,128)(2,1)} %get-tuple-element.30), channel_id=1, source_target_pairs={{0,1},{1,2},{2,3},{3,4},{4,5},{5,6},{6,7},{8,9},{9,10},{10,11},{11... | collective-permute-start | bytes 884744 | tf_op jit(solution)/shard_map/ppermute | solution.py:18
  29.5 1.9 %collective-permute-start.1 = (bf16[64,2304]{1,0:T(8,128)(2,1)}, bf16[64,2304]{1,0:T(8,128)(2,1)}, u32[]{:S(2)}, u32[]{:S(2)}) collective-permute-start(bf16[64,2304]{1,0:T(8,128)(2,1)} %get-tuple-element.31), channel_id=1, source_target_pairs={{1,0},{2,1},{3,2},{4,3},{5,4},{6,5},{7,6},{9,8},{10,9},{11,10},{12... | collective-permute-start | bytes 884744 | tf_op jit(solution)/shard_map/ppermute | solution.py:20
  31.5 0.0 copy-done.7
  31.5 0.7 fusion.50
  32.9 0.1 pad_add_fusion
  32.9 1.8 %slice.53 = bf16[128,1152]{1,0:T(8,128)(2,1)} slice(bf16[128,3456]{1,0:T(8,128)(2,1)} %copy-done.5), slice={[0:128], [0:1152]} | slice | bytes 589824 | tf_op jit(solution)/shard_map/slice | solution.py:80
  34.7 1.8 %copy.19 = bf16[128,1152]{0,1:T(8,128)(2,1)} copy(bf16[128,1152]{1,0:T(8,128)(2,1)} %slice.53) | data formatting | bytes 589824 | tf_op jit(solution)/shard_map/slice | solution.py:80
  36.6 0.0 collective-permute-done
  36.6 13.5 %collective-permute-done.1 = bf16[64,2304]{1,0:T(8,128)(2,1)} collective-permute-done((bf16[64,2304]{1,0:T(8,128)(2,1)}, bf16[64,2304]{1,0:T(8,128)(2,1)}, u32[]{:S(2)}, u32[]{:S(2)}) %collective-permute-start.1) | collective-permute-done | bytes 294944 | tf_op jit(solution)/shard_map/ppermute | solution.py:20
  50.0 0.0 copy-done.2
  50.0 1.1 %pad_maximum_fusion = bf16[256,2304]{1,0:T(8,128)(2,1)S(1)} fusion(bf16[64,2304]{1,0:T(8,128)(2,1)} %collective-permute-done.1, bf16[128,2304]{1,0:T(8,128)(2,1)S(1)} %copy-done.2, bf16[64,2304]{1,0:T(8,128)(2,1)} %collective-permute-done), kind=kLoop, calls=%fused_computation.27 | loop fusion | flops 3538944 | bytes 2359296 | tf_op jit(solution)/shard_map/concatenate | solution.py:16
  51.2 1.1 %fusion.48 = (bf16[256,1152]{1,0:T(8,128)(2,1)}, bf16[256,1152]{1,0:T(8,128)(2,1)}) fusion(bf16[256,2304]{1,0:T(8,128)(2,1)S(1)} %pad_maximum_fusion), kind=kLoop, calls=%fused_computation.63 | loop fusion | bytes 2359296 | tf_op jit(solution)/shard_map/slice | solution.py:93
  52.3 1.3 %copy.20 = bf16[256,1152]{0,1:T(8,128)(2,1)S(1)} copy(bf16[256,1152]{1,0:T(8,128)(2,1)} %get-tuple-element.28) | data formatting | bytes 1179648 | tf_op jit(solution)/shard_map/slice | solution.py:93
  53.6 2.1 %copy.18 = bf16[256,1152]{0,1:T(8,128)(2,1)} copy(bf16[256,1152]{1,0:T(8,128)(2,1)} %get-tuple-element.29) | data formatting | bytes 1179648 | tf_op jit(solution)/shard_map/slice | solution.py:93
  55.7 0.0 copy-start.6
  55.8 1.6 %fusion.19 = (f32[16,128]{1,0:T(8,128)S(1)}, f32[16,128,256]{2,1,0:T(8,128)S(1)}) fusion(pred[256]{0:T(512)(128)(4,1)S(1)} %pad_add_fusion, bf16[128,16,72]{0,2,1:T(8,128)(2,1)} %bitcast.68, bf16[256,16,72]{0,2,1:T(8,128)(2,1)S(1)} %bitcast.67), kind=kOutput, calls=%fused_computation.22 | convolution fusion | flops 77068288 | bytes 2990336 | tf_op jit(solution)/shard_map/qhd,khd->hqk/dot_general | solution.py:33
  57.4 0.9 fusion.20
  58.3 0.0 copy-done.6
  58.3 0.0 copy-start.4
  58.3 1.4 %fusion.22 = f32[128,16,72]{0,2,1:T(8,128)} fusion(bf16[256,16,72]{0,2,1:T(8,128)(2,1)S(1)} %bitcast.70, f32[16,128,256]{2,1,0:T(8,128)S(1)} %get-tuple-element.33, f32[16,128]{1,0:T(8,128)S(1)} %get-tuple-element.32, pred[256]{0:T(512)(128)(4,1)S(1)} %pad_add_fusion, f32[128,16]{0,1:T(8,128)S(1)} %bitcast.71), kind=kOutput, calls=%fused_computation.26 | convolution fusion | flops 77742080 | bytes 3293440 | tf_op jit(solution)/shard_map/hqk,khd->qhd/dot_general | solution.py:40
  59.8 19.3 %all-gather.2.cloned.1.call-done = bf16[1024,2304]{1,0:T(8,128)(2,1)} async-done(((bf16[128,2304]{1,0:T(8,128)(2,1)}), bf16[1024,2304]{1,0:T(8,128)(2,1)}) %all-gather.2.cloned.1.call-update) | async-done | bytes 4718608 | tf_op jit(solution)/shard_map/all_gather | solution.py:103
  79.0 0.0 copy-done.4
  79.0 19.7 %conditional.1 = (f32[128,1152]{0,1:T(8,128)}, f32[16,128]{1,0:T(8,128)S(1)}) conditional(s32[]{:T(128)} %convert_element_type.32, () %tuple.13, (bf16[128,1152]{1,0:T(8,128)(2,1)S(1)}, bf16[1024,2304]{1,0:T(8,128)(2,1)}) %tuple.29), branch_computations={%region_4.5_spmd, %region_5.8_spmd} | conditional | flops 620910592 | bytes 59752492 | solution.py:111
  79.0 6.7 %copy.22 = bf16[1024,2304]{0,1:T(8,128)(2,1)} copy(bf16[1024,2304]{1,0:T(8,128)(2,1)} %get-tuple-element.20) | data formatting | bytes 9437184 | tf_op jit(solution)/shard_map
  85.7 5.1 %fusion.47 = (bf16[1024,1152]{0,1:T(8,128)(2,1)}, bf16[1024,1152]{0,1:T(8,128)(2,1)}) fusion(bf16[1024,2304]{0,1:T(8,128)(2,1)} %copy.22), kind=kLoop, calls=%fused_computation.62 | loop fusion | bytes 9437184 | tf_op jit(solution)/shard_map/cond/branch_1_fun/slice | solution.py:106
  90.9 0.2 copy.21
  91.1 0.0 copy-start.1
  91.1 3.2 %multiply_reduce_fusion = (f32[16,128]{1,0:T(8,128)S(1)}, f32[16,128,1024]{2,1,0:T(8,128)S(1)}) fusion(bf16[128,16,72]{0,2,1:T(8,128)(2,1)S(1)} %bitcast.69, bf16[1024,16,72]{0,2,1:T(8,128)(2,1)} %bitcast.66), kind=kOutput, calls=%fused_computation.1 | convolution fusion | flops 306182144 | bytes 11051008 | tf_op jit(solution)/shard_map/cond/branch_1_fun/qhd,khd->hqk/dot_general | solution.py:33
  94.3 0.0 copy-done.1
  94.3 2.7 %fusion.9 = f32[128,16,72]{0,2,1:T(8,128)} fusion(bf16[1024,16,72]{0,2,1:T(8,128)(2,1)S(1)} %bitcast.65, f32[16,128,1024]{2,1,0:T(8,128)S(1)} %get-tuple-element.27, f32[16,128]{1,0:T(8,128)S(1)} %get-tuple-element.26, f32[128,16]{0,1:T(8,128)S(1)} %fusion.12), kind=kOutput, calls=%fused_computation.8 | convolution fusion | flops 308428800 | bytes 11354112 | tf_op jit(solution)/shard_map/cond/branch_1_fun/hqk,khd->qhd/dot_general | solution.py:40
  97.0 1.8 %fusion = f32[16,128]{1,0:T(8,128)S(1)} fusion(f32[16,128,1024]{2,1,0:T(8,128)S(1)} %get-tuple-element.27, f32[16,128]{1,0:T(8,128)S(1)} %get-tuple-element.26), kind=kLoop, calls=%fused_computation.2 | loop fusion | flops 6289408 | bytes 8404992 | tf_op jit(solution)/shard_map/cond/branch_1_fun/reduce_sum | solution.py:39
  98.8 2.0 %fusion.37 = bf16[128,1152]{0,1:T(8,128)(2,1)S(1)} fusion(f32[128,1152]{0,1:T(8,128)} %get-tuple-element.13, f32[128,16,72]{0,2,1:T(8,128)} %fusion.22, f32[128,16]{0,1:T(8,128)S(1)} %fusion.43, pred[]{:T(512)} %bitcast.14), kind=kLoop, calls=%fused_computation.45 | loop fusion | flops 589824 | bytes 1482753 | tf_op jit(solution)/shard_map/convert_element_type | solution.py:113
  100.8 0.0 copy-done
  100.8 1.3 %fusion.18 = bf16[1,128,1152]{2,1,0:T(8,128)(2,1)} fusion(bf16[128,1152]{0,1:T(8,128)(2,1)S(1)} %fusion.37, bf16[1152,1152]{1,0:T(8,128)(2,1)S(1)} %copy-done, bf16[1,128,1152]{2,1,0:T(8,128)(2,1)S(1)} %copy-done.3, f32[1152]{0:T(1024)S(1)} %get-tuple-element.21), kind=kOutput, calls=%fused_computation.19 | convolution fusion | flops 340328448 | bytes 3543552 | tf_op jit(solution)/shard_map/dot_general | solution.py:114
  (10 shorter events, 0.1 us)
Async XLA Ops:
  6.5 94.3 %copy-start = (bf16[1152,1152]{1,0:T(8,128)(2,1)S(1)}, bf16[1152,1152]{1,0:T(8,128)(2,1)}, u32[]{:S(2)}) copy-start(bf16[1152,1152]{1,0:T(8,128)(2,1)} %param.12) | copy-start | bytes 7962628
  6.5 7.7 %copy-start.3 = (bf16[1,128,1152]{2,1,0:T(8,128)(2,1)S(1)}, bf16[1,128,1152]{2,1,0:T(8,128)(2,1)}, u32[]{:S(2)}) copy-start(bf16[1,128,1152]{2,1,0:T(8,128)(2,1)} %param.8) | copy-start | bytes 884740
  9.5 6.3 %all-to-all-start = ((f32[4,1,864]{2,1,0:T(1,128)}), f32[4,1,864]{2,1,0:T(1,128)S(1)}, u32[]{:S(2)}, u32[]{:S(2)}) async-start(f32[4,1,864]{2,1,0:T(1,128)} %copy.17), calls=%async_computation | async-start | bytes 28672 | tf_op jit(solution)/shard_map/all_to_all | solution.py:68
  13.2 65.8 %all-gather.2.cloned.1.call-start = ((), (), s32[]{:S(2)}) async-start(), calls=%async_computation.1 | async-start | bytes 5308416 | tf_op jit(solution)/shard_map/all_gather | solution.py:103
  20.8 0.9 copy-start.5
  21.7 9.8 %copy-start.7 = (s32[1,8]{1,0:T(1,128)S(1)}, s32[1,8]{1,0:T(1,128)}, u32[]{:S(2)}) copy-start(s32[1,8]{1,0:T(1,128)} %param.13) | copy-start | bytes 100
  22.5 27.5 %copy-start.2 = (bf16[128,2304]{1,0:T(8,128)(2,1)S(1)}, bf16[128,2304]{1,0:T(8,128)(2,1)}, u32[]{:S(2)}) copy-start(bf16[128,2304]{1,0:T(8,128)(2,1)} %slice.50) | copy-start | bytes 1769476
  24.5 12.0 %collective-permute-start = (bf16[64,2304]{1,0:T(8,128)(2,1)}, bf16[64,2304]{1,0:T(8,128)(2,1)}, u32[]{:S(2)}, u32[]{:S(2)}) collective-permute-start(bf16[64,2304]{1,0:T(8,128)(2,1)} %get-tuple-element.30), channel_id=1, source_target_pairs={{0,1},{1,2},{2,3},{3,4},{4,5},{5,6},{6,7},{8,9},{9,10},{10,11},{11... | collective-permute-start | bytes 884744 | tf_op jit(solution)/shard_map/ppermute | solution.py:18
  29.5 20.5 %collective-permute-start.1 = (bf16[64,2304]{1,0:T(8,128)(2,1)}, bf16[64,2304]{1,0:T(8,128)(2,1)}, u32[]{:S(2)}, u32[]{:S(2)}) collective-permute-start(bf16[64,2304]{1,0:T(8,128)(2,1)} %get-tuple-element.31), channel_id=1, source_target_pairs={{1,0},{2,1},{3,2},{4,3},{5,4},{6,5},{7,6},{9,8},{10,9},{11,10},{12... | collective-permute-start | bytes 884744 | tf_op jit(solution)/shard_map/ppermute | solution.py:20
  55.7 2.6 %copy-start.6 = (bf16[256,1152]{0,1:T(8,128)(2,1)S(1)}, bf16[256,1152]{0,1:T(8,128)(2,1)}, u32[]{:S(2)}) copy-start(bf16[256,1152]{0,1:T(8,128)(2,1)} %copy.18) | copy-start | bytes 1769476
  58.3 20.7 %copy-start.4 = (bf16[128,1152]{1,0:T(8,128)(2,1)S(1)}, bf16[128,1152]{1,0:T(8,128)(2,1)}, u32[]{:S(2)}) copy-start(bf16[128,1152]{1,0:T(8,128)(2,1)} %slice.53) | copy-start | bytes 884740
  91.1 3.2 %copy-start.1 = (bf16[1024,1152]{0,1:T(8,128)(2,1)S(1)}, bf16[1024,1152]{0,1:T(8,128)(2,1)}, u32[]{:S(2)}) copy-start(bf16[1024,1152]{0,1:T(8,128)(2,1)} %get-tuple-element.25) | copy-start | bytes 7077892 | tf_op jit(solution)/shard_map/cond
Sparse Core Ops, SparseCore 0:
  22.7 56.2 all-gather.1
where the time goes:
time: 110 us; the launch traced here: 109 us
  waiting for transfers between devices  34 us (31%)
  local copies, waits for them, and re-layouts  24.8 us (23%)
  matrix products  17.4 us (16%)
  between operations  14.2 us (13%)
  starting transfers between devices  10.6 us (10%)
  other arithmetic  8.02 us (7%)
    all_gather x1, waiting for transfers between devices, on_device(): piece = lax.all_gather(pairs, 'tile', axis=0, tiled=True)  19.3 us
    ppermute x1, waiting for transfers between devices, with_halo(): lax.ppermute(head, axis, [((i + 1) % count, i) for i in range(ends)])  13.5 us
    another operation x2, local copies, waits for them, and re-layouts  6.92 us
    slice x1, local copies, waits for them, and re-layouts, update(): piece[:, :width]  5.12 us
    ppermute x1, starting transfers between devices, with_halo(): lax.ppermute(tail, axis, [(i, (i + 1) % count) for i in range(ends)])  4.97 us
    dot_general x2, matrix products, partial_attend(): jnp.einsum('qhd,khd->hqk', heads_q, heads_k, preferred_element_type=jnp.f...  4.82 us
    dot_general x1, matrix products, on_device(): jnp.dot(normed, w_project, preferred_element_type=jnp.float32)  4.74 us
    dot_general x2, matrix products, partial_attend(): jnp.einsum('hqk,khd->qhd', probs.astype(jnp.bfloat16), heads_v, preferred...  4.12 us
  transfers between devices with their start and end apart: 4, of which 3 were waited for; matrix products, arithmetic and copies ran while one was open for 16% of the time, Pallas kernels for 0%

commit v1 on v0

v1 whole, which is shorter than its diff:
```python
import functools
import jax
import jax.numpy as jnp
from jax import lax
from jax.experimental import pallas as pl
from jax.experimental.pallas import tpu as pltpu
from jax.sharding import PartitionSpec as P

HEADS = 16
ROW_TOKENS = 64
LANES = 128
EPS = 1e-06
LOG2E = 1.4426950408889634
F32 = jnp.float32
BF16 = jnp.bfloat16


def half_columns(width):
    first = width // 2 // LANES * LANES
    return first, width - first


def assemble_modulation(pieces, row, blocks):
    here = lax.axis_index("grp")
    count = len(pieces)
    for back, piece in enumerate(pieces):
        blocks[lax.rem(here - back + count, count)] = piece[...]
    wide = pieces[0].shape[1]
    for block in range(count):
        row[:, block * wide : (block + 1) * wide] = blocks[block]


def normalize(rows, shift, scale):
    values = rows.astype(F32)
    mean = jnp.mean(values, axis=1, keepdims=True)
    centered = values - mean
    variance = jnp.mean(centered * centered, axis=1, keepdims=True)
    return (centered * lax.rsqrt(variance + EPS) * scale + shift).astype(BF16)


def normalize_rows(source, start, target, at, rows, shift, scale, block=32):
    for i in range(0, rows, block):
        target[pl.ds(at + i, block)] = normalize(source[pl.ds(start + i, block)], shift, scale)


def head_window(head, size, width, core):
    first, wide = half_columns(width)
    extra = width // 2 - first
    lo = head * size // LANES * LANES
    hi = min(-(-((head + 1) * size + extra) // LANES) * LANES, wide)
    column = lax.broadcasted_iota(jnp.int32, (1, hi - lo), 1) + (lo - head * size) - core * extra
    return lo, hi, (column >= 0) & (column < size)


def attend_heads(heads, size, width, core, query, keys, values, bias, scores, probs, target):
    windows = [head_window(head, size, width, core) for head in heads]
    bounds = [0]
    for key in keys:
        bounds.append(bounds[-1] + key.shape[0])
    spans = [slice(a, b) for a, b in zip(bounds, bounds[1:])]
    for head, (lo, hi, mask) in zip(heads, windows):
        part = query[:, lo:hi]
        masked = jnp.where(mask, part, jnp.zeros_like(part))
        for span, key in zip(spans, keys):
            scores[head - heads[0], :, span] = lax.dot_general(
                masked, key[:, lo:hi], (((1,), (1,)), ((), ())), preferred_element_type=F32
            )
    inverse = []
    for head in heads:
        score = scores[head - heads[0]]
        if bias is not None:
            score = score + bias
        top = jnp.max(score, axis=1, keepdims=True)
        prob = jnp.exp2((score - top) * (LOG2E / size**0.5))
        inverse.append(1.0 / jnp.sum(prob, axis=1, keepdims=True))
        probs[head - heads[0]] = prob.astype(BF16)
    for at, (head, (lo, hi, mask)) in enumerate(zip(heads, windows)):
        result = sum(
            jnp.dot(probs[at, :, span], value[:, lo:hi], preferred_element_type=F32)
            for span, value in zip(spans, values)
        )
        target[:, lo:hi] += jnp.where(mask, result * inverse[at], 0.0)


def modulate_kernel(condition, w, *outs):
    columns = jnp.dot(condition[...], w[...], preferred_element_type=F32)
    here = lax.axis_index("grp")
    count = len(outs)
    which = lax.broadcasted_iota(jnp.int32, (columns.shape[0], 1), 0)
    for ahead, out in enumerate(outs):
        out[...] = jnp.sum(
            jnp.where(which == lax.rem(here + ahead, count), columns, 0.0), axis=0, keepdims=True
        )


def project_kernel(own, partner, mine, theirs, *rest, parts):
    pieces = rest[:parts]
    w, query, kv, blocks, row, normed = rest[parts:]
    count, width = own.shape
    first, wide = half_columns(width)
    core = lax.rem(lax.axis_index("tile"), 2)
    assemble_modulation(pieces, row, blocks)
    shift = row[:, :width]
    scale = 1.0 + row[:, width : 2 * width]
    edge = ROW_TOKENS
    end = edge + 2 * count
    other = 1 - core
    normalize_rows(own, 0, normed, pl.multiple_of(edge + count * core, edge), count, shift, scale)
    normalize_rows(partner, 0, normed, pl.multiple_of(edge + count * other, edge), count, shift, scale)
    inner = count - edge
    normalize_rows(
        mine, pl.multiple_of(inner * other, edge), normed, pl.multiple_of(end * core, edge), edge, shift, scale
    )
    normalize_rows(
        theirs, pl.multiple_of(inner * core, edge), normed, pl.multiple_of(end * other, edge), edge, shift, scale
    )
    at = [pl.multiple_of(section * width + first * core, LANES) for section in range(3)]
    query[...] = jnp.dot(normed[edge:end], w[:, pl.ds(at[0], wide)], preferred_element_type=F32).astype(BF16)
    for section in (1, 2):
        part = slice((section - 1) * wide, section * wide)
        kv[:, part] = jnp.dot(normed[...], w[:, pl.ds(at[section], wide)], preferred_element_type=F32).astype(BF16)


def attend_kernel(query, kv, near, scores, probs, *, size):
    edge = ROW_TOKENS
    count = query.shape[0] // 2
    wide = query.shape[1]
    core, chip, chips = place_of_chip()
    column = lax.broadcasted_iota(jnp.int32, (1, count + 2 * edge), 1)
    near[...] = jnp.zeros_like(near)
    for strip in range(2):
        rows = pl.ds(strip * count, count)
        keys = pl.ds(strip * count, count + 2 * edge)
        if strip == 0:
            hidden = (chip == 0) & (column < edge)
        else:
            hidden = (chip == chips - 1) & (column >= count + edge)
        bias = jnp.where(hidden, -1e30, 0.0)
        attend_heads(
            range(HEADS // 2), size, size * HEADS, core, query.at[rows],
            [kv.at[keys, :wide]], [kv.at[keys, wide:]], bias, scores.at[strip], probs.at[strip], near.at[rows],
        )


def place_of_chip():
    place = lax.axis_index("tile")
    return lax.rem(place, 2), place // 2, lax.axis_size("tile") // 2


def chip_marks(marks, chip):
    return [marks[0, 2 * chip] > 0, marks[0, 2 * chip + 1] > 0]


def project_pairs(raw, pairs, row, w, kv, start, width, core):
    shift = row[:, :width]
    scale = 1.0 + row[:, width : 2 * width]
    first, wide = half_columns(width)
    block = 2 * LANES

    @pl.loop(0, pairs)
    def _(i):
        at = pl.multiple_of(i * block, block)
        normalize_rows(raw, at, raw, at, block, shift, scale)
        for section in range(2):
            columns = pl.ds(pl.multiple_of((section + 1) * width + first * core, LANES), wide)
            kv[pl.ds(start + at, block), section * wide : (section + 1) * wide] = jnp.dot(
                raw[pl.ds(at, block)], w[:, columns], preferred_element_type=F32
            ).astype(BF16)


def early_kernel(*refs, parts, depth):
    mine = refs[: 2 * depth]
    theirs = refs[2 * depth : 4 * depth]
    refs = refs[4 * depth :]
    pieces = refs[:parts]
    marks, around, w, kv, blocks, row, raw, sem = refs[parts:]
    count, width = mine[0].shape
    core, chip, chips = place_of_chip()
    marked = chip_marks(marks, chip)
    inner = 2 * count

    @pl.when(marked[0] | marked[1])
    def _():
        def each_strip(act):
            for ours in (True, False):
                strips_of = mine if ours else theirs
                is_left = (core == 0) if ours else (core == 1)
                have = jnp.where(is_left, chip, chips - 1 - chip)
                base = jnp.where(is_left, 0, jnp.minimum(chip, depth))
                for d in range(depth):

                    @pl.when(d < have)
                    def _(d=d, base=base, strips_of=strips_of):
                        for k in range(2):
                            at = pl.multiple_of((2 * (base + d) + k) * count, count)
                            act(pltpu.make_async_copy(strips_of[2 * d + k], raw.at[pl.ds(at, count)], sem))

        each_strip(lambda copy: copy.start())
        kv[:inner] = around[ROW_TOKENS : ROW_TOKENS + inner]
        assemble_modulation(pieces, row, blocks)
        each_strip(lambda copy: copy.wait())
        pairs = jnp.minimum(chip, depth) + jnp.minimum(chips - 1 - chip, depth)
        project_pairs(raw, pairs, row, w, kv, inner, width, core)


def late_kernel(mine0, mine1, theirs0, theirs1, *refs, parts):
    pieces = refs[:parts]
    marks, query, most, near, w, keep, send, blocks, row, raw, last, whole, scores, probs, sem = refs[parts:]
    count, width = mine0.shape
    _, wide = half_columns(width)
    core, chip, chips = place_of_chip()
    marked = chip_marks(marks, chip)
    size = width // HEADS
    bulk = most.shape[0] - 2 * count
    whole[...] = jnp.zeros_like(whole)

    @pl.when(marked[0] | marked[1])
    def _():
        at_end = (chip == 0) | (chip == chips - 1)
        from_mine = (chip == 0) == (core == 1)

        @pl.when(at_end)
        def _():
            def start(pair):
                for k, strip in enumerate(pair):
                    pltpu.make_async_copy(strip, raw.at[pl.ds(k * count, count)], sem).start()

            @pl.when(from_mine)
            def _():
                start((mine0, mine1))

            @pl.when(jnp.logical_not(from_mine))
            def _():
                start((theirs0, theirs1))

            assemble_modulation(pieces, row, blocks)
            pltpu.make_async_copy(raw, raw, sem).wait()
            project_pairs(raw, 1, row, w, last, 0, width, core)

        @pl.when(jnp.logical_not(at_end))
        def _():
            last[...] = most[bulk:]

        for strip in range(2):

            @pl.when(marked[strip])
            def _(strip=strip):
                rows = pl.ds(strip * count, count)
                early = pl.ds(0, bulk)
                group = scores.shape[0]
                for head in range(0, HEADS // 2, group):
                    attend_heads(
                        range(head, head + group), size, width, core, query.at[rows],
                        [most.at[early, :wide], last.at[:, :wide]], [most.at[early, wide:], last.at[:, wide:]],
                        None, scores, probs, whole.at[rows],
                    )

    ours = pl.ds(pl.multiple_of(count * core, count), count)
    others = pl.ds(pl.multiple_of(count * (1 - core), count), count)
    keep[...] = (near[ours] + whole[ours]).astype(BF16)
    send[...] = (near[others] + whole[others]).astype(BF16)


def output_kernel(own, keep, got, *rest, parts):
    pieces = rest[:parts]
    wo, out, blocks, row, mixed = rest[parts:]
    _, width = own.shape
    first, wide = half_columns(width)
    core = lax.rem(lax.axis_index("tile"), 2)
    assemble_modulation(pieces, row, blocks)
    low = jnp.where(core == 0, keep[...], got[...])
    high = jnp.where(core == 0, got[...], keep[...])
    mixed[:, :first] = low[:, :first]
    mixed[:, first:wide] = low[:, first:] + high[:, : wide - first]
    mixed[:, wide:] = high[:, wide - first :]
    branch = jnp.dot(mixed[...], wo[...], preferred_element_type=F32)
    gate = row[:, 2 * width : 3 * width]
    out[...] = (own[...].astype(F32) + gate * branch).astype(BF16)


def exchange_modulation(rows):
    count = len(rows)
    pieces = [rows[0]]
    for ahead in range(1, count):
        pairs = [(i, (i + ahead) % count) for i in range(count)]
        pieces.append(lax.ppermute(rows[ahead], "grp", pairs))
    return pieces


def call(kernel, outs, scratch, in_specs, flops, args, limit):
    return pl.pallas_call(
        kernel,
        out_shape=[jax.ShapeDtypeStruct(shape, dtype) for shape, dtype in outs],
        in_specs=in_specs,
        out_specs=[pl.BlockSpec(memory_space=pltpu.VMEM)] * len(outs),
        scratch_shapes=scratch,
        cost_estimate=pl.CostEstimate(flops=flops, bytes_accessed=flops // 200, transcendentals=0),
        compiler_params=pltpu.CompilerParams(vmem_limit_bytes=limit * 1024 * 1024),
    )(*args)


def on_device(latents, condition, w_modulate, w_project, w_output, detail):
    width = w_output.shape[0]
    own = latents[0]
    count = own.shape[0]
    tiles = lax.axis_size("tile")
    parts = lax.axis_size("grp")
    chips = tiles // 2
    depth = chips - 1
    _, wide = half_columns(width)
    rows = 2 * count + 2 * ROW_TOKENS
    tokens = count * tiles
    vmem = pl.BlockSpec(memory_space=pltpu.VMEM)
    anywhere = pl.BlockSpec(memory_space=pl.ANY)
    smem = pl.BlockSpec(memory_space=pltpu.SMEM)
    swap = [(i, i ^ 1) for i in range(tiles)]
    cross = [(2 * z + 1, 2 * z + 2) for z in range(chips - 1)]
    cross = cross + [(b, a) for a, b in cross]
    along = [(2 * z, 2 * z + 2) for z in range(chips - 1)]
    along = along + [(2 * z + 3, 2 * z + 1) for z in range(chips - 1)]
    mine = [lax.ppermute(own, "tile", cross), lax.ppermute(own, "tile", along)]
    partner = lax.ppermute(own, "tile", swap)
    part_width = w_modulate.shape[1]
    pieces = call(
        modulate_kernel, [((1, part_width), F32)] * parts, [], [vmem] * 2,
        10**10, (condition, w_modulate), 16,
    )
    pieces = exchange_modulation(pieces)
    for step in range(2, 2 * depth):
        mine.append(lax.ppermute(mine[step - 2], "tile", along))
    theirs = [lax.ppermute(strip, "tile", swap) for strip in mine]
    modulation = [pltpu.VMEM((parts, 1, part_width), F32), pltpu.VMEM((1, 3 * width), F32)]
    query, around = call(
        functools.partial(project_kernel, parts=parts),
        [((2 * count, wide), BF16), ((rows, 2 * wide), BF16)],
        modulation + [pltpu.VMEM((rows, width), BF16)],
        [vmem] * (5 + parts), 2 * 10**9,
        (own, partner, mine[0], theirs[0], *pieces, w_project), 16,
    )
    (near,) = call(
        functools.partial(attend_kernel, size=width // HEADS),
        [((2 * count, wide), F32)],
        [
            pltpu.VMEM((2, HEADS // 2, count, count + 2 * ROW_TOKENS), F32),
            pltpu.VMEM((2, HEADS // 2, count, count + 2 * ROW_TOKENS), BF16),
        ],
        [vmem] * 2, 10**9, (query, around), 16,
    )
    last = 2 * (depth - 1)
    early = min(depth - 1, depth)
    (most,) = call(
        functools.partial(early_kernel, parts=parts, depth=early),
        [((tokens, 2 * wide), BF16)],
        modulation + [pltpu.VMEM((tokens - 2 * count, width), BF16), pltpu.SemaphoreType.DMA],
        [anywhere] * (4 * early) + [vmem] * parts + [smem, vmem, vmem], 10**9,
        (*mine[:last], *theirs[:last], *pieces, detail, around, w_project), 12 + tokens * width * 2 // 2**20,
    )
    group = max(1, min(HEADS // 2, 2**20 // (count * tokens)))
    keep, send = call(
        functools.partial(late_kernel, parts=parts),
        [((count, wide), BF16)] * 2,
        modulation
        + [
            pltpu.VMEM((2 * count, width), BF16),
            pltpu.VMEM((2 * count, 2 * wide), BF16),
            pltpu.VMEM((2 * count, wide), F32),
            pltpu.VMEM((group, count, tokens), F32),
            pltpu.VMEM((group, count, tokens), BF16),
            pltpu.SemaphoreType.DMA,
        ],
        [anywhere] * 4 + [vmem] * parts + [smem] + [vmem] * 4, 10**9,
        (*mine[last:], *theirs[last:], *pieces, detail, query, most, near, w_project), 22,
    )
    got = lax.ppermute(send, "tile", swap)
    (updated,) = call(
        functools.partial(output_kernel, parts=parts),
        [((count, width), BF16)],
        modulation + [pltpu.VMEM((count, width), BF16)],
        [vmem] * (4 + parts), 10**9,
        (own, keep, got, *pieces, w_output), 16,
    )
    return updated[None]


def solution(mesh):
    in_specs = (P("grp", "tile", None), P(), P(None, "grp"), P(), P(), P("grp", None))
    out_specs = P("grp", "tile", None)

    return jax.shard_map(on_device, mesh=mesh, in_specs=in_specs, out_specs=out_specs, check_vma=False)
```

time: 110 us -> 64.1 us (0.58)
  the two profiles are of different devices: /device:TPU:5 before, /device:TPU:17 now
where the time goes in v1:
time: 64.1 us; the launch traced here: 63.7 us
  starting transfers between devices  27 us (42%)
  Pallas kernels  20.7 us (32%)
  waiting for transfers between devices  9.69 us (15%)
  local copies, waits for them, and re-layouts  6.15 us (10%)
    pallas_call x6, Pallas kernels, call(): pl.pallas_call(kernel, out_shape=[jax.ShapeDtypeStruct(shape, dtype) for...  20.7 us
    ppermute x4, starting transfers between devices, on_device(): mine.append(lax.ppermute(mine[step - 2], 'tile', along))  9.3 us
    unnamed x13, local copies, waits for them, and re-layouts  6.15 us
    ppermute x2, starting transfers between devices, on_device(): mine = [lax.ppermute(own, 'tile', cross), lax.ppermute(own, 'tile', along)]  5.97 us
    ppermute x6, starting transfers between devices, on_device(): theirs = [lax.ppermute(strip, 'tile', swap) for strip in mine]  5.1 us
    ppermute x3, starting transfers between devices, exchange_modulation(): pieces.append(lax.ppermute(rows[ahead], 'grp', pairs))  4.69 us
    ppermute x3, waiting for transfers between devices, exchange_modulation(): pieces.append(lax.ppermute(rows[ahead], 'grp', pairs))  4.52 us
    ppermute x2, waiting for transfers between devices, on_device(): mine = [lax.ppermute(own, 'tile', cross), lax.ppermute(own, 'tile', along)]  3.76 us
  transfers between devices with their start and end apart: 17, of which 6 were waited for; matrix products, arithmetic and copies ran while one was open for 4% of the time, Pallas kernels for 22%

profile of v1, /device:TPU:17, one launch (start us, length us, event | category | flops | bytes accessed | tf_op | source)
XLA Modules:
  0.0 63.7 jit_solution(11727575931552672835)
XLA Ops:
  0.0 0.0 copy-start.5
  0.0 3.9 %collective-permute-start = (bf16[128,1152]{1,0:T(8,128)(2,1)}, bf16[128,1152]{1,0:T(8,128)(2,1)S(1)}, u32[]{:S(2)}, u32[]{:S(2)}) collective-permute-start(bf16[128,1152]{1,0:T(8,128)(2,1)} %bitcast.2), channel_id=1, source_target_pairs={{1,2},{3,4},{5,6},{2,1},{4,3},{6,5},{9,10},{11,12},{13,14},{10,9},... | collective-permute-start | bytes 884744 | tf_op jit(solution)/shard_map/ppermute | solution.py:321
  3.9 2.1 %collective-permute-start.3 = (bf16[128,1152]{1,0:T(8,128)(2,1)}, bf16[128,1152]{1,0:T(8,128)(2,1)S(1)}, u32[]{:S(2)}, u32[]{:S(2)}) collective-permute-start(bf16[128,1152]{1,0:T(8,128)(2,1)} %bitcast.3), channel_id=1, source_target_pairs={{0,2},{2,4},{4,6},{3,1},{5,3},{7,5},{8,10},{10,12},{12,14},{11,9},... | collective-permute-start | bytes 884744 | tf_op jit(solution)/shard_map/ppermute | solution.py:321
  6.0 2.9 %collective-permute-done.mine.refs_0_ = bf16[128,1152]{1,0:T(8,128)(2,1)S(1)} collective-permute-done((bf16[128,1152]{1,0:T(8,128)(2,1)}, bf16[128,1152]{1,0:T(8,128)(2,1)S(1)}, u32[]{:S(2)}, u32[]{:S(2)}) %collective-permute-start) | collective-permute-done | bytes 294944 | tf_op jit(solution)/shard_map/ppermute | solution.py:321
  8.9 2.1 %collective-permute-start.1 = (bf16[128,1152]{1,0:T(8,128)(2,1)S(1)}, bf16[128,1152]{1,0:T(8,128)(2,1)S(1)}, u32[]{:S(2)}, u32[]{:S(2)}) collective-permute-start(bf16[128,1152]{1,0:T(8,128)(2,1)S(1)} %collective-permute-done.mine.refs_0_), channel_id=1, source_target_pairs={{0,2},{2,4},{4,6},{3,1},{5,3},{7,5},{8,10},{10,12},{12,14},{11,9},... | collective-permute-start | bytes 884744 | tf_op jit(solution)/shard_map/ppermute | solution.py:330
  11.0 0.9 %collective-permute-done.3.refs_1_ = bf16[128,1152]{1,0:T(8,128)(2,1)S(1)} collective-permute-done((bf16[128,1152]{1,0:T(8,128)(2,1)}, bf16[128,1152]{1,0:T(8,128)(2,1)S(1)}, u32[]{:S(2)}, u32[]{:S(2)}) %collective-permute-start.3) | collective-permute-done | bytes 294944 | tf_op jit(solution)/shard_map/ppermute | solution.py:321
  11.8 2.1 %collective-permute-start.4 = (bf16[128,1152]{1,0:T(8,128)(2,1)S(1)}, bf16[128,1152]{1,0:T(8,128)(2,1)S(1)}, u32[]{:S(2)}, u32[]{:S(2)}) collective-permute-start(bf16[128,1152]{1,0:T(8,128)(2,1)S(1)} %collective-permute-done.3.refs_1_), channel_id=1, source_target_pairs={{0,2},{2,4},{4,6},{3,1},{5,3},{7,5},{8,10},{10,12},{12,14},{11,9},... | collective-permute-start | bytes 884744 | tf_op jit(solution)/shard_map/ppermute | solution.py:330
  13.9 1.9 %collective-permute-start.11 = (bf16[128,1152]{1,0:T(8,128)(2,1)}, bf16[128,1152]{1,0:T(8,128)(2,1)S(1)}, u32[]{:S(2)}, u32[]{:S(2)}) collective-permute-start(bf16[128,1152]{1,0:T(8,128)(2,1)} %bitcast.4), channel_id=1, source_target_pairs={{0,1},{1,0},{2,3},{3,2},{4,5},{5,4},{6,7},{7,6},{8,9},{9,8},{10,11... | collective-permute-start | bytes 884744 | tf_op jit(solution)/shard_map/ppermute | solution.py:322
  15.8 2.9 %copy.7.w = bf16[1152,864]{1,0:T(8,128)(2,1)S(1)} copy(bf16[1152,864]{0,1:T(8,128)(2,1)} %param.8) | data formatting | bytes 3981312 | tf_op args[2]
  18.6 0.0 copy-start.2
  18.6 0.1 collective-permute-start.12
  18.7 0.0 collective-permute-done.1.refs_2_
  18.7 3.1 %collective-permute-start.2 = (bf16[128,1152]{1,0:T(8,128)(2,1)S(1)}, bf16[128,1152]{1,0:T(8,128)(2,1)S(1)}, u32[]{:S(2)}, u32[]{:S(2)}) collective-permute-start(bf16[128,1152]{1,0:T(8,128)(2,1)S(1)} %collective-permute-done.1.refs_2_), channel_id=1, source_target_pairs={{0,2},{2,4},{4,6},{3,1},{5,3},{7,5},{8,10},{10,12},{12,14},{11,9},... | collective-permute-start | bytes 884744 | tf_op jit(solution)/shard_map/ppermute | solution.py:330
  21.8 0.0 collective-permute-done.4.refs_3_
  21.8 2.1 %collective-permute-start.5 = (bf16[128,1152]{1,0:T(8,128)(2,1)S(1)}, bf16[128,1152]{1,0:T(8,128)(2,1)S(1)}, u32[]{:S(2)}, u32[]{:S(2)}) collective-permute-start(bf16[128,1152]{1,0:T(8,128)(2,1)S(1)} %collective-permute-done.4.refs_3_), channel_id=1, source_target_pairs={{0,2},{2,4},{4,6},{3,1},{5,3},{7,5},{8,10},{10,12},{12,14},{11,9},... | collective-permute-start | bytes 884744 | tf_op jit(solution)/shard_map/ppermute | solution.py:330
  23.9 0.0 copy-done.5
  23.9 0.4 shard_map.64
  24.3 2.2 %collective-permute-start.10 = (f32[1,864]{1,0:T(1,128)S(1)}, f32[1,864]{1,0:T(1,128)S(1)}, u32[]{:S(2)}, u32[]{:S(2)}) collective-permute-start(f32[1,864]{1,0:T(1,128)S(1)} %get-tuple-element.16), channel_id=1, source_target_pairs={{0,24},{8,0},{16,8},{24,16},{1,25},{9,1},{17,9},{25,17},{2,26},{10... | collective-permute-start | bytes 10376 | tf_op jit(solution)/shard_map/ppermute | solution.py:286
  26.6 0.8 %collective-permute-done.10.rest_3_.refs_11_.refs_3_ = f32[1,864]{1,0:T(1,128)S(1)} collective-permute-done((f32[1,864]{1,0:T(1,128)S(1)}, f32[1,864]{1,0:T(1,128)S(1)}, u32[]{:S(2)}, u32[]{:S(2)}) %collective-permute-start.10) | collective-permute-done | bytes 3488 | tf_op jit(solution)/shard_map/ppermute | solution.py:286
  27.3 1.6 %collective-permute-start.8 = (f32[1,864]{1,0:T(1,128)S(1)}, f32[1,864]{1,0:T(1,128)S(1)}, u32[]{:S(2)}, u32[]{:S(2)}) collective-permute-start(f32[1,864]{1,0:T(1,128)S(1)} %get-tuple-element.14), channel_id=1, source_target_pairs={{0,8},{8,16},{16,24},{24,0},{1,9},{9,17},{17,25},{25,1},{2,10},{10... | collective-permute-start | bytes 10376 | tf_op jit(solution)/shard_map/ppermute | solution.py:286
  29.0 1.9 %collective-permute-done.8.rest_1_.refs_9_.refs_1_ = f32[1,864]{1,0:T(1,128)S(1)} collective-permute-done((f32[1,864]{1,0:T(1,128)S(1)}, f32[1,864]{1,0:T(1,128)S(1)}, u32[]{:S(2)}, u32[]{:S(2)}) %collective-permute-start.8) | collective-permute-done | bytes 3488 | tf_op jit(solution)/shard_map/ppermute | solution.py:286
  30.9 0.8 %collective-permute-start.9 = (f32[1,864]{1,0:T(1,128)S(1)}, f32[1,864]{1,0:T(1,128)S(1)}, u32[]{:S(2)}, u32[]{:S(2)}) collective-permute-start(f32[1,864]{1,0:T(1,128)S(1)} %get-tuple-element.15), channel_id=1, source_target_pairs={{0,16},{8,24},{16,0},{24,8},{1,17},{9,25},{17,1},{25,9},{2,18},{10... | collective-permute-start | bytes 10376 | tf_op jit(solution)/shard_map/ppermute | solution.py:286
  31.7 1.8 %collective-permute-done.9.rest_2_.refs_10_.refs_2_ = f32[1,864]{1,0:T(1,128)S(1)} collective-permute-done((f32[1,864]{1,0:T(1,128)S(1)}, f32[1,864]{1,0:T(1,128)S(1)}, u32[]{:S(2)}, u32[]{:S(2)}) %collective-permute-start.9) | collective-permute-done | bytes 3488 | tf_op jit(solution)/shard_map/ppermute | solution.py:286
  33.6 4.0 %collective-permute-start.13 = (bf16[128,1152]{1,0:T(8,128)(2,1)S(1)}, bf16[128,1152]{1,0:T(8,128)(2,1)S(1)}, u32[]{:S(2)}, u32[]{:S(2)}) collective-permute-start(bf16[128,1152]{1,0:T(8,128)(2,1)S(1)} %collective-permute-done.3.refs_1_), channel_id=1, source_target_pairs={{0,1},{1,0},{2,3},{3,2},{4,5},{5,4},{6,7},{7,6},{8,9},{9,8},{10,11... | collective-permute-start | bytes 884744 | tf_op jit(solution)/shard_map/ppermute | solution.py:331
  37.6 0.0 collective-permute-done.11.partner
  37.6 0.0 collective-permute-start.14
  37.6 0.0 collective-permute-done.12.theirs.refs_4_
  37.6 0.5 collective-permute-start.15
  38.1 0.0 collective-permute-done.2.mine0
  38.1 0.1 collective-permute-start.6
  38.1 0.0 collective-permute-done.5.mine1
  38.2 0.4 collective-permute-start.7
  38.6 0.0 copy-done.2
  38.6 0.0 copy-start
  38.6 3.3 %copy-done = bf16[1152,3456]{1,0:T(8,128)(2,1)S(1)} copy-done((bf16[1152,3456]{1,0:T(8,128)(2,1)S(1)}, bf16[1152,3456]{1,0:T(8,128)(2,1)}, u32[]{:S(2)}) %copy-start) | copy-done | bytes 7962648
  41.9 0.0 copy-start.1
  41.9 2.7 %shard_map.65 = (bf16[256,640]{1,0:T(8,128)(2,1)S(1)}, bf16[384,1280]{1,0:T(8,128)(2,1)S(1)}) custom-call(bf16[128,1152]{1,0:T(8,128)(2,1)S(1)} %bitcast.5, bf16[128,1152]{1,0:T(8,128)(2,1)S(1)} %collective-permute-done.11.partner, bf16[128,1152]{1,0:T(8,128)(2,1)S(1)} %collective-permute-done.mine.refs_0_, ...), custom_call_target="tpu_custom_call" | custom-call | flops 2000000000 | bytes 10000000 | tf_op jit(solution)/shard_map/pallas_call | solution.py:291
  44.6 0.0 copy-start.3
  44.6 1.4 %shard_map.67.refs_7_ = f32[256,640]{1,0:T(8,128)S(1)} custom-call(bf16[256,640]{1,0:T(8,128)(2,1)S(1)} %get-tuple-element.17.query.refs_5_, bf16[384,1280]{1,0:T(8,128)(2,1)S(1)} %get-tuple-element.18.refs_13_.kv), custom_call_target="tpu_custom_call" | custom-call | flops 1000000000 | bytes 5000000 | tf_op jit(solution)/shard_map/pallas_call | solution.py:291
  46.0 0.0 collective-permute-done.13.refs_5_
  46.0 0.0 collective-permute-done.14.refs_6_
  46.0 0.0 collective-permute-done.15.refs_7_
  46.0 0.0 copy-done.1
  46.0 0.0 copy-done.3
  46.0 9.3 %shard_map.66.refs_6_ = bf16[1024,1280]{1,0:T(8,128)(2,1)S(1)} custom-call(bf16[128,1152]{1,0:T(8,128)(2,1)S(1)} %collective-permute-done.mine.refs_0_, bf16[128,1152]{1,0:T(8,128)(2,1)S(1)} %collective-permute-done.3.refs_1_, bf16[128,1152]{1,0:T(8,128)(2,1)S(1)} %collective-permute-done.1.refs_2_, bf16[128,1152]{1,0:T(8,128)(2,1)S(1)} %collective-permute-done.4.refs_3_, ...), custom_call_target="tpu_custom_call" | custom-call | flops 1000000000 | bytes 5000000 | tf_op jit(solution)/shard_map/pallas_call | solution.py:291
  55.4 0.0 copy-start.4
  55.4 0.0 collective-permute-done.6.theirs0
  55.4 0.0 collective-permute-done.7.theirs1
  55.4 5.6 %shard_map.68 = (bf16[128,640]{1,0:T(8,128)(2,1)S(1)}, bf16[128,640]{1,0:T(8,128)(2,1)S(1)}) custom-call(bf16[128,1152]{1,0:T(8,128)(2,1)S(1)} %collective-permute-done.2.mine0, bf16[128,1152]{1,0:T(8,128)(2,1)S(1)} %collective-permute-done.5.mine1, bf16[128,1152]{1,0:T(8,128)(2,1)S(1)} %collective-permute-done.6.theirs0, ...), custom_call_target="tpu_custom_call" | custom-call | flops 1000000000 | bytes 5000000 | tf_op jit(solution)/shard_map/pallas_call | solution.py:291
  60.9 0.1 collective-permute-start.16
  61.0 1.4 %collective-permute-done.16.got = bf16[128,640]{1,0:T(8,128)(2,1)S(1)} collective-permute-done((bf16[128,640]{1,0:T(8,128)(2,1)S(1)}, bf16[128,640]{1,0:T(8,128)(2,1)S(1)}, u32[]{:S(2)}, u32[]{:S(2)}) %collective-permute-start.16) | collective-permute-done | bytes 163872 | tf_op jit(solution)/shard_map/ppermute | solution.py:374
  62.4 0.0 copy-done.4
  62.4 1.3 %shard_map.69 = bf16[128,1152]{1,0:T(8,128)(2,1)} custom-call(bf16[128,1152]{1,0:T(8,128)(2,1)S(1)} %bitcast.6, bf16[128,640]{1,0:T(8,128)(2,1)S(1)} %get-tuple-element.19.keep, bf16[128,640]{1,0:T(8,128)(2,1)S(1)} %collective-permute-done.16.got, f32[1,864]{1,0:T(1,128)S(1)} %get-tuple-element.13.rest_0_.refs_8_.refs_0_, ...), custom_call_target="tpu_custom_call" | custom-call | flops 1000000000 | bytes 5000000 | tf_op jit(solution)/shard_map/pallas_call | solution.py:291
Async XLA Ops:
  0.0 23.9 %copy-start.5 = (bf16[4,1152]{1,0:T(4,128)(2,1)S(1)}, bf16[4,1152]{1,0:T(4,128)(2,1)}, u32[]{:S(2)}) copy-start(bf16[4,1152]{1,0:T(4,128)(2,1)} %condition.1) | copy-start | bytes 27652
  0.0 8.9 %collective-permute-start = (bf16[128,1152]{1,0:T(8,128)(2,1)}, bf16[128,1152]{1,0:T(8,128)(2,1)S(1)}, u32[]{:S(2)}, u32[]{:S(2)}) collective-permute-start(bf16[128,1152]{1,0:T(8,128)(2,1)} %bitcast.2), channel_id=1, source_target_pairs={{1,2},{3,4},{5,6},{2,1},{4,3},{6,5},{9,10},{11,12},{13,14},{10,9},... | collective-permute-start | bytes 884744 | tf_op jit(solution)/shard_map/ppermute | solution.py:321
  3.9 7.9 %collective-permute-start.3 = (bf16[128,1152]{1,0:T(8,128)(2,1)}, bf16[128,1152]{1,0:T(8,128)(2,1)S(1)}, u32[]{:S(2)}, u32[]{:S(2)}) collective-permute-start(bf16[128,1152]{1,0:T(8,128)(2,1)} %bitcast.3), channel_id=1, source_target_pairs={{0,2},{2,4},{4,6},{3,1},{5,3},{7,5},{8,10},{10,12},{12,14},{11,9},... | collective-permute-start | bytes 884744 | tf_op jit(solution)/shard_map/ppermute | solution.py:321
  8.9 9.9 %collective-permute-start.1 = (bf16[128,1152]{1,0:T(8,128)(2,1)S(1)}, bf16[128,1152]{1,0:T(8,128)(2,1)S(1)}, u32[]{:S(2)}, u32[]{:S(2)}) collective-permute-start(bf16[128,1152]{1,0:T(8,128)(2,1)S(1)} %collective-permute-done.mine.refs_0_), channel_id=1, source_target_pairs={{0,2},{2,4},{4,6},{3,1},{5,3},{7,5},{8,10},{10,12},{12,14},{11,9},... | collective-permute-start | bytes 884744 | tf_op jit(solution)/shard_map/ppermute | solution.py:330
  11.8 10.0 %collective-permute-start.4 = (bf16[128,1152]{1,0:T(8,128)(2,1)S(1)}, bf16[128,1152]{1,0:T(8,128)(2,1)S(1)}, u32[]{:S(2)}, u32[]{:S(2)}) collective-permute-start(bf16[128,1152]{1,0:T(8,128)(2,1)S(1)} %collective-permute-done.3.refs_1_), channel_id=1, source_target_pairs={{0,2},{2,4},{4,6},{3,1},{5,3},{7,5},{8,10},{10,12},{12,14},{11,9},... | collective-permute-start | bytes 884744 | tf_op jit(solution)/shard_map/ppermute | solution.py:330
  13.9 23.7 %collective-permute-start.11 = (bf16[128,1152]{1,0:T(8,128)(2,1)}, bf16[128,1152]{1,0:T(8,128)(2,1)S(1)}, u32[]{:S(2)}, u32[]{:S(2)}) collective-permute-start(bf16[128,1152]{1,0:T(8,128)(2,1)} %bitcast.4), channel_id=1, source_target_pairs={{0,1},{1,0},{2,3},{3,2},{4,5},{5,4},{6,7},{7,6},{8,9},{9,8},{10,11... | collective-permute-start | bytes 884744 | tf_op jit(solution)/shard_map/ppermute | solution.py:322
  18.6 20.0 %copy-start.2 = (bf16[1,128,1152]{2,1,0:T(8,128)(2,1)S(1)}, bf16[1,128,1152]{2,1,0:T(8,128)(2,1)}, u32[]{:S(2)}) copy-start(bf16[1,128,1152]{2,1,0:T(8,128)(2,1)} %param.6) | copy-start | bytes 884740
  18.6 18.9 %collective-permute-start.12 = (bf16[128,1152]{1,0:T(8,128)(2,1)S(1)}, bf16[128,1152]{1,0:T(8,128)(2,1)S(1)}, u32[]{:S(2)}, u32[]{:S(2)}) collective-permute-start(bf16[128,1152]{1,0:T(8,128)(2,1)S(1)} %collective-permute-done.mine.refs_0_), channel_id=1, source_target_pairs={{0,1},{1,0},{2,3},{3,2},{4,5},{5,4},{6,7},{7,6},{8,9},{9,8},{10,11... | collective-permute-start | bytes 884744 | tf_op jit(solution)/shard_map/ppermute | solution.py:331
  18.7 19.3 %collective-permute-start.2 = (bf16[128,1152]{1,0:T(8,128)(2,1)S(1)}, bf16[128,1152]{1,0:T(8,128)(2,1)S(1)}, u32[]{:S(2)}, u32[]{:S(2)}) collective-permute-start(bf16[128,1152]{1,0:T(8,128)(2,1)S(1)} %collective-permute-done.1.refs_2_), channel_id=1, source_target_pairs={{0,2},{2,4},{4,6},{3,1},{5,3},{7,5},{8,10},{10,12},{12,14},{11,9},... | collective-permute-start | bytes 884744 | tf_op jit(solution)/shard_map/ppermute | solution.py:330
  21.8 16.3 %collective-permute-start.5 = (bf16[128,1152]{1,0:T(8,128)(2,1)S(1)}, bf16[128,1152]{1,0:T(8,128)(2,1)S(1)}, u32[]{:S(2)}, u32[]{:S(2)}) collective-permute-start(bf16[128,1152]{1,0:T(8,128)(2,1)S(1)} %collective-permute-done.4.refs_3_), channel_id=1, source_target_pairs={{0,2},{2,4},{4,6},{3,1},{5,3},{7,5},{8,10},{10,12},{12,14},{11,9},... | collective-permute-start | bytes 884744 | tf_op jit(solution)/shard_map/ppermute | solution.py:330
  24.3 3.0 %collective-permute-start.10 = (f32[1,864]{1,0:T(1,128)S(1)}, f32[1,864]{1,0:T(1,128)S(1)}, u32[]{:S(2)}, u32[]{:S(2)}) collective-permute-start(f32[1,864]{1,0:T(1,128)S(1)} %get-tuple-element.16), channel_id=1, source_target_pairs={{0,24},{8,0},{16,8},{24,16},{1,25},{9,1},{17,9},{25,17},{2,26},{10... | collective-permute-start | bytes 10376 | tf_op jit(solution)/shard_map/ppermute | solution.py:286
  27.3 3.6 %collective-permute-start.8 = (f32[1,864]{1,0:T(1,128)S(1)}, f32[1,864]{1,0:T(1,128)S(1)}, u32[]{:S(2)}, u32[]{:S(2)}) collective-permute-start(f32[1,864]{1,0:T(1,128)S(1)} %get-tuple-element.14), channel_id=1, source_target_pairs={{0,8},{8,16},{16,24},{24,0},{1,9},{9,17},{17,25},{25,1},{2,10},{10... | collective-permute-start | bytes 10376 | tf_op jit(solution)/shard_map/ppermute | solution.py:286
  30.9 2.7 %collective-permute-start.9 = (f32[1,864]{1,0:T(1,128)S(1)}, f32[1,864]{1,0:T(1,128)S(1)}, u32[]{:S(2)}, u32[]{:S(2)}) collective-permute-start(f32[1,864]{1,0:T(1,128)S(1)} %get-tuple-element.15), channel_id=1, source_target_pairs={{0,16},{8,24},{16,0},{24,8},{1,17},{9,25},{17,1},{25,9},{2,18},{10... | collective-permute-start | bytes 10376 | tf_op jit(solution)/shard_map/ppermute | solution.py:286
  33.6 12.4 %collective-permute-start.13 = (bf16[128,1152]{1,0:T(8,128)(2,1)S(1)}, bf16[128,1152]{1,0:T(8,128)(2,1)S(1)}, u32[]{:S(2)}, u32[]{:S(2)}) collective-permute-start(bf16[128,1152]{1,0:T(8,128)(2,1)S(1)} %collective-permute-done.3.refs_1_), channel_id=1, source_target_pairs={{0,1},{1,0},{2,3},{3,2},{4,5},{5,4},{6,7},{7,6},{8,9},{9,8},{10,11... | collective-permute-start | bytes 884744 | tf_op jit(solution)/shard_map/ppermute | solution.py:331
  37.6 8.4 %collective-permute-start.14 = (bf16[128,1152]{1,0:T(8,128)(2,1)S(1)}, bf16[128,1152]{1,0:T(8,128)(2,1)S(1)}, u32[]{:S(2)}, u32[]{:S(2)}) collective-permute-start(bf16[128,1152]{1,0:T(8,128)(2,1)S(1)} %collective-permute-done.1.refs_2_), channel_id=1, source_target_pairs={{0,1},{1,0},{2,3},{3,2},{4,5},{5,4},{6,7},{7,6},{8,9},{9,8},{10,11... | collective-permute-start | bytes 884744 | tf_op jit(solution)/shard_map/ppermute | solution.py:331
  37.6 8.4 %collective-permute-start.15 = (bf16[128,1152]{1,0:T(8,128)(2,1)S(1)}, bf16[128,1152]{1,0:T(8,128)(2,1)S(1)}, u32[]{:S(2)}, u32[]{:S(2)}) collective-permute-start(bf16[128,1152]{1,0:T(8,128)(2,1)S(1)} %collective-permute-done.4.refs_3_), channel_id=1, source_target_pairs={{0,1},{1,0},{2,3},{3,2},{4,5},{5,4},{6,7},{7,6},{8,9},{9,8},{10,11... | collective-permute-start | bytes 884744 | tf_op jit(solution)/shard_map/ppermute | solution.py:331
  38.1 17.3 %collective-permute-start.6 = (bf16[128,1152]{1,0:T(8,128)(2,1)S(1)}, bf16[128,1152]{1,0:T(8,128)(2,1)S(1)}, u32[]{:S(2)}, u32[]{:S(2)}) collective-permute-start(bf16[128,1152]{1,0:T(8,128)(2,1)S(1)} %collective-permute-done.2.mine0), channel_id=1, source_target_pairs={{0,1},{1,0},{2,3},{3,2},{4,5},{5,4},{6,7},{7,6},{8,9},{9,8},{10,11... | collective-permute-start | bytes 884744 | tf_op jit(solution)/shard_map/ppermute | solution.py:331
  38.2 17.2 %collective-permute-start.7 = (bf16[128,1152]{1,0:T(8,128)(2,1)S(1)}, bf16[128,1152]{1,0:T(8,128)(2,1)S(1)}, u32[]{:S(2)}, u32[]{:S(2)}) collective-permute-start(bf16[128,1152]{1,0:T(8,128)(2,1)S(1)} %collective-permute-done.5.mine1), channel_id=1, source_target_pairs={{0,1},{1,0},{2,3},{3,2},{4,5},{5,4},{6,7},{7,6},{8,9},{9,8},{10,11... | collective-permute-start | bytes 884744 | tf_op jit(solution)/shard_map/ppermute | solution.py:331
  38.6 3.3 %copy-start = (bf16[1152,3456]{1,0:T(8,128)(2,1)S(1)}, bf16[1152,3456]{1,0:T(8,128)(2,1)}, u32[]{:S(2)}) copy-start(bf16[1152,3456]{1,0:T(8,128)(2,1)} %refs_8_.1) | copy-start | bytes 23887876
  41.9 4.1 %copy-start.1 = (bf16[1152,3456]{1,0:T(8,128)(2,1)S(1)}, bf16[1152,3456]{1,0:T(8,128)(2,1)}, u32[]{:S(2)}) copy-start(bf16[1152,3456]{1,0:T(8,128)(2,1)} %refs_8_.1) | copy-start | bytes 23887876
  44.6 1.4 %copy-start.3 = (s32[1,8]{1,0:T(1,128)S(1)}, s32[1,8]{1,0:T(1,128)}, u32[]{:S(2)}) copy-start(s32[1,8]{1,0:T(1,128)} %refs_4_.1) | copy-start | bytes 100
  55.4 7.1 %copy-start.4 = (bf16[1152,1152]{1,0:T(8,128)(2,1)S(1)}, bf16[1152,1152]{1,0:T(8,128)(2,1)}, u32[]{:S(2)}) copy-start(bf16[1152,1152]{1,0:T(8,128)(2,1)} %rest_4_.3) | copy-start | bytes 7962628
  60.9 1.5 %collective-permute-start.16 = (bf16[128,640]{1,0:T(8,128)(2,1)S(1)}, bf16[128,640]{1,0:T(8,128)(2,1)S(1)}, u32[]{:S(2)}, u32[]{:S(2)}) collective-permute-start(bf16[128,640]{1,0:T(8,128)(2,1)S(1)} %get-tuple-element.20), channel_id=1, source_target_pairs={{0,1},{1,0},{2,3},{3,2},{4,5},{5,4},{6,7},{7,6},{8,9},{9,8},{10,11... | collective-permute-start | bytes 491528 | tf_op jit(solution)/shard_map/ppermute | solution.py:374

commit v2 on v1

--- a/solution.py
+++ b/solution.py
@@ -82,8 +82,14 @@
         target[:, lo:hi] += jnp.where(mask, result * inverse[at], 0.0)
 
 
-def modulate_kernel(condition, w, *outs):
-    columns = jnp.dot(condition[...], w[...], preferred_element_type=F32)
+def first_kernel(out):
+    out[...] = jnp.zeros_like(out)
+
+
+def modulate_kernel(condition, w, _, *outs):
+    columns = lax.dot_general(
+        condition[...], w[...], (((1,), (1,)), ((), ())), preferred_element_type=F32
+    )
     here = lax.axis_index("grp")
     count = len(outs)
     which = lax.broadcasted_iota(jnp.int32, (columns.shape[0], 1), 0)
@@ -95,7 +101,7 @@
 
 def project_kernel(own, partner, mine, theirs, *rest, parts):
     pieces = rest[:parts]
-    w, query, kv, blocks, row, normed = rest[parts:]
+    w, query, kv, row, blocks, normed = rest[parts:]
     count, width = own.shape
     first, wide = half_columns(width)
     core = lax.rem(lax.axis_index("tile"), 2)
@@ -151,109 +157,69 @@
     return [marks[0, 2 * chip] > 0, marks[0, 2 * chip + 1] > 0]
 
 
-def project_pairs(raw, pairs, row, w, kv, start, width, core):
+def pair_kernel(ours0, ours1, theirs0, theirs1, row, marks, before, w, kv, normed, *, distance, first_call):
+    _, chip, _ = place_of_chip()
+    marked = chip_marks(marks, chip)
+    count = ours0.shape[0]
+
+    @pl.when(marked[0] | marked[1])
+    def _():
+        if first_call:
+            kv[: 2 * count] = before[ROW_TOKENS : ROW_TOKENS + 2 * count]
+        add_pairs((ours0, ours1), (theirs0, theirs1), row, w, kv, normed, distance)
+
+
+def add_pairs(ours, theirs, row, w, kv, normed, distance):
+    count, width = ours[0].shape
+    core, chip, chips = place_of_chip()
+    first, wide = half_columns(width)
     shift = row[:, :width]
     scale = 1.0 + row[:, width : 2 * width]
-    first, wide = half_columns(width)
-    block = 2 * LANES
-
-    @pl.loop(0, pairs)
-    def _(i):
-        at = pl.multiple_of(i * block, block)
-        normalize_rows(raw, at, raw, at, block, shift, scale)
-        for section in range(2):
-            columns = pl.ds(pl.multiple_of((section + 1) * width + first * core, LANES), wide)
-            kv[pl.ds(start + at, block), section * wide : (section + 1) * wide] = jnp.dot(
-                raw[pl.ds(at, block)], w[:, columns], preferred_element_type=F32
-            ).astype(BF16)
-
-
-def early_kernel(*refs, parts, depth):
-    mine = refs[: 2 * depth]
-    theirs = refs[2 * depth : 4 * depth]
-    refs = refs[4 * depth :]
-    pieces = refs[:parts]
-    marks, around, w, kv, blocks, row, raw, sem = refs[parts:]
-    count, width = mine[0].shape
-    core, chip, chips = place_of_chip()
+    lefts = chip
+    rights = chips - 1 - chip
+    nearer = jnp.minimum(lefts, distance - 1) + jnp.minimum(rights, distance - 1)
+    for mine, pair in ((True, ours), (False, theirs)):
+        is_left = (core == 0) if mine else (core == 1)
+        have = jnp.where(is_left, lefts, rights) >= distance
+        slot = nearer + jnp.where(is_left | (lefts < distance), 0, 1)
+
+        @pl.when(have)
+        def _(pair=pair, slot=slot):
+            at = pl.multiple_of(2 * count * (slot + 1), 2 * count)
+            for k, strip in enumerate(pair):
+                normalize_rows(strip, 0, normed, k * count, count, shift, scale)
+            for section in range(2):
+                columns = pl.ds(pl.multiple_of((section + 1) * width + first * core, LANES), wide)
+                kv[pl.ds(at, 2 * count), section * wide : (section + 1) * wide] = jnp.dot(
+                    normed[...], w[:, columns], preferred_element_type=F32
+                ).astype(BF16)
+
+
+def late_kernel(
+    ours0, ours1, theirs0, theirs1, row, marks, query, before, near, w,
+    kv, keep, send, normed, whole, scores, probs, *, distance,
+):
+    count, width = ours0.shape
+    _, wide = half_columns(width)
+    core, chip, _ = place_of_chip()
     marked = chip_marks(marks, chip)
-    inner = 2 * count
+    whole[...] = jnp.zeros_like(whole)
 
     @pl.when(marked[0] | marked[1])
     def _():
-        def each_strip(act):
-            for ours in (True, False):
-                strips_of = mine if ours else theirs
-                is_left = (core == 0) if ours else (core == 1)
-                have = jnp.where(is_left, chip, chips - 1 - chip)
-                base = jnp.where(is_left, 0, jnp.minimum(chip, depth))
-                for d in range(depth):
-
-                    @pl.when(d < have)
-                    def _(d=d, base=base, strips_of=strips_of):
-                        for k in range(2):
-                            at = pl.multiple_of((2 * (base + d) + k) * count, count)
-                            act(pltpu.make_async_copy(strips_of[2 * d + k], raw.at[pl.ds(at, count)], sem))
-
-        each_strip(lambda copy: copy.start())
-        kv[:inner] = around[ROW_TOKENS : ROW_TOKENS + inner]
-        assemble_modulation(pieces, row, blocks)
-        each_strip(lambda copy: copy.wait())
-        pairs = jnp.minimum(chip, depth) + jnp.minimum(chips - 1 - chip, depth)
-        project_pairs(raw, pairs, row, w, kv, inner, width, core)
-
-
-def late_kernel(mine0, mine1, theirs0, theirs1, *refs, parts):
-    pieces = refs[:parts]
-    marks, query, most, near, w, keep, send, blocks, row, raw, last, whole, scores, probs, sem = refs[parts:]
-    count, width = mine0.shape
-    _, wide = half_columns(width)
-    core, chip, chips = place_of_chip()
-    marked = chip_marks(marks, chip)
-    size = width // HEADS
-    bulk = most.shape[0] - 2 * count
-    whole[...] = jnp.zeros_like(whole)
-
-    @pl.when(marked[0] | marked[1])
-    def _():
-        at_end = (chip == 0) | (chip == chips - 1)
-        from_mine = (chip == 0) == (core == 1)
-
-        @pl.when(at_end)
-        def _():
-            def start(pair):
-                for k, strip in enumerate(pair):
-                    pltpu.make_async_copy(strip, raw.at[pl.ds(k * count, count)], sem).start()
-
-            @pl.when(from_mine)
-            def _():
-                start((mine0, mine1))
-
-            @pl.when(jnp.logical_not(from_mine))
-            def _():
-                start((theirs0, theirs1))
-
-            assemble_modulation(pieces, row, blocks)
-            pltpu.make_async_copy(raw, raw, sem).wait()
-            project_pairs(raw, 1, row, w, last, 0, width, core)
-
-        @pl.when(jnp.logical_not(at_end))
-        def _():
-            last[...] = most[bulk:]
-
-        for strip in range(2):
-
-            @pl.when(marked[strip])
-            def _(strip=strip):
-                rows = pl.ds(strip * count, count)
-                early = pl.ds(0, bulk)
-                group = scores.shape[0]
-                for head in range(0, HEADS // 2, group):
-                    attend_heads(
-                        range(head, head + group), size, width, core, query.at[rows],
-                        [most.at[early, :wide], last.at[:, :wide]], [most.at[early, wide:], last.at[:, wide:]],
-                        None, scores, probs, whole.at[rows],
-                    )
+        add_pairs((ours0, ours1), (theirs0, theirs1), row, w, kv, normed, distance)
+
+    for strip in range(2):
+
+        @pl.when(marked[strip])
+        def _(strip=strip):
+            rows = pl.ds(strip * count, count)
+            group = scores.shape[0]
+            for head in range(0, HEADS // 2, group):
+                attend_heads(
+                    range(head, head + group), width // HEADS, width, core, query.at[rows],
+                    [kv.at[:, :wide]], [kv.at[:, wide:]], None, scores, probs, whole.at[rows],
+                )
 
     ours = pl.ds(pl.multiple_of(count * core, count), count)
     others = pl.ds(pl.multiple_of(count * (1 - core), count), count)
@@ -261,13 +227,10 @@
     send[...] = (near[others] + whole[others]).astype(BF16)
 
 
-def output_kernel(own, keep, got, *rest, parts):
-    pieces = rest[:parts]
-    wo, out, blocks, row, mixed = rest[parts:]
+def output_kernel(own, keep, got, row, wo, out, mixed):
     _, width = own.shape
     first, wide = half_columns(width)
     core = lax.rem(lax.axis_index("tile"), 2)
-    assemble_modulation(pieces, row, blocks)
     low = jnp.where(core == 0, keep[...], got[...])
     high = jnp.where(core == 0, got[...], keep[...])
     mixed[:, :first] = low[:, :first]
@@ -287,13 +250,14 @@
     return pieces
 
 
-def call(kernel, outs, scratch, in_specs, flops, args, limit):
+def call(kernel, outs, scratch, in_specs, flops, args, limit, aliases={}):
     return pl.pallas_call(
         kernel,
         out_shape=[jax.ShapeDtypeStruct(shape, dtype) for shape, dtype in outs],
         in_specs=in_specs,
         out_specs=[pl.BlockSpec(memory_space=pltpu.VMEM)] * len(outs),
         scratch_shapes=scratch,
+        input_output_aliases=aliases,
         cost_estimate=pl.CostEstimate(flops=flops, bytes_accessed=flops // 200, transcendentals=0),
         compiler_params=pltpu.CompilerParams(vmem_limit_bytes=limit * 1024 * 1024),
     )(*args)
@@ -314,26 +278,29 @@
     anywhere = pl.BlockSpec(memory_space=pl.ANY)
     smem = pl.BlockSpec(memory_space=pltpu.SMEM)
     swap = [(i, i ^ 1) for i in range(tiles)]
+
+    def along(distance):
+        right = [(2 * z - 2, 2 * z) for z in range(distance, chips)]
+        return right + [(2 * z + 3, 2 * z + 1) for z in range(chips - distance)]
+
     cross = [(2 * z + 1, 2 * z + 2) for z in range(chips - 1)]
     cross = cross + [(b, a) for a, b in cross]
-    along = [(2 * z, 2 * z + 2) for z in range(chips - 1)]
-    along = along + [(2 * z + 3, 2 * z + 1) for z in range(chips - 1)]
-    mine = [lax.ppermute(own, "tile", cross), lax.ppermute(own, "tile", along)]
+    mine = [lax.ppermute(own, "tile", cross), lax.ppermute(own, "tile", along(1))]
     partner = lax.ppermute(own, "tile", swap)
     part_width = w_modulate.shape[1]
+    (token,) = call(first_kernel, [((8, LANES), F32)], [], [], 10**10, (), 16)
     pieces = call(
-        modulate_kernel, [((1, part_width), F32)] * parts, [], [vmem] * 2,
-        10**10, (condition, w_modulate), 16,
+        modulate_kernel, [((1, part_width), F32)] * parts, [], [vmem] * 3,
+        10**10, (condition, w_modulate.T, token), 16,
     )
     pieces = exchange_modulation(pieces)
     for step in range(2, 2 * depth):
-        mine.append(lax.ppermute(mine[step - 2], "tile", along))
+        mine.append(lax.ppermute(mine[step - 2], "tile", along(step // 2 + 1)))
     theirs = [lax.ppermute(strip, "tile", swap) for strip in mine]
-    modulation = [pltpu.VMEM((parts, 1, part_width), F32), pltpu.VMEM((1, 3 * width), F32)]
-    query, around = call(
+    query, around, row = call(
         functools.partial(project_kernel, parts=parts),
-        [((2 * count, wide), BF16), ((rows, 2 * wide), BF16)],
-        modulation + [pltpu.VMEM((rows, width), BF16)],
+        [((2 * count, wide), BF16), ((rows, 2 * wide), BF16), ((1, 3 * width), F32)],
+        [pltpu.VMEM((parts, 1, part_width), F32), pltpu.VMEM((rows, width), BF16)],
         [vmem] * (5 + parts), 2 * 10**9,
         (own, partner, mine[0], theirs[0], *pieces, w_project), 16,
     )
@@ -346,38 +313,37 @@
         ],
         [vmem] * 2, 10**9, (query, around), 16,
     )
-    last = 2 * (depth - 1)
-    early = min(depth - 1, depth)
-    (most,) = call(
-        functools.partial(early_kernel, parts=parts, depth=early),
-        [((tokens, 2 * wide), BF16)],
-        modulation + [pltpu.VMEM((tokens - 2 * count, width), BF16), pltpu.SemaphoreType.DMA],
-        [anywhere] * (4 * early) + [vmem] * parts + [smem, vmem, vmem], 10**9,
-        (*mine[:last], *theirs[:last], *pieces, detail, around, w_project), 12 + tokens * width * 2 // 2**20,
-    )
+    kv = around
+    kv_out = ((tokens, 2 * wide), BF16)
+    pair_scratch = [pltpu.VMEM((2 * count, width), BF16)]
+
+    def strips_at(distance):
+        at = slice(2 * distance - 2, 2 * distance)
+        return (*mine[at], *theirs[at])
+
+    for distance in range(1, depth):
+        (kv,) = call(
+            functools.partial(pair_kernel, distance=distance, first_call=distance == 1),
+            [kv_out], pair_scratch, [vmem] * 5 + [smem] + [vmem] * 2, 10**9,
+            (*strips_at(distance), row, detail, kv, w_project), 12, {} if distance == 1 else {6: 0},
+        )
     group = max(1, min(HEADS // 2, 2**20 // (count * tokens)))
-    keep, send = call(
-        functools.partial(late_kernel, parts=parts),
-        [((count, wide), BF16)] * 2,
-        modulation
+    _, keep, send = call(
+        functools.partial(late_kernel, distance=depth),
+        [kv_out] + [((count, wide), BF16)] * 2,
+        pair_scratch
         + [
-            pltpu.VMEM((2 * count, width), BF16),
-            pltpu.VMEM((2 * count, 2 * wide), BF16),
             pltpu.VMEM((2 * count, wide), F32),
             pltpu.VMEM((group, count, tokens), F32),
             pltpu.VMEM((group, count, tokens), BF16),
-            pltpu.SemaphoreType.DMA,
         ],
-        [anywhere] * 4 + [vmem] * parts + [smem] + [vmem] * 4, 10**9,
-        (*mine[last:], *theirs[last:], *pieces, detail, query, most, near, w_project), 22,
+        [vmem] * 5 + [smem] + [vmem] * 4, 10**9,
+        (*strips_at(depth), row, detail, query, kv, near, w_project), 22, {7: 0},
     )
     got = lax.ppermute(send, "tile", swap)
     (updated,) = call(
-        functools.partial(output_kernel, parts=parts),
-        [((count, width), BF16)],
-        modulation + [pltpu.VMEM((count, width), BF16)],
-        [vmem] * (4 + parts), 10**9,
-        (own, keep, got, *pieces, w_output), 16,
+        output_kernel, [((count, width), BF16)],
+        [pltpu.VMEM((count, width), BF16)], [vmem] * 5, 10**9, (own, keep, got, row, w_output), 16,
     )
     return updated[None]
 

time: 64.1 us -> 56.9 us (0.89)
  local copies, waits for them, and re-layouts: 6.15 us -> 0.04 us
  Pallas kernels: 20.7 us -> 17.3 us
  starting transfers between devices: 27 us -> 28.5 us
  waiting for transfers between devices: 9.69 us -> 10.6 us
    ppermute x6, starting transfers between devices: 5.1 us -> 12.9 us  [on_device(): theirs = [lax.ppermute(strip, 'tile', swap) for strip in mine]]
    unnamed x13 -> x14, local copies, waits for them, and re-layouts: 6.15 us -> 0.04 us
    ppermute x6, starting transfers between devices: 15.3 us -> 11.5 us  [the longest x4 5.5 us: on_device(): mine.append(lax.ppermute(mine[step - 2], 'tile', along(step // 2 + 1)))]
    pallas_call x6 -> x8, Pallas kernels: 20.7 us -> 17.3 us  [call(): pl.pallas_call(kernel, out_shape=[jax.ShapeDtypeStruct(shape, dtype) for...]
    ppermute x1, starting transfers between devices: 1.87 us -> 0.3 us  [on_device(): partner = lax.ppermute(own, 'tile', swap)]
    ppermute x6, waiting for transfers between devices: 3.77 us -> 4.74 us  [the longest x1 2.59 us: on_device(): lax.ppermute(own, 'tile', cross)]
    ppermute x3, starting transfers between devices: 4.69 us -> 3.76 us  [exchange_modulation(): pieces.append(lax.ppermute(rows[ahead], 'grp', pairs))]
  transfers between devices with their start and end apart: 17 -> 17, of which waited for: 6 -> 7; matrix products, arithmetic and copies ran while one was open for 4% -> 0% of each run, Pallas kernels for 22% -> 18%
where the time goes in v2:
time: 56.9 us; the launch traced here: 56.7 us
  starting transfers between devices  28.5 us (50%)
  Pallas kernels  17.3 us (30%)
  waiting for transfers between devices  10.6 us (19%)
    pallas_call x8, Pallas kernels, call(): pl.pallas_call(kernel, out_shape=[jax.ShapeDtypeStruct(shape, dtype) for...  17.3 us
    ppermute x6, starting transfers between devices, on_device(): theirs = [lax.ppermute(strip, 'tile', swap) for strip in mine]  12.9 us
    ppermute x4, starting transfers between devices, on_device(): mine.append(lax.ppermute(mine[step - 2], 'tile', along(step // 2 + 1)))  5.5 us
    ppermute x3, waiting for transfers between devices, exchange_modulation(): pieces.append(lax.ppermute(rows[ahead], 'grp', pairs))  4.54 us
    ppermute x1, starting transfers between devices, on_device(): lax.ppermute(own, 'tile', cross)  3.89 us
    ppermute x3, starting transfers between devices, exchange_modulation(): pieces.append(lax.ppermute(rows[ahead], 'grp', pairs))  3.76 us
    ppermute x1, waiting for transfers between devices, on_device(): lax.ppermute(own, 'tile', cross)  2.59 us
    ppermute x1, starting transfers between devices, on_device(): lax.ppermute(own, 'tile', along(1))  2.08 us
  transfers between devices with their start and end apart: 17, of which 7 were waited for; matrix products, arithmetic and copies ran while one was open for 0% of the time, Pallas kernels for 18%

profile of v2, /device:TPU:17, one launch (start us, length us, event | category | flops | bytes accessed | tf_op | source)
XLA Modules:
  0.0 56.7 jit_solution(12559950521177469205)
XLA Ops:
  0.0 0.0 copy-start.3
  0.0 0.0 copy-start.4
  0.0 3.9 %collective-permute-start = (bf16[128,1152]{1,0:T(8,128)(2,1)}, bf16[128,1152]{1,0:T(8,128)(2,1)S(1)}, u32[]{:S(2)}, u32[]{:S(2)}) collective-permute-start(bf16[128,1152]{1,0:T(8,128)(2,1)} %bitcast.5), channel_id=1, source_target_pairs={{1,2},{3,4},{5,6},{2,1},{4,3},{6,5},{9,10},{11,12},{13,14},{10,9},... | collective-permute-start | bytes 884744 | tf_op jit(solution)/shard_map/ppermute | solution.py:288
  3.9 2.1 %collective-permute-start.3 = (bf16[128,1152]{1,0:T(8,128)(2,1)}, bf16[128,1152]{1,0:T(8,128)(2,1)S(1)}, u32[]{:S(2)}, u32[]{:S(2)}) collective-permute-start(bf16[128,1152]{1,0:T(8,128)(2,1)} %bitcast.6), channel_id=1, source_target_pairs={{0,2},{2,4},{4,6},{3,1},{5,3},{7,5},{8,10},{10,12},{12,14},{11,9},... | collective-permute-start | bytes 884744 | tf_op jit(solution)/shard_map/ppermute | solution.py:288
  6.0 0.3 collective-permute-start.8
  6.3 2.6 %collective-permute-done.mine.ours0 = bf16[128,1152]{1,0:T(8,128)(2,1)S(1)} collective-permute-done((bf16[128,1152]{1,0:T(8,128)(2,1)}, bf16[128,1152]{1,0:T(8,128)(2,1)S(1)}, u32[]{:S(2)}, u32[]{:S(2)}) %collective-permute-start) | collective-permute-done | bytes 294944 | tf_op jit(solution)/shard_map/ppermute | solution.py:288
  8.9 2.1 %collective-permute-start.1 = (bf16[128,1152]{1,0:T(8,128)(2,1)S(1)}, bf16[128,1152]{1,0:T(8,128)(2,1)S(1)}, u32[]{:S(2)}, u32[]{:S(2)}) collective-permute-start(bf16[128,1152]{1,0:T(8,128)(2,1)S(1)} %collective-permute-done.mine.ours0), channel_id=1, source_target_pairs={{2,4},{4,6},{3,1},{5,3},{10,12},{12,14},{11,9},{13,11},{18,20},{20... | collective-permute-start | bytes 884744 | tf_op jit(solution)/shard_map/ppermute | solution.py:298
  11.0 0.9 %collective-permute-done.3.ours1 = bf16[128,1152]{1,0:T(8,128)(2,1)S(1)} collective-permute-done((bf16[128,1152]{1,0:T(8,128)(2,1)}, bf16[128,1152]{1,0:T(8,128)(2,1)S(1)}, u32[]{:S(2)}, u32[]{:S(2)}) %collective-permute-start.3) | collective-permute-done | bytes 294944 | tf_op jit(solution)/shard_map/ppermute | solution.py:288
  11.8 2.1 %collective-permute-start.4 = (bf16[128,1152]{1,0:T(8,128)(2,1)S(1)}, bf16[128,1152]{1,0:T(8,128)(2,1)S(1)}, u32[]{:S(2)}, u32[]{:S(2)}) collective-permute-start(bf16[128,1152]{1,0:T(8,128)(2,1)S(1)} %collective-permute-done.3.ours1), channel_id=1, source_target_pairs={{2,4},{4,6},{3,1},{5,3},{10,12},{12,14},{11,9},{13,11},{18,20},{20... | collective-permute-start | bytes 884744 | tf_op jit(solution)/shard_map/ppermute | solution.py:298
  13.9 0.0 slice-start
  13.9 1.9 %collective-permute-start.9 = (bf16[128,1152]{1,0:T(8,128)(2,1)S(1)}, bf16[128,1152]{1,0:T(8,128)(2,1)S(1)}, u32[]{:S(2)}, u32[]{:S(2)}) collective-permute-start(bf16[128,1152]{1,0:T(8,128)(2,1)S(1)} %collective-permute-done.mine.ours0), channel_id=1, source_target_pairs={{0,1},{1,0},{2,3},{3,2},{4,5},{5,4},{6,7},{7,6},{8,9},{9,8},{10,11... | collective-permute-start | bytes 884744 | tf_op jit(solution)/shard_map/ppermute | solution.py:299
  15.8 0.0 collective-permute-done.1.ours0
  15.8 0.7 %collective-permute-start.2 = (bf16[128,1152]{1,0:T(8,128)(2,1)S(1)}, bf16[128,1152]{1,0:T(8,128)(2,1)S(1)}, u32[]{:S(2)}, u32[]{:S(2)}) collective-permute-start(bf16[128,1152]{1,0:T(8,128)(2,1)S(1)} %collective-permute-done.1.ours0), channel_id=1, source_target_pairs={{4,6},{3,1},{12,14},{11,9},{20,22},{19,17},{28,30},{27,25}} | collective-permute-start | bytes 884744 | tf_op jit(solution)/shard_map/ppermute | solution.py:298
  16.5 1.3 %collective-permute-done.4.ours1 = bf16[128,1152]{1,0:T(8,128)(2,1)S(1)} collective-permute-done((bf16[128,1152]{1,0:T(8,128)(2,1)S(1)}, bf16[128,1152]{1,0:T(8,128)(2,1)S(1)}, u32[]{:S(2)}, u32[]{:S(2)}) %collective-permute-start.4) | collective-permute-done | bytes 294944 | tf_op jit(solution)/shard_map/ppermute | solution.py:298
  17.8 0.7 %collective-permute-start.5 = (bf16[128,1152]{1,0:T(8,128)(2,1)S(1)}, bf16[128,1152]{1,0:T(8,128)(2,1)S(1)}, u32[]{:S(2)}, u32[]{:S(2)}) collective-permute-start(bf16[128,1152]{1,0:T(8,128)(2,1)S(1)} %collective-permute-done.4.ours1), channel_id=1, source_target_pairs={{4,6},{3,1},{12,14},{11,9},{20,22},{19,17},{28,30},{27,25}} | collective-permute-start | bytes 884744 | tf_op jit(solution)/shard_map/ppermute | solution.py:298
  18.4 0.0 copy-done.3
  18.4 0.0 copy-done.4
  18.5 0.0 slice-start.1
  18.5 0.0 copy-start
  18.5 0.7 %shard_map.65 = (f32[1,864]{1,0:T(1,128)S(1)}, f32[1,864]{1,0:T(1,128)S(1)}, f32[1,864]{1,0:T(1,128)S(1)}, f32[1,864]{1,0:T(1,128)S(1)}) custom-call(bf16[4,1152]{1,0:T(4,128)(2,1)S(1)} %copy-done.4, bf16[864,1152]{1,0:T(8,128)(2,1)S(1)} %bitcast.10, f32[8,128]{1,0:T(8,128)S(1)} %shard_map.64._), custom_call_target="tpu_custom_call" | custom-call | flops 10000000000 | bytes 50000000 | tf_op jit(solution)/shard_map/pallas_call | solution.py:254
  19.1 1.3 %collective-permute-start.10 = (f32[1,864]{1,0:T(1,128)S(1)}, f32[1,864]{1,0:T(1,128)S(1)}, u32[]{:S(2)}, u32[]{:S(2)}) collective-permute-start(f32[1,864]{1,0:T(1,128)S(1)} %get-tuple-element.15), channel_id=1, source_target_pairs={{0,8},{8,16},{16,24},{24,0},{1,9},{9,17},{17,25},{25,1},{2,10},{10... | collective-permute-start | bytes 10376 | tf_op jit(solution)/shard_map/ppermute | solution.py:249
  20.4 2.1 %collective-permute-done.10.rest_1_ = f32[1,864]{1,0:T(1,128)S(1)} collective-permute-done((f32[1,864]{1,0:T(1,128)S(1)}, f32[1,864]{1,0:T(1,128)S(1)}, u32[]{:S(2)}, u32[]{:S(2)}) %collective-permute-start.10) | collective-permute-done | bytes 3488 | tf_op jit(solution)/shard_map/ppermute | solution.py:249
  22.5 1.2 %collective-permute-start.11 = (f32[1,864]{1,0:T(1,128)S(1)}, f32[1,864]{1,0:T(1,128)S(1)}, u32[]{:S(2)}, u32[]{:S(2)}) collective-permute-start(f32[1,864]{1,0:T(1,128)S(1)} %get-tuple-element.16), channel_id=1, source_target_pairs={{0,16},{8,24},{16,0},{24,8},{1,17},{9,25},{17,1},{25,9},{2,18},{10... | collective-permute-start | bytes 10376 | tf_op jit(solution)/shard_map/ppermute | solution.py:249
  23.8 1.2 %collective-permute-done.11.rest_2_ = f32[1,864]{1,0:T(1,128)S(1)} collective-permute-done((f32[1,864]{1,0:T(1,128)S(1)}, f32[1,864]{1,0:T(1,128)S(1)}, u32[]{:S(2)}, u32[]{:S(2)}) %collective-permute-start.11) | collective-permute-done | bytes 3488 | tf_op jit(solution)/shard_map/ppermute | solution.py:249
  25.0 1.3 %collective-permute-start.12 = (f32[1,864]{1,0:T(1,128)S(1)}, f32[1,864]{1,0:T(1,128)S(1)}, u32[]{:S(2)}, u32[]{:S(2)}) collective-permute-start(f32[1,864]{1,0:T(1,128)S(1)} %get-tuple-element.17), channel_id=1, source_target_pairs={{0,24},{8,0},{16,8},{24,16},{1,25},{9,1},{17,9},{25,17},{2,26},{10... | collective-permute-start | bytes 10376 | tf_op jit(solution)/shard_map/ppermute | solution.py:249
  26.3 1.2 %collective-permute-done.12.rest_3_ = f32[1,864]{1,0:T(1,128)S(1)} collective-permute-done((f32[1,864]{1,0:T(1,128)S(1)}, f32[1,864]{1,0:T(1,128)S(1)}, u32[]{:S(2)}, u32[]{:S(2)}) %collective-permute-start.12) | collective-permute-done | bytes 3488 | tf_op jit(solution)/shard_map/ppermute | solution.py:249
  27.4 10.0 %collective-permute-start.15 = (bf16[128,1152]{1,0:T(8,128)(2,1)S(1)}, bf16[128,1152]{1,0:T(8,128)(2,1)S(1)}, u32[]{:S(2)}, u32[]{:S(2)}) collective-permute-start(bf16[128,1152]{1,0:T(8,128)(2,1)S(1)} %collective-permute-done.3.ours1), channel_id=1, source_target_pairs={{0,1},{1,0},{2,3},{3,2},{4,5},{5,4},{6,7},{7,6},{8,9},{9,8},{10,11... | collective-permute-start | bytes 884744 | tf_op jit(solution)/shard_map/ppermute | solution.py:299
  37.4 0.0 collective-permute-done.8.partner
  37.4 0.0 collective-permute-start.13
  37.4 0.0 collective-permute-done.9.theirs.theirs0
  37.4 0.5 collective-permute-start.14
  37.9 0.0 collective-permute-done.2.ours0
  37.9 0.1 collective-permute-start.6
  38.0 0.0 collective-permute-done.5.ours1
  38.0 0.4 collective-permute-start.7
  38.5 0.0 slice-done
  38.5 0.0 slice-done.1
  38.5 0.0 copy-done
  38.5 2.7 %shard_map.66 = (bf16[256,640]{1,0:T(8,128)(2,1)S(1)}, bf16[384,1280]{1,0:T(8,128)(2,1)S(1)}, f32[1,3456]{1,0:T(1,128)S(1)}) custom-call(bf16[128,1152]{1,0:T(8,128)(2,1)S(1)} %bitcast.8, bf16[128,1152]{1,0:T(8,128)(2,1)S(1)} %collective-permute-done.8.partner, bf16[128,1152]{1,0:T(8,128)(2,1)S(1)} %collective-permute-done.mine.ours0, ...), custom_call_target="tpu_custom_call" | custom-call | flops 2000000000 | bytes 10000000 | tf_op jit(solution)/shard_map/pallas_call | solution.py:254
  41.2 0.0 copy-start.1
  41.2 1.4 %shard_map.69.near = f32[256,640]{1,0:T(8,128)S(1)} custom-call(bf16[256,640]{1,0:T(8,128)(2,1)S(1)} %get-tuple-element.19.query, bf16[384,1280]{1,0:T(8,128)(2,1)S(1)} %get-tuple-element.20.before.kv), custom_call_target="tpu_custom_call" | custom-call | flops 1000000000 | bytes 5000000 | tf_op jit(solution)/shard_map/pallas_call | solution.py:254
  42.6 0.0 collective-permute-done.15.theirs1
  42.6 0.0 copy-done.1
  42.6 3.5 %shard_map.67.before = bf16[1024,1280]{1,0:T(8,128)(2,1)S(1)} custom-call(bf16[128,1152]{1,0:T(8,128)(2,1)S(1)} %collective-permute-done.mine.ours0, bf16[128,1152]{1,0:T(8,128)(2,1)S(1)} %collective-permute-done.3.ours1, bf16[128,1152]{1,0:T(8,128)(2,1)S(1)} %collective-permute-done.9.theirs.theirs0, bf16[128,1152]{1,0:T(8,128)(2,1)S(1)} %collective-permute-done.15.theirs1, ...), custom_call_target="tpu_custom_call" | custom-call | flops 1000000000 | bytes 5000000 | tf_op jit(solution)/shard_map/pallas_call | solution.py:254
  46.1 0.0 collective-permute-done.13.theirs0
  46.1 0.0 collective-permute-done.14.theirs1
  46.1 2.0 %shard_map.68.before = bf16[1024,1280]{1,0:T(8,128)(2,1)S(1)} custom-call(bf16[128,1152]{1,0:T(8,128)(2,1)S(1)} %collective-permute-done.1.ours0, bf16[128,1152]{1,0:T(8,128)(2,1)S(1)} %collective-permute-done.4.ours1, bf16[128,1152]{1,0:T(8,128)(2,1)S(1)} %collective-permute-done.13.theirs0, ...), custom_call_target="tpu_custom_call", output_to_operand_aliasing={{}: (6, {})} | custom-call | flops 1000000000 | bytes 5000000 | tf_op jit(solution)/shard_map/pallas_call | solution.py:254
  48.2 0.0 copy-start.2
  48.2 0.0 collective-permute-done.6.theirs0
  48.2 0.0 collective-permute-done.7.theirs1
  48.2 5.7 %shard_map.70 = (bf16[1024,1280]{1,0:T(8,128)(2,1)S(1)}, bf16[128,640]{1,0:T(8,128)(2,1)S(1)}, bf16[128,640]{1,0:T(8,128)(2,1)S(1)}) custom-call(bf16[128,1152]{1,0:T(8,128)(2,1)S(1)} %collective-permute-done.2.ours0, bf16[128,1152]{1,0:T(8,128)(2,1)S(1)} %collective-permute-done.5.ours1, ...), custom_call_target="tpu_custom_call", output_to_operand_aliasing={{0}: (7, {})} | custom-call | flops 1000000000 | bytes 5000000 | tf_op jit(solution)/shard_map/pallas_call | solution.py:254
  53.9 0.2 collective-permute-start.16
  54.0 1.3 %collective-permute-done.16.got = bf16[128,640]{1,0:T(8,128)(2,1)S(1)} collective-permute-done((bf16[128,640]{1,0:T(8,128)(2,1)S(1)}, bf16[128,640]{1,0:T(8,128)(2,1)S(1)}, u32[]{:S(2)}, u32[]{:S(2)}) %collective-permute-start.16) | collective-permute-done | bytes 163872 | tf_op jit(solution)/shard_map/ppermute | solution.py:343
  55.3 0.0 copy-done.2
  55.3 1.3 %shard_map.71 = bf16[128,1152]{1,0:T(8,128)(2,1)} custom-call(bf16[128,1152]{1,0:T(8,128)(2,1)S(1)} %bitcast.9, bf16[128,640]{1,0:T(8,128)(2,1)S(1)} %get-tuple-element.21.keep, bf16[128,640]{1,0:T(8,128)(2,1)S(1)} %collective-permute-done.16.got, f32[1,3456]{1,0:T(1,128)S(1)} %get-tuple-element.18.row, bf16[1152,1152]{1,0:T(8,128)(2,1)S(1)} %copy-done.2), custom_call_target="tpu_custom_call" | custom-call | flops 1000000000 | bytes 5000000 | tf_op jit(solution)/shard_map/pallas_call | solution.py:254
  (2 shorter events, 0.0 us)
Async XLA Ops:
  0.0 18.4 %copy-start.3 = (bf16[1152,864]{0,1:T(8,128)(2,1)S(1)}, bf16[1152,864]{0,1:T(8,128)(2,1)}, u32[]{:S(2)}) copy-start(bf16[1152,864]{0,1:T(8,128)(2,1)} %param.8) | copy-start | bytes 5971972
  0.0 18.4 %copy-start.4 = (bf16[4,1152]{1,0:T(4,128)(2,1)S(1)}, bf16[4,1152]{1,0:T(4,128)(2,1)}, u32[]{:S(2)}) copy-start(bf16[4,1152]{1,0:T(4,128)(2,1)} %condition.1) | copy-start | bytes 27652
  0.0 8.9 %collective-permute-start = (bf16[128,1152]{1,0:T(8,128)(2,1)}, bf16[128,1152]{1,0:T(8,128)(2,1)S(1)}, u32[]{:S(2)}, u32[]{:S(2)}) collective-permute-start(bf16[128,1152]{1,0:T(8,128)(2,1)} %bitcast.5), channel_id=1, source_target_pairs={{1,2},{3,4},{5,6},{2,1},{4,3},{6,5},{9,10},{11,12},{13,14},{10,9},... | collective-permute-start | bytes 884744 | tf_op jit(solution)/shard_map/ppermute | solution.py:288
  3.9 7.9 %collective-permute-start.3 = (bf16[128,1152]{1,0:T(8,128)(2,1)}, bf16[128,1152]{1,0:T(8,128)(2,1)S(1)}, u32[]{:S(2)}, u32[]{:S(2)}) collective-permute-start(bf16[128,1152]{1,0:T(8,128)(2,1)} %bitcast.6), channel_id=1, source_target_pairs={{0,2},{2,4},{4,6},{3,1},{5,3},{7,5},{8,10},{10,12},{12,14},{11,9},... | collective-permute-start | bytes 884744 | tf_op jit(solution)/shard_map/ppermute | solution.py:288
  6.0 31.4 %collective-permute-start.8 = (bf16[128,1152]{1,0:T(8,128)(2,1)}, bf16[128,1152]{1,0:T(8,128)(2,1)S(1)}, u32[]{:S(2)}, u32[]{:S(2)}) collective-permute-start(bf16[128,1152]{1,0:T(8,128)(2,1)} %bitcast.7), channel_id=1, source_target_pairs={{0,1},{1,0},{2,3},{3,2},{4,5},{5,4},{6,7},{7,6},{8,9},{9,8},{10,11... | collective-permute-start | bytes 884744 | tf_op jit(solution)/shard_map/ppermute | solution.py:289
  8.9 6.9 %collective-permute-start.1 = (bf16[128,1152]{1,0:T(8,128)(2,1)S(1)}, bf16[128,1152]{1,0:T(8,128)(2,1)S(1)}, u32[]{:S(2)}, u32[]{:S(2)}) collective-permute-start(bf16[128,1152]{1,0:T(8,128)(2,1)S(1)} %collective-permute-done.mine.ours0), channel_id=1, source_target_pairs={{2,4},{4,6},{3,1},{5,3},{10,12},{12,14},{11,9},{13,11},{18,20},{20... | collective-permute-start | bytes 884744 | tf_op jit(solution)/shard_map/ppermute | solution.py:298
  11.8 5.9 %collective-permute-start.4 = (bf16[128,1152]{1,0:T(8,128)(2,1)S(1)}, bf16[128,1152]{1,0:T(8,128)(2,1)S(1)}, u32[]{:S(2)}, u32[]{:S(2)}) collective-permute-start(bf16[128,1152]{1,0:T(8,128)(2,1)S(1)} %collective-permute-done.3.ours1), channel_id=1, source_target_pairs={{2,4},{4,6},{3,1},{5,3},{10,12},{12,14},{11,9},{13,11},{18,20},{20... | collective-permute-start | bytes 884744 | tf_op jit(solution)/shard_map/ppermute | solution.py:298
  13.9 24.6 %slice-start = ((s8[7962624]{0:T(1024)(128)(4,1)}), s8[4194304]{0:T(1024)(128)(4,1)S(1)}, s32[]{:S(2)}) async-start(s8[7962624]{0:T(1024)(128)(4,1)} %bitcast.3), calls=%async_computation | async-start | bytes 8388608
  13.9 23.5 %collective-permute-start.9 = (bf16[128,1152]{1,0:T(8,128)(2,1)S(1)}, bf16[128,1152]{1,0:T(8,128)(2,1)S(1)}, u32[]{:S(2)}, u32[]{:S(2)}) collective-permute-start(bf16[128,1152]{1,0:T(8,128)(2,1)S(1)} %collective-permute-done.mine.ours0), channel_id=1, source_target_pairs={{0,1},{1,0},{2,3},{3,2},{4,5},{5,4},{6,7},{7,6},{8,9},{9,8},{10,11... | collective-permute-start | bytes 884744 | tf_op jit(solution)/shard_map/ppermute | solution.py:299
  15.8 22.2 %collective-permute-start.2 = (bf16[128,1152]{1,0:T(8,128)(2,1)S(1)}, bf16[128,1152]{1,0:T(8,128)(2,1)S(1)}, u32[]{:S(2)}, u32[]{:S(2)}) collective-permute-start(bf16[128,1152]{1,0:T(8,128)(2,1)S(1)} %collective-permute-done.1.ours0), channel_id=1, source_target_pairs={{4,6},{3,1},{12,14},{11,9},{20,22},{19,17},{28,30},{27,25}} | collective-permute-start | bytes 884744 | tf_op jit(solution)/shard_map/ppermute | solution.py:298
  17.8 20.3 %collective-permute-start.5 = (bf16[128,1152]{1,0:T(8,128)(2,1)S(1)}, bf16[128,1152]{1,0:T(8,128)(2,1)S(1)}, u32[]{:S(2)}, u32[]{:S(2)}) collective-permute-start(bf16[128,1152]{1,0:T(8,128)(2,1)S(1)} %collective-permute-done.4.ours1), channel_id=1, source_target_pairs={{4,6},{3,1},{12,14},{11,9},{20,22},{19,17},{28,30},{27,25}} | collective-permute-start | bytes 884744 | tf_op jit(solution)/shard_map/ppermute | solution.py:298
  18.5 20.0 %slice-start.1 = ((s8[7962624]{0:T(1024)(128)(4,1)}), s8[3768320]{0:T(1024)(128)(4,1)S(1)}, s32[]{:S(2)}) async-start(s8[7962624]{0:T(1024)(128)(4,1)} %bitcast.3), calls=%async_computation.1 | async-start | bytes 7536640
  18.5 20.0 %copy-start = (bf16[1,128,1152]{2,1,0:T(8,128)(2,1)S(1)}, bf16[1,128,1152]{2,1,0:T(8,128)(2,1)}, u32[]{:S(2)}) copy-start(bf16[1,128,1152]{2,1,0:T(8,128)(2,1)} %param.6) | copy-start | bytes 884740
  19.1 3.4 %collective-permute-start.10 = (f32[1,864]{1,0:T(1,128)S(1)}, f32[1,864]{1,0:T(1,128)S(1)}, u32[]{:S(2)}, u32[]{:S(2)}) collective-permute-start(f32[1,864]{1,0:T(1,128)S(1)} %get-tuple-element.15), channel_id=1, source_target_pairs={{0,8},{8,16},{16,24},{24,0},{1,9},{9,17},{17,25},{25,1},{2,10},{10... | collective-permute-start | bytes 10376 | tf_op jit(solution)/shard_map/ppermute | solution.py:249
  22.5 2.5 %collective-permute-start.11 = (f32[1,864]{1,0:T(1,128)S(1)}, f32[1,864]{1,0:T(1,128)S(1)}, u32[]{:S(2)}, u32[]{:S(2)}) collective-permute-start(f32[1,864]{1,0:T(1,128)S(1)} %get-tuple-element.16), channel_id=1, source_target_pairs={{0,16},{8,24},{16,0},{24,8},{1,17},{9,25},{17,1},{25,9},{2,18},{10... | collective-permute-start | bytes 10376 | tf_op jit(solution)/shard_map/ppermute | solution.py:249
  25.0 2.5 %collective-permute-start.12 = (f32[1,864]{1,0:T(1,128)S(1)}, f32[1,864]{1,0:T(1,128)S(1)}, u32[]{:S(2)}, u32[]{:S(2)}) collective-permute-start(f32[1,864]{1,0:T(1,128)S(1)} %get-tuple-element.17), channel_id=1, source_target_pairs={{0,24},{8,0},{16,8},{24,16},{1,25},{9,1},{17,9},{25,17},{2,26},{10... | collective-permute-start | bytes 10376 | tf_op jit(solution)/shard_map/ppermute | solution.py:249
  27.4 15.1 %collective-permute-start.15 = (bf16[128,1152]{1,0:T(8,128)(2,1)S(1)}, bf16[128,1152]{1,0:T(8,128)(2,1)S(1)}, u32[]{:S(2)}, u32[]{:S(2)}) collective-permute-start(bf16[128,1152]{1,0:T(8,128)(2,1)S(1)} %collective-permute-done.3.ours1), channel_id=1, source_target_pairs={{0,1},{1,0},{2,3},{3,2},{4,5},{5,4},{6,7},{7,6},{8,9},{9,8},{10,11... | collective-permute-start | bytes 884744 | tf_op jit(solution)/shard_map/ppermute | solution.py:299
  37.4 8.7 %collective-permute-start.13 = (bf16[128,1152]{1,0:T(8,128)(2,1)S(1)}, bf16[128,1152]{1,0:T(8,128)(2,1)S(1)}, u32[]{:S(2)}, u32[]{:S(2)}) collective-permute-start(bf16[128,1152]{1,0:T(8,128)(2,1)S(1)} %collective-permute-done.1.ours0), channel_id=1, source_target_pairs={{0,1},{1,0},{2,3},{3,2},{4,5},{5,4},{6,7},{7,6},{8,9},{9,8},{10,11... | collective-permute-start | bytes 884744 | tf_op jit(solution)/shard_map/ppermute | solution.py:299
  37.4 8.7 %collective-permute-start.14 = (bf16[128,1152]{1,0:T(8,128)(2,1)S(1)}, bf16[128,1152]{1,0:T(8,128)(2,1)S(1)}, u32[]{:S(2)}, u32[]{:S(2)}) collective-permute-start(bf16[128,1152]{1,0:T(8,128)(2,1)S(1)} %collective-permute-done.4.ours1), channel_id=1, source_target_pairs={{0,1},{1,0},{2,3},{3,2},{4,5},{5,4},{6,7},{7,6},{8,9},{9,8},{10,11... | collective-permute-start | bytes 884744 | tf_op jit(solution)/shard_map/ppermute | solution.py:299
  37.9 10.2 %collective-permute-start.6 = (bf16[128,1152]{1,0:T(8,128)(2,1)S(1)}, bf16[128,1152]{1,0:T(8,128)(2,1)S(1)}, u32[]{:S(2)}, u32[]{:S(2)}) collective-permute-start(bf16[128,1152]{1,0:T(8,128)(2,1)S(1)} %collective-permute-done.2.ours0), channel_id=1, source_target_pairs={{0,1},{1,0},{2,3},{3,2},{4,5},{5,4},{6,7},{7,6},{8,9},{9,8},{10,11... | collective-permute-start | bytes 884744 | tf_op jit(solution)/shard_map/ppermute | solution.py:299
  38.0 10.2 %collective-permute-start.7 = (bf16[128,1152]{1,0:T(8,128)(2,1)S(1)}, bf16[128,1152]{1,0:T(8,128)(2,1)S(1)}, u32[]{:S(2)}, u32[]{:S(2)}) collective-permute-start(bf16[128,1152]{1,0:T(8,128)(2,1)S(1)} %collective-permute-done.5.ours1), channel_id=1, source_target_pairs={{0,1},{1,0},{2,3},{3,2},{4,5},{5,4},{6,7},{7,6},{8,9},{9,8},{10,11... | collective-permute-start | bytes 884744 | tf_op jit(solution)/shard_map/ppermute | solution.py:299
  41.2 1.4 %copy-start.1 = (s32[1,8]{1,0:T(1,128)S(1)}, s32[1,8]{1,0:T(1,128)}, u32[]{:S(2)}) copy-start(s32[1,8]{1,0:T(1,128)} %marks.5) | copy-start | bytes 100
  48.2 7.2 %copy-start.2 = (bf16[1152,1152]{1,0:T(8,128)(2,1)S(1)}, bf16[1152,1152]{1,0:T(8,128)(2,1)}, u32[]{:S(2)}) copy-start(bf16[1152,1152]{1,0:T(8,128)(2,1)} %wo.1) | copy-start | bytes 7962628
  53.9 1.5 %collective-permute-start.16 = (bf16[128,640]{1,0:T(8,128)(2,1)S(1)}, bf16[128,640]{1,0:T(8,128)(2,1)S(1)}, u32[]{:S(2)}, u32[]{:S(2)}) collective-permute-start(bf16[128,640]{1,0:T(8,128)(2,1)S(1)} %get-tuple-element.22), channel_id=1, source_target_pairs={{0,1},{1,0},{2,3},{3,2},{4,5},{5,4},{6,7},{7,6},{8,9},{9,8},{10,11... | collective-permute-start | bytes 491528 | tf_op jit(solution)/shard_map/ppermute | solution.py:343

commit v3 on v2

--- a/solution.py
+++ b/solution.py
@@ -154,22 +154,26 @@
 
 
 def chip_marks(marks, chip):
-    return [marks[0, 2 * chip] > 0, marks[0, 2 * chip + 1] > 0]
-
-
-def pair_kernel(ours0, ours1, theirs0, theirs1, row, marks, before, w, kv, normed, *, distance, first_call):
+    values = marks[...]
+    column = lax.broadcasted_iota(jnp.int32, values.shape, 1)
+    return [jnp.max(jnp.where(column == 2 * chip + core, values, 0)) > 0 for core in range(2)]
+
+
+def strip_kernel(*refs, strips, distance, offset):
+    ours, theirs = refs[:strips], refs[strips : 2 * strips]
+    row, marks, before, w, kv, normed = refs[2 * strips :]
     _, chip, _ = place_of_chip()
     marked = chip_marks(marks, chip)
-    count = ours0.shape[0]
+    count = ours[0].shape[0]
 
     @pl.when(marked[0] | marked[1])
     def _():
-        if first_call:
+        if distance == 1:
             kv[: 2 * count] = before[ROW_TOKENS : ROW_TOKENS + 2 * count]
-        add_pairs((ours0, ours1), (theirs0, theirs1), row, w, kv, normed, distance)
-
-
-def add_pairs(ours, theirs, row, w, kv, normed, distance):
+        add_pairs(ours, theirs, row, w, kv, normed, distance, offset * count)
+
+
+def add_pairs(ours, theirs, row, w, kv, normed, distance, offset):
     count, width = ours[0].shape
     core, chip, chips = place_of_chip()
     first, wide = half_columns(width)
@@ -185,21 +189,22 @@
 
         @pl.when(have)
         def _(pair=pair, slot=slot):
-            at = pl.multiple_of(2 * count * (slot + 1), 2 * count)
+            at = pl.multiple_of(2 * count * (slot + 1) + offset, count)
+            rows = len(pair) * count
             for k, strip in enumerate(pair):
                 normalize_rows(strip, 0, normed, k * count, count, shift, scale)
             for section in range(2):
                 columns = pl.ds(pl.multiple_of((section + 1) * width + first * core, LANES), wide)
-                kv[pl.ds(at, 2 * count), section * wide : (section + 1) * wide] = jnp.dot(
-                    normed[...], w[:, columns], preferred_element_type=F32
+                kv[pl.ds(at, rows), section * wide : (section + 1) * wide] = jnp.dot(
+                    normed[:rows], w[:, columns], preferred_element_type=F32
                 ).astype(BF16)
 
 
 def late_kernel(
-    ours0, ours1, theirs0, theirs1, row, marks, query, before, near, w,
+    ours, theirs, row, marks, query, before, near, w,
     kv, keep, send, normed, whole, scores, probs, *, distance,
 ):
-    count, width = ours0.shape
+    count, width = ours.shape
     _, wide = half_columns(width)
     core, chip, _ = place_of_chip()
     marked = chip_marks(marks, chip)
@@ -207,7 +212,7 @@
 
     @pl.when(marked[0] | marked[1])
     def _():
-        add_pairs((ours0, ours1), (theirs0, theirs1), row, w, kv, normed, distance)
+        add_pairs((ours,), (theirs,), row, w, kv, normed, distance, count)
 
     for strip in range(2):
 
@@ -275,8 +280,6 @@
     rows = 2 * count + 2 * ROW_TOKENS
     tokens = count * tiles
     vmem = pl.BlockSpec(memory_space=pltpu.VMEM)
-    anywhere = pl.BlockSpec(memory_space=pl.ANY)
-    smem = pl.BlockSpec(memory_space=pltpu.SMEM)
     swap = [(i, i ^ 1) for i in range(tiles)]
 
     def along(distance):
@@ -317,15 +320,14 @@
     kv_out = ((tokens, 2 * wide), BF16)
     pair_scratch = [pltpu.VMEM((2 * count, width), BF16)]
 
-    def strips_at(distance):
-        at = slice(2 * distance - 2, 2 * distance)
-        return (*mine[at], *theirs[at])
-
-    for distance in range(1, depth):
+    groups = [(0, 2)] + [(at, 1) for at in range(2, len(mine) - 1)]
+    for at, strips in groups:
+        some = slice(at, at + strips)
         (kv,) = call(
-            functools.partial(pair_kernel, distance=distance, first_call=distance == 1),
-            [kv_out], pair_scratch, [vmem] * 5 + [smem] + [vmem] * 2, 10**9,
-            (*strips_at(distance), row, detail, kv, w_project), 12, {} if distance == 1 else {6: 0},
+            functools.partial(strip_kernel, strips=strips, distance=at // 2 + 1, offset=at % 2),
+            [kv_out], pair_scratch, [vmem] * (2 * strips + 4), 10**9,
+            (*mine[some], *theirs[some], row, detail, kv, w_project), 12,
+            {} if at == 0 else {2 * strips + 2: 0},
         )
     group = max(1, min(HEADS // 2, 2**20 // (count * tokens)))
     _, keep, send = call(
@@ -337,8 +339,8 @@
             pltpu.VMEM((group, count, tokens), F32),
             pltpu.VMEM((group, count, tokens), BF16),
         ],
-        [vmem] * 5 + [smem] + [vmem] * 4, 10**9,
-        (*strips_at(depth), row, detail, query, kv, near, w_project), 22, {7: 0},
+        [vmem] * 8, 10**9,
+        (mine[-1], theirs[-1], row, detail, query, kv, near, w_project), 22, {5: 0},
     )
     got = lax.ppermute(send, "tile", swap)
     (updated,) = call(

time: 56.9 us -> 53.4 us (0.938)
  waiting for transfers between devices: 10.6 us -> 7.31 us
    ppermute x4, waiting for transfers between devices: 1.3 us -> 0.01 us  [on_device(): mine.append(lax.ppermute(mine[step - 2], 'tile', along(step // 2 + 1)))]
    ppermute x3, waiting for transfers between devices: 4.54 us -> 3.42 us  [exchange_modulation(): pieces.append(lax.ppermute(rows[ahead], 'grp', pairs))]
    ppermute x1, waiting for transfers between devices: 0.85 us -> 0.01 us  [on_device(): lax.ppermute(own, 'tile', along(1))]
    ppermute x3, starting transfers between devices: 3.76 us -> 4.35 us  [exchange_modulation(): pieces.append(lax.ppermute(rows[ahead], 'grp', pairs))]
    pallas_call x8 -> x10, Pallas kernels: 17.3 us -> 17 us  [call(): pl.pallas_call(kernel, out_shape=[jax.ShapeDtypeStruct(shape, dtype) for...]
  transfers between devices with their start and end apart: 17 -> 17, of which waited for: 7 -> 5; matrix products, arithmetic and copies ran while one was open for 0% -> 0% of each run, Pallas kernels for 18% -> 20%
where the time goes in v3:
time: 53.4 us; the launch traced here: 53.2 us
  starting transfers between devices  28.6 us (54%)
  Pallas kernels  17 us (32%)
  waiting for transfers between devices  7.31 us (14%)
    pallas_call x10, Pallas kernels, call(): pl.pallas_call(kernel, out_shape=[jax.ShapeDtypeStruct(shape, dtype) for...  17 us
    ppermute x6, starting transfers between devices, on_device(): theirs = [lax.ppermute(strip, 'tile', swap) for strip in mine]  13 us
    ppermute x4, starting transfers between devices, on_device(): mine.append(lax.ppermute(mine[step - 2], 'tile', along(step // 2 + 1)))  5.04 us
    ppermute x3, starting transfers between devices, exchange_modulation(): pieces.append(lax.ppermute(rows[ahead], 'grp', pairs))  4.35 us
    ppermute x1, starting transfers between devices, on_device(): lax.ppermute(own, 'tile', cross)  3.89 us
    ppermute x3, waiting for transfers between devices, exchange_modulation(): pieces.append(lax.ppermute(rows[ahead], 'grp', pairs))  3.42 us
    ppermute x1, waiting for transfers between devices, on_device(): lax.ppermute(own, 'tile', cross)  2.59 us
    ppermute x1, starting transfers between devices, on_device(): lax.ppermute(own, 'tile', along(1))  2.08 us
  transfers between devices with their start and end apart: 17, of which 5 were waited for; matrix products, arithmetic and copies ran while one was open for 0% of the time, Pallas kernels for 20%

profile of v3, /device:TPU:17, one launch (start us, length us, event | category | flops | bytes accessed | tf_op | source)
XLA Modules:
  0.0 53.2 jit_solution(16465482690752154345)
XLA Ops:
  0.0 0.0 copy-start.3
  0.0 0.0 copy-start.4
  0.0 3.9 %collective-permute-start.5 = (bf16[128,1152]{1,0:T(8,128)(2,1)}, bf16[128,1152]{1,0:T(8,128)(2,1)S(1)}, u32[]{:S(2)}, u32[]{:S(2)}) collective-permute-start(bf16[128,1152]{1,0:T(8,128)(2,1)} %bitcast.5), channel_id=1, source_target_pairs={{1,2},{3,4},{5,6},{2,1},{4,3},{6,5},{9,10},{11,12},{13,14},{10,9},... | collective-permute-start | bytes 884744 | tf_op jit(solution)/shard_map/ppermute | solution.py:291
  3.9 0.1 collective-permute-start.4
  4.0 2.1 %collective-permute-start = (bf16[128,1152]{1,0:T(8,128)(2,1)}, bf16[128,1152]{1,0:T(8,128)(2,1)S(1)}, u32[]{:S(2)}, u32[]{:S(2)}) collective-permute-start(bf16[128,1152]{1,0:T(8,128)(2,1)} %bitcast.7), channel_id=1, source_target_pairs={{0,2},{2,4},{4,6},{3,1},{5,3},{7,5},{8,10},{10,12},{12,14},{11,9},... | collective-permute-start | bytes 884744 | tf_op jit(solution)/shard_map/ppermute | solution.py:291
  6.1 2.6 %collective-permute-done.5.mine.refs_0_ = bf16[128,1152]{1,0:T(8,128)(2,1)S(1)} collective-permute-done((bf16[128,1152]{1,0:T(8,128)(2,1)}, bf16[128,1152]{1,0:T(8,128)(2,1)S(1)}, u32[]{:S(2)}, u32[]{:S(2)}) %collective-permute-start.5) | collective-permute-done | bytes 294944 | tf_op jit(solution)/shard_map/ppermute | solution.py:291
  8.7 2.1 %collective-permute-start.10 = (bf16[128,1152]{1,0:T(8,128)(2,1)S(1)}, bf16[128,1152]{1,0:T(8,128)(2,1)S(1)}, u32[]{:S(2)}, u32[]{:S(2)}) collective-permute-start(bf16[128,1152]{1,0:T(8,128)(2,1)S(1)} %collective-permute-done.5.mine.refs_0_), channel_id=1, source_target_pairs={{2,4},{4,6},{3,1},{5,3},{10,12},{12,14},{11,9},{13,11},{18,20},{20... | collective-permute-start | bytes 884744 | tf_op jit(solution)/shard_map/ppermute | solution.py:301
  10.7 0.0 slice-start
  10.8 2.3 %collective-permute-start.6 = (bf16[128,1152]{1,0:T(8,128)(2,1)S(1)}, bf16[128,1152]{1,0:T(8,128)(2,1)S(1)}, u32[]{:S(2)}, u32[]{:S(2)}) collective-permute-start(bf16[128,1152]{1,0:T(8,128)(2,1)S(1)} %collective-permute-done.5.mine.refs_0_), channel_id=1, source_target_pairs={{0,1},{1,0},{2,3},{3,2},{4,5},{5,4},{6,7},{7,6},{8,9},{9,8},{10,11... | collective-permute-start | bytes 884744 | tf_op jit(solution)/shard_map/ppermute | solution.py:302
  13.1 0.0 collective-permute-done.refs_1_
  13.1 1.6 %collective-permute-start.1 = (bf16[128,1152]{1,0:T(8,128)(2,1)S(1)}, bf16[128,1152]{1,0:T(8,128)(2,1)S(1)}, u32[]{:S(2)}, u32[]{:S(2)}) collective-permute-start(bf16[128,1152]{1,0:T(8,128)(2,1)S(1)} %collective-permute-done.refs_1_), channel_id=1, source_target_pairs={{2,4},{4,6},{3,1},{5,3},{10,12},{12,14},{11,9},{13,11},{18,20},{20... | collective-permute-start | bytes 884744 | tf_op jit(solution)/shard_map/ppermute | solution.py:301
  14.7 0.0 collective-permute-done.10.refs_0_
  14.7 0.7 %collective-permute-start.11 = (bf16[128,1152]{1,0:T(8,128)(2,1)S(1)}, bf16[128,1152]{1,0:T(8,128)(2,1)S(1)}, u32[]{:S(2)}, u32[]{:S(2)}) collective-permute-start(bf16[128,1152]{1,0:T(8,128)(2,1)S(1)} %collective-permute-done.10.refs_0_), channel_id=1, source_target_pairs={{4,6},{3,1},{12,14},{11,9},{20,22},{19,17},{28,30},{27,25}} | collective-permute-start | bytes 884744 | tf_op jit(solution)/shard_map/ppermute | solution.py:301
  15.4 0.0 copy-done.3
  15.4 0.0 copy-done.4
  15.4 0.0 slice-start.1
  15.5 0.0 copy-start
  15.5 0.7 %shard_map.65 = (f32[1,864]{1,0:T(1,128)S(1)}, f32[1,864]{1,0:T(1,128)S(1)}, f32[1,864]{1,0:T(1,128)S(1)}, f32[1,864]{1,0:T(1,128)S(1)}) custom-call(bf16[4,1152]{1,0:T(4,128)(2,1)S(1)} %copy-done.4, bf16[864,1152]{1,0:T(8,128)(2,1)S(1)} %bitcast.10, f32[8,128]{1,0:T(8,128)S(1)} %shard_map.64._), custom_call_target="tpu_custom_call" | custom-call | flops 10000000000 | bytes 50000000 | tf_op jit(solution)/shard_map/pallas_call | solution.py:259
  16.1 1.3 %collective-permute-start.7 = (f32[1,864]{1,0:T(1,128)S(1)}, f32[1,864]{1,0:T(1,128)S(1)}, u32[]{:S(2)}, u32[]{:S(2)}) collective-permute-start(f32[1,864]{1,0:T(1,128)S(1)} %get-tuple-element.15), channel_id=1, source_target_pairs={{0,8},{8,16},{16,24},{24,0},{1,9},{9,17},{17,25},{25,1},{2,10},{10... | collective-permute-start | bytes 10376 | tf_op jit(solution)/shard_map/ppermute | solution.py:254
  17.4 2.1 %collective-permute-done.7.rest_1_ = f32[1,864]{1,0:T(1,128)S(1)} collective-permute-done((f32[1,864]{1,0:T(1,128)S(1)}, f32[1,864]{1,0:T(1,128)S(1)}, u32[]{:S(2)}, u32[]{:S(2)}) %collective-permute-start.7) | collective-permute-done | bytes 3488 | tf_op jit(solution)/shard_map/ppermute | solution.py:254
  19.5 1.2 %collective-permute-start.8 = (f32[1,864]{1,0:T(1,128)S(1)}, f32[1,864]{1,0:T(1,128)S(1)}, u32[]{:S(2)}, u32[]{:S(2)}) collective-permute-start(f32[1,864]{1,0:T(1,128)S(1)} %get-tuple-element.16), channel_id=1, source_target_pairs={{0,16},{8,24},{16,0},{24,8},{1,17},{9,25},{17,1},{25,9},{2,18},{10... | collective-permute-start | bytes 10376 | tf_op jit(solution)/shard_map/ppermute | solution.py:254
  20.8 1.2 %collective-permute-done.8.rest_2_ = f32[1,864]{1,0:T(1,128)S(1)} collective-permute-done((f32[1,864]{1,0:T(1,128)S(1)}, f32[1,864]{1,0:T(1,128)S(1)}, u32[]{:S(2)}, u32[]{:S(2)}) %collective-permute-start.8) | collective-permute-done | bytes 3488 | tf_op jit(solution)/shard_map/ppermute | solution.py:254
  22.0 1.9 %collective-permute-start.9 = (f32[1,864]{1,0:T(1,128)S(1)}, f32[1,864]{1,0:T(1,128)S(1)}, u32[]{:S(2)}, u32[]{:S(2)}) collective-permute-start(f32[1,864]{1,0:T(1,128)S(1)} %get-tuple-element.17), channel_id=1, source_target_pairs={{0,24},{8,0},{16,8},{24,16},{1,25},{9,1},{17,9},{25,17},{2,26},{10... | collective-permute-start | bytes 10376 | tf_op jit(solution)/shard_map/ppermute | solution.py:254
  23.8 0.0 collective-permute-done.1.refs_0_
  23.8 0.7 %collective-permute-start.2 = (bf16[128,1152]{1,0:T(8,128)(2,1)S(1)}, bf16[128,1152]{1,0:T(8,128)(2,1)S(1)}, u32[]{:S(2)}, u32[]{:S(2)}) collective-permute-start(bf16[128,1152]{1,0:T(8,128)(2,1)S(1)} %collective-permute-done.1.refs_0_), channel_id=1, source_target_pairs={{4,6},{3,1},{12,14},{11,9},{20,22},{19,17},{28,30},{27,25}} | collective-permute-start | bytes 884744 | tf_op jit(solution)/shard_map/ppermute | solution.py:301
  24.5 0.1 collective-permute-done.9.rest_3_
  24.6 9.5 %collective-permute-start.15 = (bf16[128,1152]{1,0:T(8,128)(2,1)S(1)}, bf16[128,1152]{1,0:T(8,128)(2,1)S(1)}, u32[]{:S(2)}, u32[]{:S(2)}) collective-permute-start(bf16[128,1152]{1,0:T(8,128)(2,1)S(1)} %collective-permute-done.refs_1_), channel_id=1, source_target_pairs={{0,1},{1,0},{2,3},{3,2},{4,5},{5,4},{6,7},{7,6},{8,9},{9,8},{10,11... | collective-permute-start | bytes 884744 | tf_op jit(solution)/shard_map/ppermute | solution.py:302
  34.1 0.0 collective-permute-done.4.partner
  34.1 0.0 collective-permute-start.14
  34.1 0.0 collective-permute-done.6.theirs.refs_2_
  34.1 0.5 collective-permute-start.13
  34.6 0.0 slice-done
  34.6 0.0 slice-done.1
  34.6 0.0 copy-done
  34.6 2.7 %shard_map.66 = (bf16[256,640]{1,0:T(8,128)(2,1)S(1)}, bf16[384,1280]{1,0:T(8,128)(2,1)S(1)}, f32[1,3456]{1,0:T(1,128)S(1)}) custom-call(bf16[128,1152]{1,0:T(8,128)(2,1)S(1)} %bitcast.8, bf16[128,1152]{1,0:T(8,128)(2,1)S(1)} %collective-permute-done.4.partner, bf16[128,1152]{1,0:T(8,128)(2,1)S(1)} %collective-permute-done.5.mine.refs_0_, ...), custom_call_target="tpu_custom_call" | custom-call | flops 2000000000 | bytes 10000000 | tf_op jit(solution)/shard_map/pallas_call | solution.py:259
  37.3 0.0 copy-start.1
  37.3 0.0 collective-permute-done.11.refs_0_
  37.4 0.1 collective-permute-start.12
  37.5 1.3 %shard_map.71.near = f32[256,640]{1,0:T(8,128)S(1)} custom-call(bf16[256,640]{1,0:T(8,128)(2,1)S(1)} %get-tuple-element.19.query, bf16[384,1280]{1,0:T(8,128)(2,1)S(1)} %get-tuple-element.20.refs_6_.kv), custom_call_target="tpu_custom_call" | custom-call | flops 1000000000 | bytes 5000000 | tf_op jit(solution)/shard_map/pallas_call | solution.py:259
  38.8 0.0 collective-permute-done.2.ours
  38.8 0.5 collective-permute-start.3
  39.4 0.0 collective-permute-done.15.refs_3_
  39.4 0.0 copy-done.1
  39.4 3.2 %shard_map.67.refs_4_ = bf16[1024,1280]{1,0:T(8,128)(2,1)S(1)} custom-call(bf16[128,1152]{1,0:T(8,128)(2,1)S(1)} %collective-permute-done.5.mine.refs_0_, bf16[128,1152]{1,0:T(8,128)(2,1)S(1)} %collective-permute-done.refs_1_, bf16[128,1152]{1,0:T(8,128)(2,1)S(1)} %collective-permute-done.6.theirs.refs_2_, ...), custom_call_target="tpu_custom_call" | custom-call | flops 1000000000 | bytes 5000000 | tf_op jit(solution)/shard_map/pallas_call | solution.py:259
  42.5 0.0 collective-permute-done.14.refs_1_
  42.5 1.1 %shard_map.68.refs_4_ = bf16[1024,1280]{1,0:T(8,128)(2,1)S(1)} custom-call(bf16[128,1152]{1,0:T(8,128)(2,1)S(1)} %collective-permute-done.10.refs_0_, bf16[128,1152]{1,0:T(8,128)(2,1)S(1)} %collective-permute-done.14.refs_1_, f32[1,3456]{1,0:T(1,128)S(1)} %get-tuple-element.18.refs_4_.refs_2_.row, ...), custom_call_target="tpu_custom_call", output_to_operand_aliasing={{}: (4, {})} | custom-call | flops 1000000000 | bytes 5000000 | tf_op jit(solution)/shard_map/pallas_call | solution.py:259
  43.7 0.0 collective-permute-done.13.refs_1_
  43.7 1.1 %shard_map.69.refs_4_ = bf16[1024,1280]{1,0:T(8,128)(2,1)S(1)} custom-call(bf16[128,1152]{1,0:T(8,128)(2,1)S(1)} %collective-permute-done.1.refs_0_, bf16[128,1152]{1,0:T(8,128)(2,1)S(1)} %collective-permute-done.13.refs_1_, f32[1,3456]{1,0:T(1,128)S(1)} %get-tuple-element.18.refs_4_.refs_2_.row, ...), custom_call_target="tpu_custom_call", output_to_operand_aliasing={{}: (4, {})} | custom-call | flops 1000000000 | bytes 5000000 | tf_op jit(solution)/shard_map/pallas_call | solution.py:259
  44.8 0.0 collective-permute-done.12.refs_1_
  44.8 0.4 shard_map.70.before
  45.2 0.0 copy-start.2
  45.2 0.0 collective-permute-done.3.theirs
  45.2 5.1 %shard_map.72 = (bf16[1024,1280]{1,0:T(8,128)(2,1)S(1)}, bf16[128,640]{1,0:T(8,128)(2,1)S(1)}, bf16[128,640]{1,0:T(8,128)(2,1)S(1)}) custom-call(bf16[128,1152]{1,0:T(8,128)(2,1)S(1)} %collective-permute-done.2.ours, bf16[128,1152]{1,0:T(8,128)(2,1)S(1)} %collective-permute-done.3.theirs, ...), custom_call_target="tpu_custom_call", output_to_operand_aliasing={{0}: (5, {})} | custom-call | flops 1000000000 | bytes 5000000 | tf_op jit(solution)/shard_map/pallas_call | solution.py:259
  50.4 0.2 collective-permute-start.16
  50.6 1.3 %collective-permute-done.16.got = bf16[128,640]{1,0:T(8,128)(2,1)S(1)} collective-permute-done((bf16[128,640]{1,0:T(8,128)(2,1)S(1)}, bf16[128,640]{1,0:T(8,128)(2,1)S(1)}, u32[]{:S(2)}, u32[]{:S(2)}) %collective-permute-start.16) | collective-permute-done | bytes 163872 | tf_op jit(solution)/shard_map/ppermute | solution.py:345
  51.8 0.0 copy-done.2
  51.8 1.3 %shard_map.73 = bf16[128,1152]{1,0:T(8,128)(2,1)} custom-call(bf16[128,1152]{1,0:T(8,128)(2,1)S(1)} %bitcast.9, bf16[128,640]{1,0:T(8,128)(2,1)S(1)} %get-tuple-element.21.keep, bf16[128,640]{1,0:T(8,128)(2,1)S(1)} %collective-permute-done.16.got, f32[1,3456]{1,0:T(1,128)S(1)} %get-tuple-element.18.refs_4_.refs_2_.row, bf16[1152,1152]{1,0:T(8,128)(2,1)S(1)} %copy-done.2), custom_call_target="tpu_custom_call" | custom-call | flops 1000000000 | bytes 5000000 | tf_op jit(solution)/shard_map/pallas_call | solution.py:259
  (2 shorter events, 0.0 us)
Async XLA Ops:
  0.0 15.4 %copy-start.3 = (bf16[1152,864]{0,1:T(8,128)(2,1)S(1)}, bf16[1152,864]{0,1:T(8,128)(2,1)}, u32[]{:S(2)}) copy-start(bf16[1152,864]{0,1:T(8,128)(2,1)} %param.8) | copy-start | bytes 5971972
  0.0 15.4 %copy-start.4 = (bf16[4,1152]{1,0:T(4,128)(2,1)S(1)}, bf16[4,1152]{1,0:T(4,128)(2,1)}, u32[]{:S(2)}) copy-start(bf16[4,1152]{1,0:T(4,128)(2,1)} %condition.1) | copy-start | bytes 27652
  0.0 8.7 %collective-permute-start.5 = (bf16[128,1152]{1,0:T(8,128)(2,1)}, bf16[128,1152]{1,0:T(8,128)(2,1)S(1)}, u32[]{:S(2)}, u32[]{:S(2)}) collective-permute-start(bf16[128,1152]{1,0:T(8,128)(2,1)} %bitcast.5), channel_id=1, source_target_pairs={{1,2},{3,4},{5,6},{2,1},{4,3},{6,5},{9,10},{11,12},{13,14},{10,9},... | collective-permute-start | bytes 884744 | tf_op jit(solution)/shard_map/ppermute | solution.py:291
  3.9 30.2 %collective-permute-start.4 = (bf16[128,1152]{1,0:T(8,128)(2,1)}, bf16[128,1152]{1,0:T(8,128)(2,1)S(1)}, u32[]{:S(2)}, u32[]{:S(2)}) collective-permute-start(bf16[128,1152]{1,0:T(8,128)(2,1)} %bitcast.6), channel_id=1, source_target_pairs={{0,1},{1,0},{2,3},{3,2},{4,5},{5,4},{6,7},{7,6},{8,9},{9,8},{10,11... | collective-permute-start | bytes 884744 | tf_op jit(solution)/shard_map/ppermute | solution.py:292
  4.0 9.1 %collective-permute-start = (bf16[128,1152]{1,0:T(8,128)(2,1)}, bf16[128,1152]{1,0:T(8,128)(2,1)S(1)}, u32[]{:S(2)}, u32[]{:S(2)}) collective-permute-start(bf16[128,1152]{1,0:T(8,128)(2,1)} %bitcast.7), channel_id=1, source_target_pairs={{0,2},{2,4},{4,6},{3,1},{5,3},{7,5},{8,10},{10,12},{12,14},{11,9},... | collective-permute-start | bytes 884744 | tf_op jit(solution)/shard_map/ppermute | solution.py:291
  8.7 6.1 %collective-permute-start.10 = (bf16[128,1152]{1,0:T(8,128)(2,1)S(1)}, bf16[128,1152]{1,0:T(8,128)(2,1)S(1)}, u32[]{:S(2)}, u32[]{:S(2)}) collective-permute-start(bf16[128,1152]{1,0:T(8,128)(2,1)S(1)} %collective-permute-done.5.mine.refs_0_), channel_id=1, source_target_pairs={{2,4},{4,6},{3,1},{5,3},{10,12},{12,14},{11,9},{13,11},{18,20},{20... | collective-permute-start | bytes 884744 | tf_op jit(solution)/shard_map/ppermute | solution.py:301
  10.7 23.9 %slice-start = ((s8[7962624]{0:T(1024)(128)(4,1)}), s8[4194304]{0:T(1024)(128)(4,1)S(1)}, s32[]{:S(2)}) async-start(s8[7962624]{0:T(1024)(128)(4,1)} %bitcast.3), calls=%async_computation | async-start | bytes 8388608
  10.8 23.3 %collective-permute-start.6 = (bf16[128,1152]{1,0:T(8,128)(2,1)S(1)}, bf16[128,1152]{1,0:T(8,128)(2,1)S(1)}, u32[]{:S(2)}, u32[]{:S(2)}) collective-permute-start(bf16[128,1152]{1,0:T(8,128)(2,1)S(1)} %collective-permute-done.5.mine.refs_0_), channel_id=1, source_target_pairs={{0,1},{1,0},{2,3},{3,2},{4,5},{5,4},{6,7},{7,6},{8,9},{9,8},{10,11... | collective-permute-start | bytes 884744 | tf_op jit(solution)/shard_map/ppermute | solution.py:302
  13.1 10.7 %collective-permute-start.1 = (bf16[128,1152]{1,0:T(8,128)(2,1)S(1)}, bf16[128,1152]{1,0:T(8,128)(2,1)S(1)}, u32[]{:S(2)}, u32[]{:S(2)}) collective-permute-start(bf16[128,1152]{1,0:T(8,128)(2,1)S(1)} %collective-permute-done.refs_1_), channel_id=1, source_target_pairs={{2,4},{4,6},{3,1},{5,3},{10,12},{12,14},{11,9},{13,11},{18,20},{20... | collective-permute-start | bytes 884744 | tf_op jit(solution)/shard_map/ppermute | solution.py:301
  14.7 22.6 %collective-permute-start.11 = (bf16[128,1152]{1,0:T(8,128)(2,1)S(1)}, bf16[128,1152]{1,0:T(8,128)(2,1)S(1)}, u32[]{:S(2)}, u32[]{:S(2)}) collective-permute-start(bf16[128,1152]{1,0:T(8,128)(2,1)S(1)} %collective-permute-done.10.refs_0_), channel_id=1, source_target_pairs={{4,6},{3,1},{12,14},{11,9},{20,22},{19,17},{28,30},{27,25}} | collective-permute-start | bytes 884744 | tf_op jit(solution)/shard_map/ppermute | solution.py:301
  15.4 19.2 %slice-start.1 = ((s8[7962624]{0:T(1024)(128)(4,1)}), s8[3768320]{0:T(1024)(128)(4,1)S(1)}, s32[]{:S(2)}) async-start(s8[7962624]{0:T(1024)(128)(4,1)} %bitcast.3), calls=%async_computation.1 | async-start | bytes 7536640
  15.5 19.2 %copy-start = (bf16[1,128,1152]{2,1,0:T(8,128)(2,1)S(1)}, bf16[1,128,1152]{2,1,0:T(8,128)(2,1)}, u32[]{:S(2)}) copy-start(bf16[1,128,1152]{2,1,0:T(8,128)(2,1)} %param.6) | copy-start | bytes 884740
  16.1 3.4 %collective-permute-start.7 = (f32[1,864]{1,0:T(1,128)S(1)}, f32[1,864]{1,0:T(1,128)S(1)}, u32[]{:S(2)}, u32[]{:S(2)}) collective-permute-start(f32[1,864]{1,0:T(1,128)S(1)} %get-tuple-element.15), channel_id=1, source_target_pairs={{0,8},{8,16},{16,24},{24,0},{1,9},{9,17},{17,25},{25,1},{2,10},{10... | collective-permute-start | bytes 10376 | tf_op jit(solution)/shard_map/ppermute | solution.py:254
  19.5 2.5 %collective-permute-start.8 = (f32[1,864]{1,0:T(1,128)S(1)}, f32[1,864]{1,0:T(1,128)S(1)}, u32[]{:S(2)}, u32[]{:S(2)}) collective-permute-start(f32[1,864]{1,0:T(1,128)S(1)} %get-tuple-element.16), channel_id=1, source_target_pairs={{0,16},{8,24},{16,0},{24,8},{1,17},{9,25},{17,1},{25,9},{2,18},{10... | collective-permute-start | bytes 10376 | tf_op jit(solution)/shard_map/ppermute | solution.py:254
  22.0 2.6 %collective-permute-start.9 = (f32[1,864]{1,0:T(1,128)S(1)}, f32[1,864]{1,0:T(1,128)S(1)}, u32[]{:S(2)}, u32[]{:S(2)}) collective-permute-start(f32[1,864]{1,0:T(1,128)S(1)} %get-tuple-element.17), channel_id=1, source_target_pairs={{0,24},{8,0},{16,8},{24,16},{1,25},{9,1},{17,9},{25,17},{2,26},{10... | collective-permute-start | bytes 10376 | tf_op jit(solution)/shard_map/ppermute | solution.py:254
  23.8 15.0 %collective-permute-start.2 = (bf16[128,1152]{1,0:T(8,128)(2,1)S(1)}, bf16[128,1152]{1,0:T(8,128)(2,1)S(1)}, u32[]{:S(2)}, u32[]{:S(2)}) collective-permute-start(bf16[128,1152]{1,0:T(8,128)(2,1)S(1)} %collective-permute-done.1.refs_0_), channel_id=1, source_target_pairs={{4,6},{3,1},{12,14},{11,9},{20,22},{19,17},{28,30},{27,25}} | collective-permute-start | bytes 884744 | tf_op jit(solution)/shard_map/ppermute | solution.py:301
  24.6 14.8 %collective-permute-start.15 = (bf16[128,1152]{1,0:T(8,128)(2,1)S(1)}, bf16[128,1152]{1,0:T(8,128)(2,1)S(1)}, u32[]{:S(2)}, u32[]{:S(2)}) collective-permute-start(bf16[128,1152]{1,0:T(8,128)(2,1)S(1)} %collective-permute-done.refs_1_), channel_id=1, source_target_pairs={{0,1},{1,0},{2,3},{3,2},{4,5},{5,4},{6,7},{7,6},{8,9},{9,8},{10,11... | collective-permute-start | bytes 884744 | tf_op jit(solution)/shard_map/ppermute | solution.py:302
  34.1 8.4 %collective-permute-start.14 = (bf16[128,1152]{1,0:T(8,128)(2,1)S(1)}, bf16[128,1152]{1,0:T(8,128)(2,1)S(1)}, u32[]{:S(2)}, u32[]{:S(2)}) collective-permute-start(bf16[128,1152]{1,0:T(8,128)(2,1)S(1)} %collective-permute-done.10.refs_0_), channel_id=1, source_target_pairs={{0,1},{1,0},{2,3},{3,2},{4,5},{5,4},{6,7},{7,6},{8,9},{9,8},{10,11... | collective-permute-start | bytes 884744 | tf_op jit(solution)/shard_map/ppermute | solution.py:302
  34.1 9.6 %collective-permute-start.13 = (bf16[128,1152]{1,0:T(8,128)(2,1)S(1)}, bf16[128,1152]{1,0:T(8,128)(2,1)S(1)}, u32[]{:S(2)}, u32[]{:S(2)}) collective-permute-start(bf16[128,1152]{1,0:T(8,128)(2,1)S(1)} %collective-permute-done.1.refs_0_), channel_id=1, source_target_pairs={{0,1},{1,0},{2,3},{3,2},{4,5},{5,4},{6,7},{7,6},{8,9},{9,8},{10,11... | collective-permute-start | bytes 884744 | tf_op jit(solution)/shard_map/ppermute | solution.py:302
  37.3 2.0 %copy-start.1 = (s32[1,8]{1,0:T(1,128)S(1)}, s32[1,8]{1,0:T(1,128)}, u32[]{:S(2)}) copy-start(s32[1,8]{1,0:T(1,128)} %marks.1) | copy-start | bytes 100
  37.4 7.4 %collective-permute-start.12 = (bf16[128,1152]{1,0:T(8,128)(2,1)S(1)}, bf16[128,1152]{1,0:T(8,128)(2,1)S(1)}, u32[]{:S(2)}, u32[]{:S(2)}) collective-permute-start(bf16[128,1152]{1,0:T(8,128)(2,1)S(1)} %collective-permute-done.11.refs_0_), channel_id=1, source_target_pairs={{0,1},{1,0},{2,3},{3,2},{4,5},{5,4},{6,7},{7,6},{8,9},{9,8},{10,11... | collective-permute-start | bytes 884744 | tf_op jit(solution)/shard_map/ppermute | solution.py:302
  38.8 6.4 %collective-permute-start.3 = (bf16[128,1152]{1,0:T(8,128)(2,1)S(1)}, bf16[128,1152]{1,0:T(8,128)(2,1)S(1)}, u32[]{:S(2)}, u32[]{:S(2)}) collective-permute-start(bf16[128,1152]{1,0:T(8,128)(2,1)S(1)} %collective-permute-done.2.ours), channel_id=1, source_target_pairs={{0,1},{1,0},{2,3},{3,2},{4,5},{5,4},{6,7},{7,6},{8,9},{9,8},{10,11... | collective-permute-start | bytes 884744 | tf_op jit(solution)/shard_map/ppermute | solution.py:302
  45.2 6.6 %copy-start.2 = (bf16[1152,1152]{1,0:T(8,128)(2,1)S(1)}, bf16[1152,1152]{1,0:T(8,128)(2,1)}, u32[]{:S(2)}) copy-start(bf16[1152,1152]{1,0:T(8,128)(2,1)} %wo.1) | copy-start | bytes 7962628
  50.4 1.5 %collective-permute-start.16 = (bf16[128,640]{1,0:T(8,128)(2,1)S(1)}, bf16[128,640]{1,0:T(8,128)(2,1)S(1)}, u32[]{:S(2)}, u32[]{:S(2)}) collective-permute-start(bf16[128,640]{1,0:T(8,128)(2,1)S(1)} %get-tuple-element.22), channel_id=1, source_target_pairs={{0,1},{1,0},{2,3},{3,2},{4,5},{5,4},{6,7},{7,6},{8,9},{9,8},{10,11... | collective-permute-start | bytes 491528 | tf_op jit(solution)/shard_map/ppermute | solution.py:345

commit v4 on v3

--- a/solution.py
+++ b/solution.py
@@ -23,8 +23,8 @@
 def assemble_modulation(pieces, row, blocks):
     here = lax.axis_index("grp")
     count = len(pieces)
-    for back, piece in enumerate(pieces):
-        blocks[lax.rem(here - back + count, count)] = piece[...]
+    for bits, piece in enumerate(pieces):
+        blocks[lax.bitwise_xor(here, bits)] = piece[...]
     wide = pieces[0].shape[1]
     for block in range(count):
         row[:, block * wide : (block + 1) * wide] = blocks[block]
@@ -91,15 +91,14 @@
         condition[...], w[...], (((1,), (1,)), ((), ())), preferred_element_type=F32
     )
     here = lax.axis_index("grp")
-    count = len(outs)
     which = lax.broadcasted_iota(jnp.int32, (columns.shape[0], 1), 0)
-    for ahead, out in enumerate(outs):
+    for bits, out in enumerate(outs):
         out[...] = jnp.sum(
-            jnp.where(which == lax.rem(here + ahead, count), columns, 0.0), axis=0, keepdims=True
+            jnp.where(which == lax.bitwise_xor(here, bits), columns, 0.0), axis=0, keepdims=True
         )
 
 
-def project_kernel(own, partner, mine, theirs, *rest, parts):
+def project_kernel(own, partner, *rest, parts):
     pieces = rest[:parts]
     w, query, kv, row, blocks, normed = rest[parts:]
     count, width = own.shape
@@ -108,30 +107,38 @@
     assemble_modulation(pieces, row, blocks)
     shift = row[:, :width]
     scale = 1.0 + row[:, width : 2 * width]
+    normalize_rows(own, 0, normed, pl.multiple_of(count * core, count), count, shift, scale)
+    normalize_rows(partner, 0, normed, pl.multiple_of(count * (1 - core), count), count, shift, scale)
+    for section, (target, to) in enumerate(((query, 0), (kv, 0), (kv, wide))):
+        at = pl.multiple_of(section * width + first * core, LANES)
+        target[:, to : to + wide] = jnp.dot(
+            normed[...], w[:, pl.ds(at, wide)], preferred_element_type=F32
+        ).astype(BF16)
+
+
+def attend_kernel(mine, theirs, row, query, pairs, w, near, normed, kv, scores, probs):
     edge = ROW_TOKENS
+    count, width = mine.shape
+    first, wide = half_columns(width)
+    core, chip, chips = place_of_chip()
+    other = 1 - core
+    inner = count - edge
     end = edge + 2 * count
-    other = 1 - core
-    normalize_rows(own, 0, normed, pl.multiple_of(edge + count * core, edge), count, shift, scale)
-    normalize_rows(partner, 0, normed, pl.multiple_of(edge + count * other, edge), count, shift, scale)
-    inner = count - edge
+    shift = row[:, :width]
+    scale = 1.0 + row[:, width : 2 * width]
     normalize_rows(
-        mine, pl.multiple_of(inner * other, edge), normed, pl.multiple_of(end * core, edge), edge, shift, scale
+        mine, pl.multiple_of(inner * other, edge), normed, pl.multiple_of(edge * core, edge), edge, shift, scale
     )
     normalize_rows(
-        theirs, pl.multiple_of(inner * core, edge), normed, pl.multiple_of(end * other, edge), edge, shift, scale
-    )
-    at = [pl.multiple_of(section * width + first * core, LANES) for section in range(3)]
-    query[...] = jnp.dot(normed[edge:end], w[:, pl.ds(at[0], wide)], preferred_element_type=F32).astype(BF16)
-    for section in (1, 2):
-        part = slice((section - 1) * wide, section * wide)
-        kv[:, part] = jnp.dot(normed[...], w[:, pl.ds(at[section], wide)], preferred_element_type=F32).astype(BF16)
-
-
-def attend_kernel(query, kv, near, scores, probs, *, size):
-    edge = ROW_TOKENS
-    count = query.shape[0] // 2
-    wide = query.shape[1]
-    core, chip, chips = place_of_chip()
+        theirs, pl.multiple_of(inner * core, edge), normed, pl.multiple_of(edge * other, edge), edge, shift, scale
+    )
+    kv[edge:end] = pairs[...]
+    for section in range(2):
+        at = pl.multiple_of((section + 1) * width + first * core, LANES)
+        margins = jnp.dot(normed[...], w[:, pl.ds(at, wide)], preferred_element_type=F32).astype(BF16)
+        part = slice(section * wide, (section + 1) * wide)
+        kv[:edge, part] = margins[:edge]
+        kv[end:, part] = margins[edge:]
     column = lax.broadcasted_iota(jnp.int32, (1, count + 2 * edge), 1)
     near[...] = jnp.zeros_like(near)
     for strip in range(2):
@@ -143,7 +150,7 @@
             hidden = (chip == chips - 1) & (column >= count + edge)
         bias = jnp.where(hidden, -1e30, 0.0)
         attend_heads(
-            range(HEADS // 2), size, size * HEADS, core, query.at[rows],
+            range(HEADS // 2), width // HEADS, width, core, query.at[rows],
             [kv.at[keys, :wide]], [kv.at[keys, wide:]], bias, scores.at[strip], probs.at[strip], near.at[rows],
         )
 
@@ -159,22 +166,20 @@
     return [jnp.max(jnp.where(column == 2 * chip + core, values, 0)) > 0 for core in range(2)]
 
 
-def strip_kernel(*refs, strips, distance, offset):
-    ours, theirs = refs[:strips], refs[strips : 2 * strips]
-    row, marks, before, w, kv, normed = refs[2 * strips :]
+def strip_kernel(ours, theirs, row, marks, before, w, kv, normed, *, distance, offset):
     _, chip, _ = place_of_chip()
     marked = chip_marks(marks, chip)
-    count = ours[0].shape[0]
+    count = ours.shape[0]
 
     @pl.when(marked[0] | marked[1])
     def _():
-        if distance == 1:
-            kv[: 2 * count] = before[ROW_TOKENS : ROW_TOKENS + 2 * count]
-        add_pairs(ours, theirs, row, w, kv, normed, distance, offset * count)
-
-
-def add_pairs(ours, theirs, row, w, kv, normed, distance, offset):
-    count, width = ours[0].shape
+        if distance == 1 and offset == 0:
+            kv[: 2 * count] = before[...]
+        add_strips(ours, theirs, row, w, kv, normed, distance, offset * count)
+
+
+def add_strips(ours, theirs, row, w, kv, normed, distance, offset):
+    count, width = ours.shape
     core, chip, chips = place_of_chip()
     first, wide = half_columns(width)
     shift = row[:, :width]
@@ -182,21 +187,19 @@
     lefts = chip
     rights = chips - 1 - chip
     nearer = jnp.minimum(lefts, distance - 1) + jnp.minimum(rights, distance - 1)
-    for mine, pair in ((True, ours), (False, theirs)):
+    for mine, strip in ((True, ours), (False, theirs)):
         is_left = (core == 0) if mine else (core == 1)
         have = jnp.where(is_left, lefts, rights) >= distance
         slot = nearer + jnp.where(is_left | (lefts < distance), 0, 1)
 
         @pl.when(have)
-        def _(pair=pair, slot=slot):
+        def _(strip=strip, slot=slot):
             at = pl.multiple_of(2 * count * (slot + 1) + offset, count)
-            rows = len(pair) * count
-            for k, strip in enumerate(pair):
-                normalize_rows(strip, 0, normed, k * count, count, shift, scale)
+            normalize_rows(strip, 0, normed, 0, count, shift, scale)
             for section in range(2):
                 columns = pl.ds(pl.multiple_of((section + 1) * width + first * core, LANES), wide)
-                kv[pl.ds(at, rows), section * wide : (section + 1) * wide] = jnp.dot(
-                    normed[:rows], w[:, columns], preferred_element_type=F32
+                kv[pl.ds(at, count), section * wide : (section + 1) * wide] = jnp.dot(
+                    normed[...], w[:, columns], preferred_element_type=F32
                 ).astype(BF16)
 
 
@@ -212,7 +215,7 @@
 
     @pl.when(marked[0] | marked[1])
     def _():
-        add_pairs((ours,), (theirs,), row, w, kv, normed, distance, count)
+        add_strips(ours, theirs, row, w, kv, normed, distance, count)
 
     for strip in range(2):
 
@@ -249,9 +252,9 @@
 def exchange_modulation(rows):
     count = len(rows)
     pieces = [rows[0]]
-    for ahead in range(1, count):
-        pairs = [(i, (i + ahead) % count) for i in range(count)]
-        pieces.append(lax.ppermute(rows[ahead], "grp", pairs))
+    for bits in range(1, count):
+        pairs = [(i, i ^ bits) for i in range(count)]
+        pieces.append(lax.ppermute(rows[bits], "grp", pairs))
     return pieces
 
 
@@ -300,34 +303,31 @@
     for step in range(2, 2 * depth):
         mine.append(lax.ppermute(mine[step - 2], "tile", along(step // 2 + 1)))
     theirs = [lax.ppermute(strip, "tile", swap) for strip in mine]
-    query, around, row = call(
+    query, kv, row = call(
         functools.partial(project_kernel, parts=parts),
-        [((2 * count, wide), BF16), ((rows, 2 * wide), BF16), ((1, 3 * width), F32)],
-        [pltpu.VMEM((parts, 1, part_width), F32), pltpu.VMEM((rows, width), BF16)],
-        [vmem] * (5 + parts), 2 * 10**9,
-        (own, partner, mine[0], theirs[0], *pieces, w_project), 16,
+        [((2 * count, wide), BF16), ((2 * count, 2 * wide), BF16), ((1, 3 * width), F32)],
+        [pltpu.VMEM((parts, 1, part_width), F32), pltpu.VMEM((2 * count, width), BF16)],
+        [vmem] * (3 + parts), 2 * 10**9, (own, partner, *pieces, w_project), 16,
     )
     (near,) = call(
-        functools.partial(attend_kernel, size=width // HEADS),
+        attend_kernel,
         [((2 * count, wide), F32)],
         [
+            pltpu.VMEM((2 * ROW_TOKENS, width), BF16),
+            pltpu.VMEM((rows, 2 * wide), BF16),
             pltpu.VMEM((2, HEADS // 2, count, count + 2 * ROW_TOKENS), F32),
             pltpu.VMEM((2, HEADS // 2, count, count + 2 * ROW_TOKENS), BF16),
         ],
-        [vmem] * 2, 10**9, (query, around), 16,
-    )
-    kv = around
+        [vmem] * 6, 10**9, (mine[0], theirs[0], row, query, kv, w_project), 16,
+    )
     kv_out = ((tokens, 2 * wide), BF16)
-    pair_scratch = [pltpu.VMEM((2 * count, width), BF16)]
-
-    groups = [(0, 2)] + [(at, 1) for at in range(2, len(mine) - 1)]
-    for at, strips in groups:
-        some = slice(at, at + strips)
+    pair_scratch = [pltpu.VMEM((count, width), BF16)]
+
+    for at in range(len(mine) - 1):
         (kv,) = call(
-            functools.partial(strip_kernel, strips=strips, distance=at // 2 + 1, offset=at % 2),
-            [kv_out], pair_scratch, [vmem] * (2 * strips + 4), 10**9,
-            (*mine[some], *theirs[some], row, detail, kv, w_project), 12,
-            {} if at == 0 else {2 * strips + 2: 0},
+            functools.partial(strip_kernel, distance=at // 2 + 1, offset=at % 2),
+            [kv_out], pair_scratch, [vmem] * 6, 10**9,
+            (mine[at], theirs[at], row, detail, kv, w_project), 12, {} if at == 0 else {4: 0},
         )
     group = max(1, min(HEADS // 2, 2**20 // (count * tokens)))
     _, keep, send = call(

time: 53.4 us -> 55.5 us (1.039)
  waiting for transfers between devices: 7.31 us -> 8.15 us
  Pallas kernels: 17 us -> 17.6 us
  starting transfers between devices: 28.6 us -> 29.2 us
    ppermute x3, waiting for transfers between devices: 3.42 us -> 4.23 us  [exchange_modulation(): pieces.append(lax.ppermute(rows[bits], 'grp', pairs))]
    pallas_call x10 -> x11, Pallas kernels: 17 us -> 17.6 us  [call(): pl.pallas_call(kernel, out_shape=[jax.ShapeDtypeStruct(shape, dtype) for...]
  transfers between devices with their start and end apart: 17 -> 17, of which waited for: 5 -> 5; matrix products, arithmetic and copies ran while one was open for 0% -> 0% of each run, Pallas kernels for 20% -> 21%
where the time goes in v4:
time: 55.5 us; the launch traced here: 55.3 us
  starting transfers between devices  29.2 us (53%)
  Pallas kernels  17.6 us (32%)
  waiting for transfers between devices  8.15 us (15%)
    pallas_call x11, Pallas kernels, call(): pl.pallas_call(kernel, out_shape=[jax.ShapeDtypeStruct(shape, dtype) for...  17.6 us
    ppermute x6, starting transfers between devices, on_device(): theirs = [lax.ppermute(strip, 'tile', swap) for strip in mine]  13.3 us
    ppermute x4, starting transfers between devices, on_device(): mine.append(lax.ppermute(mine[step - 2], 'tile', along(step // 2 + 1)))  5.05 us
    ppermute x3, starting transfers between devices, exchange_modulation(): pieces.append(lax.ppermute(rows[bits], 'grp', pairs))  4.67 us
    ppermute x3, waiting for transfers between devices, exchange_modulation(): pieces.append(lax.ppermute(rows[bits], 'grp', pairs))  4.23 us
    ppermute x1, starting transfers between devices, on_device(): lax.ppermute(own, 'tile', cross)  3.89 us
    ppermute x1, waiting for transfers between devices, on_device(): lax.ppermute(own, 'tile', cross)  2.59 us
    ppermute x1, starting transfers between devices, on_device(): lax.ppermute(own, 'tile', along(1))  2.08 us
  transfers between devices with their start and end apart: 17, of which 5 were waited for; matrix products, arithmetic and copies ran while one was open for 0% of the time, Pallas kernels for 21%

profile of v4, /device:TPU:17, one launch (start us, length us, event | category | flops | bytes accessed | tf_op | source)
XLA Modules:
  0.0 55.3 jit_solution(7142152944262557132)
XLA Ops:
  0.0 0.0 copy-start.3
  0.0 0.0 copy-start.4
  0.0 3.9 %collective-permute-start.8 = (bf16[128,1152]{1,0:T(8,128)(2,1)}, bf16[128,1152]{1,0:T(8,128)(2,1)S(1)}, u32[]{:S(2)}, u32[]{:S(2)}) collective-permute-start(bf16[128,1152]{1,0:T(8,128)(2,1)} %bitcast.5), channel_id=1, source_target_pairs={{1,2},{3,4},{5,6},{2,1},{4,3},{6,5},{9,10},{11,12},{13,14},{10,9},... | collective-permute-start | bytes 884744 | tf_op jit(solution)/shard_map/ppermute | solution.py:294
  3.9 0.1 collective-permute-start.4
  4.0 2.1 %collective-permute-start = (bf16[128,1152]{1,0:T(8,128)(2,1)}, bf16[128,1152]{1,0:T(8,128)(2,1)S(1)}, u32[]{:S(2)}, u32[]{:S(2)}) collective-permute-start(bf16[128,1152]{1,0:T(8,128)(2,1)} %bitcast.7), channel_id=1, source_target_pairs={{0,2},{2,4},{4,6},{3,1},{5,3},{7,5},{8,10},{10,12},{12,14},{11,9},... | collective-permute-start | bytes 884744 | tf_op jit(solution)/shard_map/ppermute | solution.py:294
  6.1 2.6 %collective-permute-done.8.ours.mine = bf16[128,1152]{1,0:T(8,128)(2,1)S(1)} collective-permute-done((bf16[128,1152]{1,0:T(8,128)(2,1)}, bf16[128,1152]{1,0:T(8,128)(2,1)S(1)}, u32[]{:S(2)}, u32[]{:S(2)}) %collective-permute-start.8) | collective-permute-done | bytes 294944 | tf_op jit(solution)/shard_map/ppermute | solution.py:294
  8.7 2.1 %collective-permute-start.9 = (bf16[128,1152]{1,0:T(8,128)(2,1)S(1)}, bf16[128,1152]{1,0:T(8,128)(2,1)S(1)}, u32[]{:S(2)}, u32[]{:S(2)}) collective-permute-start(bf16[128,1152]{1,0:T(8,128)(2,1)S(1)} %collective-permute-done.8.ours.mine), channel_id=1, source_target_pairs={{2,4},{4,6},{3,1},{5,3},{10,12},{12,14},{11,9},{13,11},{18,20},{20... | collective-permute-start | bytes 884744 | tf_op jit(solution)/shard_map/ppermute | solution.py:304
  10.7 0.0 slice-start
  10.8 2.3 %collective-permute-start.15 = (bf16[128,1152]{1,0:T(8,128)(2,1)S(1)}, bf16[128,1152]{1,0:T(8,128)(2,1)S(1)}, u32[]{:S(2)}, u32[]{:S(2)}) collective-permute-start(bf16[128,1152]{1,0:T(8,128)(2,1)S(1)} %collective-permute-done.8.ours.mine), channel_id=1, source_target_pairs={{0,1},{1,0},{2,3},{3,2},{4,5},{5,4},{6,7},{7,6},{8,9},{9,8},{10,11... | collective-permute-start | bytes 884744 | tf_op jit(solution)/shard_map/ppermute | solution.py:305
  13.1 0.0 collective-permute-done.ours
  13.1 1.6 %collective-permute-start.1 = (bf16[128,1152]{1,0:T(8,128)(2,1)S(1)}, bf16[128,1152]{1,0:T(8,128)(2,1)S(1)}, u32[]{:S(2)}, u32[]{:S(2)}) collective-permute-start(bf16[128,1152]{1,0:T(8,128)(2,1)S(1)} %collective-permute-done.ours), channel_id=1, source_target_pairs={{2,4},{4,6},{3,1},{5,3},{10,12},{12,14},{11,9},{13,11},{18,20},{20... | collective-permute-start | bytes 884744 | tf_op jit(solution)/shard_map/ppermute | solution.py:304
  14.7 0.0 collective-permute-done.9.ours
  14.7 0.7 %collective-permute-start.10 = (bf16[128,1152]{1,0:T(8,128)(2,1)S(1)}, bf16[128,1152]{1,0:T(8,128)(2,1)S(1)}, u32[]{:S(2)}, u32[]{:S(2)}) collective-permute-start(bf16[128,1152]{1,0:T(8,128)(2,1)S(1)} %collective-permute-done.9.ours), channel_id=1, source_target_pairs={{4,6},{3,1},{12,14},{11,9},{20,22},{19,17},{28,30},{27,25}} | collective-permute-start | bytes 884744 | tf_op jit(solution)/shard_map/ppermute | solution.py:304
  15.4 0.0 copy-done.3
  15.4 0.0 copy-done.4
  15.4 0.0 slice-start.1
  15.5 0.0 copy-start
  15.5 0.7 %shard_map.65 = (f32[1,864]{1,0:T(1,128)S(1)}, f32[1,864]{1,0:T(1,128)S(1)}, f32[1,864]{1,0:T(1,128)S(1)}, f32[1,864]{1,0:T(1,128)S(1)}) custom-call(bf16[4,1152]{1,0:T(4,128)(2,1)S(1)} %copy-done.4, bf16[864,1152]{1,0:T(8,128)(2,1)S(1)} %bitcast.10, f32[8,128]{1,0:T(8,128)S(1)} %shard_map.64._), custom_call_target="tpu_custom_call" | custom-call | flops 10000000000 | bytes 50000000 | tf_op jit(solution)/shard_map/pallas_call | solution.py:262
  16.1 1.3 %collective-permute-start.5 = (f32[1,864]{1,0:T(1,128)S(1)}, f32[1,864]{1,0:T(1,128)S(1)}, u32[]{:S(2)}, u32[]{:S(2)}) collective-permute-start(f32[1,864]{1,0:T(1,128)S(1)} %get-tuple-element.15), channel_id=1, source_target_pairs={{0,8},{8,0},{16,24},{24,16},{1,9},{9,1},{17,25},{25,17},{2,10},{10... | collective-permute-start | bytes 10376 | tf_op jit(solution)/shard_map/ppermute | solution.py:257
  17.4 1.5 %collective-permute-done.5.rest_1_ = f32[1,864]{1,0:T(1,128)S(1)} collective-permute-done((f32[1,864]{1,0:T(1,128)S(1)}, f32[1,864]{1,0:T(1,128)S(1)}, u32[]{:S(2)}, u32[]{:S(2)}) %collective-permute-start.5) | collective-permute-done | bytes 3488 | tf_op jit(solution)/shard_map/ppermute | solution.py:257
  18.9 1.2 %collective-permute-start.6 = (f32[1,864]{1,0:T(1,128)S(1)}, f32[1,864]{1,0:T(1,128)S(1)}, u32[]{:S(2)}, u32[]{:S(2)}) collective-permute-start(f32[1,864]{1,0:T(1,128)S(1)} %get-tuple-element.16), channel_id=1, source_target_pairs={{0,16},{8,24},{16,0},{24,8},{1,17},{9,25},{17,1},{25,9},{2,18},{10... | collective-permute-start | bytes 10376 | tf_op jit(solution)/shard_map/ppermute | solution.py:257
  20.2 1.5 %collective-permute-done.6.rest_2_ = f32[1,864]{1,0:T(1,128)S(1)} collective-permute-done((f32[1,864]{1,0:T(1,128)S(1)}, f32[1,864]{1,0:T(1,128)S(1)}, u32[]{:S(2)}, u32[]{:S(2)}) %collective-permute-start.6) | collective-permute-done | bytes 3488 | tf_op jit(solution)/shard_map/ppermute | solution.py:257
  21.7 2.2 %collective-permute-start.7 = (f32[1,864]{1,0:T(1,128)S(1)}, f32[1,864]{1,0:T(1,128)S(1)}, u32[]{:S(2)}, u32[]{:S(2)}) collective-permute-start(f32[1,864]{1,0:T(1,128)S(1)} %get-tuple-element.17), channel_id=1, source_target_pairs={{0,24},{8,16},{16,8},{24,0},{1,25},{9,17},{17,9},{25,1},{2,26},{10... | collective-permute-start | bytes 10376 | tf_op jit(solution)/shard_map/ppermute | solution.py:257
  23.9 1.2 %collective-permute-done.7.rest_3_ = f32[1,864]{1,0:T(1,128)S(1)} collective-permute-done((f32[1,864]{1,0:T(1,128)S(1)}, f32[1,864]{1,0:T(1,128)S(1)}, u32[]{:S(2)}, u32[]{:S(2)}) %collective-permute-start.7) | collective-permute-done | bytes 3488 | tf_op jit(solution)/shard_map/ppermute | solution.py:257
  25.0 9.1 %collective-permute-start.14 = (bf16[128,1152]{1,0:T(8,128)(2,1)S(1)}, bf16[128,1152]{1,0:T(8,128)(2,1)S(1)}, u32[]{:S(2)}, u32[]{:S(2)}) collective-permute-start(bf16[128,1152]{1,0:T(8,128)(2,1)S(1)} %collective-permute-done.ours), channel_id=1, source_target_pairs={{0,1},{1,0},{2,3},{3,2},{4,5},{5,4},{6,7},{7,6},{8,9},{9,8},{10,11... | collective-permute-start | bytes 884744 | tf_op jit(solution)/shard_map/ppermute | solution.py:305
  34.1 0.0 collective-permute-done.4.partner
  34.1 0.0 collective-permute-start.13
  34.1 0.0 collective-permute-done.1.ours
  34.1 0.7 %collective-permute-start.2 = (bf16[128,1152]{1,0:T(8,128)(2,1)S(1)}, bf16[128,1152]{1,0:T(8,128)(2,1)S(1)}, u32[]{:S(2)}, u32[]{:S(2)}) collective-permute-start(bf16[128,1152]{1,0:T(8,128)(2,1)S(1)} %collective-permute-done.1.ours), channel_id=1, source_target_pairs={{4,6},{3,1},{12,14},{11,9},{20,22},{19,17},{28,30},{27,25}} | collective-permute-start | bytes 884744 | tf_op jit(solution)/shard_map/ppermute | solution.py:304
  34.8 0.0 slice-done
  34.8 0.0 slice-done.1
  34.8 0.0 copy-done
  34.8 0.0 copy-start.1
  34.9 2.0 %shard_map.66 = (bf16[256,640]{1,0:T(8,128)(2,1)S(1)}, bf16[256,1280]{1,0:T(8,128)(2,1)S(1)}, f32[1,3456]{1,0:T(1,128)S(1)}) custom-call(bf16[128,1152]{1,0:T(8,128)(2,1)S(1)} %bitcast.8, bf16[128,1152]{1,0:T(8,128)(2,1)S(1)} %collective-permute-done.4.partner, f32[1,864]{1,0:T(1,128)S(1)} %get-tuple-element.14.rest_0_, ...), custom_call_target="tpu_custom_call" | custom-call | flops 2000000000 | bytes 10000000 | tf_op jit(solution)/shard_map/pallas_call | solution.py:262
  36.9 0.0 collective-permute-done.15.theirs
  36.9 1.2 %collective-permute-start.12 = (bf16[128,1152]{1,0:T(8,128)(2,1)S(1)}, bf16[128,1152]{1,0:T(8,128)(2,1)S(1)}, u32[]{:S(2)}, u32[]{:S(2)}) collective-permute-start(bf16[128,1152]{1,0:T(8,128)(2,1)S(1)} %collective-permute-done.1.ours), channel_id=1, source_target_pairs={{0,1},{1,0},{2,3},{3,2},{4,5},{5,4},{6,7},{7,6},{8,9},{9,8},{10,11... | collective-permute-start | bytes 884744 | tf_op jit(solution)/shard_map/ppermute | solution.py:305
  38.1 0.0 copy-done.1
  38.1 2.0 %shard_map.67.before = bf16[1024,1280]{1,0:T(8,128)(2,1)S(1)} custom-call(bf16[128,1152]{1,0:T(8,128)(2,1)S(1)} %collective-permute-done.8.ours.mine, bf16[128,1152]{1,0:T(8,128)(2,1)S(1)} %collective-permute-done.15.theirs, f32[1,3456]{1,0:T(1,128)S(1)} %get-tuple-element.18.row, s32[1,8]{1,0:T(1,128)S(1)} %copy-done.1, ...), custom_call_target="tpu_custom_call" | custom-call | flops 1000000000 | bytes 5000000 | tf_op jit(solution)/shard_map/pallas_call | solution.py:262
  40.2 0.0 collective-permute-done.10.ours
  40.2 0.1 collective-permute-start.11
  40.3 2.2 %shard_map.72.near = f32[256,640]{1,0:T(8,128)S(1)} custom-call(bf16[128,1152]{1,0:T(8,128)(2,1)S(1)} %collective-permute-done.8.ours.mine, bf16[128,1152]{1,0:T(8,128)(2,1)S(1)} %collective-permute-done.15.theirs, f32[1,3456]{1,0:T(1,128)S(1)} %get-tuple-element.18.row, bf16[256,640]{1,0:T(8,128)(2,1)S(1)} %get-tuple-element.19.query, ...), custom_call_target="tpu_custom_call" | custom-call | flops 1000000000 | bytes 5000000 | tf_op jit(solution)/shard_map/pallas_call | solution.py:262
  42.5 0.0 collective-permute-done.2.ours
  42.5 0.5 collective-permute-start.3
  43.0 0.0 collective-permute-done.14.theirs
  43.0 2.0 %shard_map.68.before = bf16[1024,1280]{1,0:T(8,128)(2,1)S(1)} custom-call(bf16[128,1152]{1,0:T(8,128)(2,1)S(1)} %collective-permute-done.ours, bf16[128,1152]{1,0:T(8,128)(2,1)S(1)} %collective-permute-done.14.theirs, f32[1,3456]{1,0:T(1,128)S(1)} %get-tuple-element.18.row, s32[1,8]{1,0:T(1,128)S(1)} %copy-done.1, ...), custom_call_target="tpu_custom_call", output_to_operand_aliasing={{}: (4, {})} | custom-call | flops 1000000000 | bytes 5000000 | tf_op jit(solution)/shard_map/pallas_call | solution.py:262
  45.0 0.0 collective-permute-done.13.theirs
  45.0 1.1 %shard_map.69.before = bf16[1024,1280]{1,0:T(8,128)(2,1)S(1)} custom-call(bf16[128,1152]{1,0:T(8,128)(2,1)S(1)} %collective-permute-done.9.ours, bf16[128,1152]{1,0:T(8,128)(2,1)S(1)} %collective-permute-done.13.theirs, f32[1,3456]{1,0:T(1,128)S(1)} %get-tuple-element.18.row, s32[1,8]{1,0:T(1,128)S(1)} %copy-done.1, ...), custom_call_target="tpu_custom_call", output_to_operand_aliasing={{}: (4, {})} | custom-call | flops 1000000000 | bytes 5000000 | tf_op jit(solution)/shard_map/pallas_call | solution.py:262
  46.1 0.0 collective-permute-done.12.theirs
  46.1 1.1 %shard_map.70.before = bf16[1024,1280]{1,0:T(8,128)(2,1)S(1)} custom-call(bf16[128,1152]{1,0:T(8,128)(2,1)S(1)} %collective-permute-done.1.ours, bf16[128,1152]{1,0:T(8,128)(2,1)S(1)} %collective-permute-done.12.theirs, f32[1,3456]{1,0:T(1,128)S(1)} %get-tuple-element.18.row, s32[1,8]{1,0:T(1,128)S(1)} %copy-done.1, ...), custom_call_target="tpu_custom_call", output_to_operand_aliasing={{}: (4, {})} | custom-call | flops 1000000000 | bytes 5000000 | tf_op jit(solution)/shard_map/pallas_call | solution.py:262
  47.3 0.0 collective-permute-done.11.theirs
  47.3 0.4 shard_map.71.before
  47.7 0.0 copy-start.2
  47.7 0.0 collective-permute-done.3.theirs
  47.7 4.8 %shard_map.73 = (bf16[1024,1280]{1,0:T(8,128)(2,1)S(1)}, bf16[128,640]{1,0:T(8,128)(2,1)S(1)}, bf16[128,640]{1,0:T(8,128)(2,1)S(1)}) custom-call(bf16[128,1152]{1,0:T(8,128)(2,1)S(1)} %collective-permute-done.2.ours, bf16[128,1152]{1,0:T(8,128)(2,1)S(1)} %collective-permute-done.3.theirs, ...), custom_call_target="tpu_custom_call", output_to_operand_aliasing={{0}: (5, {})} | custom-call | flops 1000000000 | bytes 5000000 | tf_op jit(solution)/shard_map/pallas_call | solution.py:262
  52.5 0.2 collective-permute-start.16
  52.7 1.3 %collective-permute-done.16.got = bf16[128,640]{1,0:T(8,128)(2,1)S(1)} collective-permute-done((bf16[128,640]{1,0:T(8,128)(2,1)S(1)}, bf16[128,640]{1,0:T(8,128)(2,1)S(1)}, u32[]{:S(2)}, u32[]{:S(2)}) %collective-permute-start.16) | collective-permute-done | bytes 163872 | tf_op jit(solution)/shard_map/ppermute | solution.py:345
  54.0 0.0 copy-done.2
  54.0 1.3 %shard_map.74 = bf16[128,1152]{1,0:T(8,128)(2,1)} custom-call(bf16[128,1152]{1,0:T(8,128)(2,1)S(1)} %bitcast.9, bf16[128,640]{1,0:T(8,128)(2,1)S(1)} %get-tuple-element.21.keep, bf16[128,640]{1,0:T(8,128)(2,1)S(1)} %collective-permute-done.16.got, f32[1,3456]{1,0:T(1,128)S(1)} %get-tuple-element.18.row, bf16[1152,1152]{1,0:T(8,128)(2,1)S(1)} %copy-done.2), custom_call_target="tpu_custom_call" | custom-call | flops 1000000000 | bytes 5000000 | tf_op jit(solution)/shard_map/pallas_call | solution.py:262
  (2 shorter events, 0.0 us)
Async XLA Ops:
  0.0 15.4 %copy-start.3 = (bf16[1152,864]{0,1:T(8,128)(2,1)S(1)}, bf16[1152,864]{0,1:T(8,128)(2,1)}, u32[]{:S(2)}) copy-start(bf16[1152,864]{0,1:T(8,128)(2,1)} %param.8) | copy-start | bytes 5971972
  0.0 15.4 %copy-start.4 = (bf16[4,1152]{1,0:T(4,128)(2,1)S(1)}, bf16[4,1152]{1,0:T(4,128)(2,1)}, u32[]{:S(2)}) copy-start(bf16[4,1152]{1,0:T(4,128)(2,1)} %condition.1) | copy-start | bytes 27652
  0.0 8.7 %collective-permute-start.8 = (bf16[128,1152]{1,0:T(8,128)(2,1)}, bf16[128,1152]{1,0:T(8,128)(2,1)S(1)}, u32[]{:S(2)}, u32[]{:S(2)}) collective-permute-start(bf16[128,1152]{1,0:T(8,128)(2,1)} %bitcast.5), channel_id=1, source_target_pairs={{1,2},{3,4},{5,6},{2,1},{4,3},{6,5},{9,10},{11,12},{13,14},{10,9},... | collective-permute-start | bytes 884744 | tf_op jit(solution)/shard_map/ppermute | solution.py:294
  3.9 30.2 %collective-permute-start.4 = (bf16[128,1152]{1,0:T(8,128)(2,1)}, bf16[128,1152]{1,0:T(8,128)(2,1)S(1)}, u32[]{:S(2)}, u32[]{:S(2)}) collective-permute-start(bf16[128,1152]{1,0:T(8,128)(2,1)} %bitcast.6), channel_id=1, source_target_pairs={{0,1},{1,0},{2,3},{3,2},{4,5},{5,4},{6,7},{7,6},{8,9},{9,8},{10,11... | collective-permute-start | bytes 884744 | tf_op jit(solution)/shard_map/ppermute | solution.py:295
  4.0 9.1 %collective-permute-start = (bf16[128,1152]{1,0:T(8,128)(2,1)}, bf16[128,1152]{1,0:T(8,128)(2,1)S(1)}, u32[]{:S(2)}, u32[]{:S(2)}) collective-permute-start(bf16[128,1152]{1,0:T(8,128)(2,1)} %bitcast.7), channel_id=1, source_target_pairs={{0,2},{2,4},{4,6},{3,1},{5,3},{7,5},{8,10},{10,12},{12,14},{11,9},... | collective-permute-start | bytes 884744 | tf_op jit(solution)/shard_map/ppermute | solution.py:294
  8.7 6.1 %collective-permute-start.9 = (bf16[128,1152]{1,0:T(8,128)(2,1)S(1)}, bf16[128,1152]{1,0:T(8,128)(2,1)S(1)}, u32[]{:S(2)}, u32[]{:S(2)}) collective-permute-start(bf16[128,1152]{1,0:T(8,128)(2,1)S(1)} %collective-permute-done.8.ours.mine), channel_id=1, source_target_pairs={{2,4},{4,6},{3,1},{5,3},{10,12},{12,14},{11,9},{13,11},{18,20},{20... | collective-permute-start | bytes 884744 | tf_op jit(solution)/shard_map/ppermute | solution.py:304
  10.7 24.1 %slice-start = ((s8[7962624]{0:T(1024)(128)(4,1)}), s8[4194304]{0:T(1024)(128)(4,1)S(1)}, s32[]{:S(2)}) async-start(s8[7962624]{0:T(1024)(128)(4,1)} %bitcast.3), calls=%async_computation | async-start | bytes 8388608
  10.8 26.1 %collective-permute-start.15 = (bf16[128,1152]{1,0:T(8,128)(2,1)S(1)}, bf16[128,1152]{1,0:T(8,128)(2,1)S(1)}, u32[]{:S(2)}, u32[]{:S(2)}) collective-permute-start(bf16[128,1152]{1,0:T(8,128)(2,1)S(1)} %collective-permute-done.8.ours.mine), channel_id=1, source_target_pairs={{0,1},{1,0},{2,3},{3,2},{4,5},{5,4},{6,7},{7,6},{8,9},{9,8},{10,11... | collective-permute-start | bytes 884744 | tf_op jit(solution)/shard_map/ppermute | solution.py:305
  13.1 21.0 %collective-permute-start.1 = (bf16[128,1152]{1,0:T(8,128)(2,1)S(1)}, bf16[128,1152]{1,0:T(8,128)(2,1)S(1)}, u32[]{:S(2)}, u32[]{:S(2)}) collective-permute-start(bf16[128,1152]{1,0:T(8,128)(2,1)S(1)} %collective-permute-done.ours), channel_id=1, source_target_pairs={{2,4},{4,6},{3,1},{5,3},{10,12},{12,14},{11,9},{13,11},{18,20},{20... | collective-permute-start | bytes 884744 | tf_op jit(solution)/shard_map/ppermute | solution.py:304
  14.7 25.4 %collective-permute-start.10 = (bf16[128,1152]{1,0:T(8,128)(2,1)S(1)}, bf16[128,1152]{1,0:T(8,128)(2,1)S(1)}, u32[]{:S(2)}, u32[]{:S(2)}) collective-permute-start(bf16[128,1152]{1,0:T(8,128)(2,1)S(1)} %collective-permute-done.9.ours), channel_id=1, source_target_pairs={{4,6},{3,1},{12,14},{11,9},{20,22},{19,17},{28,30},{27,25}} | collective-permute-start | bytes 884744 | tf_op jit(solution)/shard_map/ppermute | solution.py:304
  15.4 19.4 %slice-start.1 = ((s8[7962624]{0:T(1024)(128)(4,1)}), s8[3768320]{0:T(1024)(128)(4,1)S(1)}, s32[]{:S(2)}) async-start(s8[7962624]{0:T(1024)(128)(4,1)} %bitcast.3), calls=%async_computation.1 | async-start | bytes 7536640
  15.5 19.4 %copy-start = (bf16[1,128,1152]{2,1,0:T(8,128)(2,1)S(1)}, bf16[1,128,1152]{2,1,0:T(8,128)(2,1)}, u32[]{:S(2)}) copy-start(bf16[1,128,1152]{2,1,0:T(8,128)(2,1)} %param.6) | copy-start | bytes 884740
  16.1 2.8 %collective-permute-start.5 = (f32[1,864]{1,0:T(1,128)S(1)}, f32[1,864]{1,0:T(1,128)S(1)}, u32[]{:S(2)}, u32[]{:S(2)}) collective-permute-start(f32[1,864]{1,0:T(1,128)S(1)} %get-tuple-element.15), channel_id=1, source_target_pairs={{0,8},{8,0},{16,24},{24,16},{1,9},{9,1},{17,25},{25,17},{2,10},{10... | collective-permute-start | bytes 10376 | tf_op jit(solution)/shard_map/ppermute | solution.py:257
  18.9 2.7 %collective-permute-start.6 = (f32[1,864]{1,0:T(1,128)S(1)}, f32[1,864]{1,0:T(1,128)S(1)}, u32[]{:S(2)}, u32[]{:S(2)}) collective-permute-start(f32[1,864]{1,0:T(1,128)S(1)} %get-tuple-element.16), channel_id=1, source_target_pairs={{0,16},{8,24},{16,0},{24,8},{1,17},{9,25},{17,1},{25,9},{2,18},{10... | collective-permute-start | bytes 10376 | tf_op jit(solution)/shard_map/ppermute | solution.py:257
  21.7 3.4 %collective-permute-start.7 = (f32[1,864]{1,0:T(1,128)S(1)}, f32[1,864]{1,0:T(1,128)S(1)}, u32[]{:S(2)}, u32[]{:S(2)}) collective-permute-start(f32[1,864]{1,0:T(1,128)S(1)} %get-tuple-element.17), channel_id=1, source_target_pairs={{0,24},{8,16},{16,8},{24,0},{1,25},{9,17},{17,9},{25,1},{2,26},{10... | collective-permute-start | bytes 10376 | tf_op jit(solution)/shard_map/ppermute | solution.py:257
  25.0 18.0 %collective-permute-start.14 = (bf16[128,1152]{1,0:T(8,128)(2,1)S(1)}, bf16[128,1152]{1,0:T(8,128)(2,1)S(1)}, u32[]{:S(2)}, u32[]{:S(2)}) collective-permute-start(bf16[128,1152]{1,0:T(8,128)(2,1)S(1)} %collective-permute-done.ours), channel_id=1, source_target_pairs={{0,1},{1,0},{2,3},{3,2},{4,5},{5,4},{6,7},{7,6},{8,9},{9,8},{10,11... | collective-permute-start | bytes 884744 | tf_op jit(solution)/shard_map/ppermute | solution.py:305
  34.1 10.9 %collective-permute-start.13 = (bf16[128,1152]{1,0:T(8,128)(2,1)S(1)}, bf16[128,1152]{1,0:T(8,128)(2,1)S(1)}, u32[]{:S(2)}, u32[]{:S(2)}) collective-permute-start(bf16[128,1152]{1,0:T(8,128)(2,1)S(1)} %collective-permute-done.9.ours), channel_id=1, source_target_pairs={{0,1},{1,0},{2,3},{3,2},{4,5},{5,4},{6,7},{7,6},{8,9},{9,8},{10,11... | collective-permute-start | bytes 884744 | tf_op jit(solution)/shard_map/ppermute | solution.py:305
  34.1 8.3 %collective-permute-start.2 = (bf16[128,1152]{1,0:T(8,128)(2,1)S(1)}, bf16[128,1152]{1,0:T(8,128)(2,1)S(1)}, u32[]{:S(2)}, u32[]{:S(2)}) collective-permute-start(bf16[128,1152]{1,0:T(8,128)(2,1)S(1)} %collective-permute-done.1.ours), channel_id=1, source_target_pairs={{4,6},{3,1},{12,14},{11,9},{20,22},{19,17},{28,30},{27,25}} | collective-permute-start | bytes 884744 | tf_op jit(solution)/shard_map/ppermute | solution.py:304
  34.8 3.3 %copy-start.1 = (s32[1,8]{1,0:T(1,128)S(1)}, s32[1,8]{1,0:T(1,128)}, u32[]{:S(2)}) copy-start(s32[1,8]{1,0:T(1,128)} %marks.11) | copy-start | bytes 100
  36.9 9.2 %collective-permute-start.12 = (bf16[128,1152]{1,0:T(8,128)(2,1)S(1)}, bf16[128,1152]{1,0:T(8,128)(2,1)S(1)}, u32[]{:S(2)}, u32[]{:S(2)}) collective-permute-start(bf16[128,1152]{1,0:T(8,128)(2,1)S(1)} %collective-permute-done.1.ours), channel_id=1, source_target_pairs={{0,1},{1,0},{2,3},{3,2},{4,5},{5,4},{6,7},{7,6},{8,9},{9,8},{10,11... | collective-permute-start | bytes 884744 | tf_op jit(solution)/shard_map/ppermute | solution.py:305
  40.2 7.1 %collective-permute-start.11 = (bf16[128,1152]{1,0:T(8,128)(2,1)S(1)}, bf16[128,1152]{1,0:T(8,128)(2,1)S(1)}, u32[]{:S(2)}, u32[]{:S(2)}) collective-permute-start(bf16[128,1152]{1,0:T(8,128)(2,1)S(1)} %collective-permute-done.10.ours), channel_id=1, source_target_pairs={{0,1},{1,0},{2,3},{3,2},{4,5},{5,4},{6,7},{7,6},{8,9},{9,8},{10,11... | collective-permute-start | bytes 884744 | tf_op jit(solution)/shard_map/ppermute | solution.py:305
  42.5 5.2 %collective-permute-start.3 = (bf16[128,1152]{1,0:T(8,128)(2,1)S(1)}, bf16[128,1152]{1,0:T(8,128)(2,1)S(1)}, u32[]{:S(2)}, u32[]{:S(2)}) collective-permute-start(bf16[128,1152]{1,0:T(8,128)(2,1)S(1)} %collective-permute-done.2.ours), channel_id=1, source_target_pairs={{0,1},{1,0},{2,3},{3,2},{4,5},{5,4},{6,7},{7,6},{8,9},{9,8},{10,11... | collective-permute-start | bytes 884744 | tf_op jit(solution)/shard_map/ppermute | solution.py:305
  47.7 6.3 %copy-start.2 = (bf16[1152,1152]{1,0:T(8,128)(2,1)S(1)}, bf16[1152,1152]{1,0:T(8,128)(2,1)}, u32[]{:S(2)}) copy-start(bf16[1152,1152]{1,0:T(8,128)(2,1)} %wo.1) | copy-start | bytes 7962628
  52.5 1.5 %collective-permute-start.16 = (bf16[128,640]{1,0:T(8,128)(2,1)S(1)}, bf16[128,640]{1,0:T(8,128)(2,1)S(1)}, u32[]{:S(2)}, u32[]{:S(2)}) collective-permute-start(bf16[128,640]{1,0:T(8,128)(2,1)S(1)} %get-tuple-element.22), channel_id=1, source_target_pairs={{0,1},{1,0},{2,3},{3,2},{4,5},{5,4},{6,7},{7,6},{8,9},{9,8},{10,11... | collective-permute-start | bytes 491528 | tf_op jit(solution)/shard_map/ppermute | solution.py:345

commit v5 on v4

--- a/solution.py
+++ b/solution.py
@@ -217,17 +217,30 @@
     def _():
         add_strips(ours, theirs, row, w, kv, normed, distance, count)
 
-    for strip in range(2):
-
-        @pl.when(marked[strip])
-        def _(strip=strip):
-            rows = pl.ds(strip * count, count)
-            group = scores.shape[0]
-            for head in range(0, HEADS // 2, group):
-                attend_heads(
-                    range(head, head + group), width // HEADS, width, core, query.at[rows],
-                    [kv.at[:, :wide]], [kv.at[:, wide:]], None, scores, probs, whole.at[rows],
-                )
+    def attend_rows(rows, height):
+        group = scores.shape[0]
+        for head in range(0, HEADS // 2, group):
+            attend_heads(
+                range(head, head + group), width // HEADS, width, core, query.at[rows],
+                [kv.at[:, :wide]], [kv.at[:, wide:]], None,
+                scores.at[:, pl.ds(0, height)], probs.at[:, pl.ds(0, height)], whole.at[rows],
+            )
+
+    if scores.shape[1] > count:
+
+        @pl.when(marked[0] & marked[1])
+        def _():
+            attend_rows(pl.ds(0, 2 * count), 2 * count)
+
+        @pl.when(marked[0] != marked[1])
+        def _():
+            attend_rows(pl.ds(pl.multiple_of(jnp.where(marked[0], 0, count), count), count), count)
+    else:
+        for strip in range(2):
+
+            @pl.when(marked[strip])
+            def _(strip=strip):
+                attend_rows(pl.ds(strip * count, count), count)
 
     ours = pl.ds(pl.multiple_of(count * core, count), count)
     others = pl.ds(pl.multiple_of(count * (1 - core), count), count)
@@ -330,17 +343,18 @@
             (mine[at], theirs[at], row, detail, kv, w_project), 12, {} if at == 0 else {4: 0},
         )
     group = max(1, min(HEADS // 2, 2**20 // (count * tokens)))
+    height = 2 * count if group == HEADS // 2 else count
     _, keep, send = call(
         functools.partial(late_kernel, distance=depth),
         [kv_out] + [((count, wide), BF16)] * 2,
         pair_scratch
         + [
             pltpu.VMEM((2 * count, wide), F32),
-            pltpu.VMEM((group, count, tokens), F32),
-            pltpu.VMEM((group, count, tokens), BF16),
+            pltpu.VMEM((group, height, tokens), F32),
+            pltpu.VMEM((group, height, tokens), BF16),
         ],
         [vmem] * 8, 10**9,
-        (mine[-1], theirs[-1], row, detail, query, kv, near, w_project), 22, {5: 0},
+        (mine[-1], theirs[-1], row, detail, query, kv, near, w_project), 30 if height > count else 22, {5: 0},
     )
     got = lax.ppermute(send, "tile", swap)
     (updated,) = call(

time: 55.5 us -> 54.5 us (0.982)
  Pallas kernels: 17.6 us -> 16.6 us
    pallas_call x11, Pallas kernels: 17.6 us -> 16.6 us  [call(): pl.pallas_call(kernel, out_shape=[jax.ShapeDtypeStruct(shape, dtype) for...]
where the time goes in v5:
time: 54.5 us; the launch traced here: 54.3 us
  starting transfers between devices  29.2 us (54%)
  Pallas kernels  16.6 us (30%)
  waiting for transfers between devices  8.17 us (15%)
    pallas_call x11, Pallas kernels, call(): pl.pallas_call(kernel, out_shape=[jax.ShapeDtypeStruct(shape, dtype) for...  16.6 us
    ppermute x6, starting transfers between devices, on_device(): theirs = [lax.ppermute(strip, 'tile', swap) for strip in mine]  13.3 us
    ppermute x4, starting transfers between devices, on_device(): mine.append(lax.ppermute(mine[step - 2], 'tile', along(step // 2 + 1)))  5.05 us
    ppermute x3, starting transfers between devices, exchange_modulation(): pieces.append(lax.ppermute(rows[bits], 'grp', pairs))  4.67 us
    ppermute x3, waiting for transfers between devices, exchange_modulation(): pieces.append(lax.ppermute(rows[bits], 'grp', pairs))  4.23 us
    ppermute x1, starting transfers between devices, on_device(): lax.ppermute(own, 'tile', cross)  3.89 us
    ppermute x1, waiting for transfers between devices, on_device(): lax.ppermute(own, 'tile', cross)  2.59 us
    ppermute x1, starting transfers between devices, on_device(): lax.ppermute(own, 'tile', along(1))  2.08 us
  transfers between devices with their start and end apart: 17, of which 5 were waited for; matrix products, arithmetic and copies ran while one was open for 0% of the time, Pallas kernels for 21%

profile of v5, /device:TPU:17, one launch (start us, length us, event | category | flops | bytes accessed | tf_op | source)
XLA Modules:
  0.0 54.3 jit_solution(10488047574430210173)
XLA Ops:
  0.0 0.0 copy-start.3
  0.0 0.0 copy-start.4
  0.0 3.9 %collective-permute-start.8 = (bf16[128,1152]{1,0:T(8,128)(2,1)}, bf16[128,1152]{1,0:T(8,128)(2,1)S(1)}, u32[]{:S(2)}, u32[]{:S(2)}) collective-permute-start(bf16[128,1152]{1,0:T(8,128)(2,1)} %bitcast.5), channel_id=1, source_target_pairs={{1,2},{3,4},{5,6},{2,1},{4,3},{6,5},{9,10},{11,12},{13,14},{10,9},... | collective-permute-start | bytes 884744 | tf_op jit(solution)/shard_map/ppermute | solution.py:307
  3.9 0.1 collective-permute-start.4
  4.0 2.1 %collective-permute-start = (bf16[128,1152]{1,0:T(8,128)(2,1)}, bf16[128,1152]{1,0:T(8,128)(2,1)S(1)}, u32[]{:S(2)}, u32[]{:S(2)}) collective-permute-start(bf16[128,1152]{1,0:T(8,128)(2,1)} %bitcast.7), channel_id=1, source_target_pairs={{0,2},{2,4},{4,6},{3,1},{5,3},{7,5},{8,10},{10,12},{12,14},{11,9},... | collective-permute-start | bytes 884744 | tf_op jit(solution)/shard_map/ppermute | solution.py:307
  6.1 2.6 %collective-permute-done.8.ours.mine = bf16[128,1152]{1,0:T(8,128)(2,1)S(1)} collective-permute-done((bf16[128,1152]{1,0:T(8,128)(2,1)}, bf16[128,1152]{1,0:T(8,128)(2,1)S(1)}, u32[]{:S(2)}, u32[]{:S(2)}) %collective-permute-start.8) | collective-permute-done | bytes 294944 | tf_op jit(solution)/shard_map/ppermute | solution.py:307
  8.7 2.1 %collective-permute-start.9 = (bf16[128,1152]{1,0:T(8,128)(2,1)S(1)}, bf16[128,1152]{1,0:T(8,128)(2,1)S(1)}, u32[]{:S(2)}, u32[]{:S(2)}) collective-permute-start(bf16[128,1152]{1,0:T(8,128)(2,1)S(1)} %collective-permute-done.8.ours.mine), channel_id=1, source_target_pairs={{2,4},{4,6},{3,1},{5,3},{10,12},{12,14},{11,9},{13,11},{18,20},{20... | collective-permute-start | bytes 884744 | tf_op jit(solution)/shard_map/ppermute | solution.py:317
  10.7 0.0 slice-start
  10.8 2.3 %collective-permute-start.15 = (bf16[128,1152]{1,0:T(8,128)(2,1)S(1)}, bf16[128,1152]{1,0:T(8,128)(2,1)S(1)}, u32[]{:S(2)}, u32[]{:S(2)}) collective-permute-start(bf16[128,1152]{1,0:T(8,128)(2,1)S(1)} %collective-permute-done.8.ours.mine), channel_id=1, source_target_pairs={{0,1},{1,0},{2,3},{3,2},{4,5},{5,4},{6,7},{7,6},{8,9},{9,8},{10,11... | collective-permute-start | bytes 884744 | tf_op jit(solution)/shard_map/ppermute | solution.py:318
  13.1 0.0 collective-permute-done.ours
  13.1 1.6 %collective-permute-start.1 = (bf16[128,1152]{1,0:T(8,128)(2,1)S(1)}, bf16[128,1152]{1,0:T(8,128)(2,1)S(1)}, u32[]{:S(2)}, u32[]{:S(2)}) collective-permute-start(bf16[128,1152]{1,0:T(8,128)(2,1)S(1)} %collective-permute-done.ours), channel_id=1, source_target_pairs={{2,4},{4,6},{3,1},{5,3},{10,12},{12,14},{11,9},{13,11},{18,20},{20... | collective-permute-start | bytes 884744 | tf_op jit(solution)/shard_map/ppermute | solution.py:317
  14.7 0.0 collective-permute-done.9.ours
  14.7 0.7 %collective-permute-start.10 = (bf16[128,1152]{1,0:T(8,128)(2,1)S(1)}, bf16[128,1152]{1,0:T(8,128)(2,1)S(1)}, u32[]{:S(2)}, u32[]{:S(2)}) collective-permute-start(bf16[128,1152]{1,0:T(8,128)(2,1)S(1)} %collective-permute-done.9.ours), channel_id=1, source_target_pairs={{4,6},{3,1},{12,14},{11,9},{20,22},{19,17},{28,30},{27,25}} | collective-permute-start | bytes 884744 | tf_op jit(solution)/shard_map/ppermute | solution.py:317
  15.4 0.0 copy-done.3
  15.4 0.0 copy-done.4
  15.4 0.0 slice-start.1
  15.5 0.0 copy-start
  15.5 0.7 %shard_map.65 = (f32[1,864]{1,0:T(1,128)S(1)}, f32[1,864]{1,0:T(1,128)S(1)}, f32[1,864]{1,0:T(1,128)S(1)}, f32[1,864]{1,0:T(1,128)S(1)}) custom-call(bf16[4,1152]{1,0:T(4,128)(2,1)S(1)} %copy-done.4, bf16[864,1152]{1,0:T(8,128)(2,1)S(1)} %bitcast.10, f32[8,128]{1,0:T(8,128)S(1)} %shard_map.64._), custom_call_target="tpu_custom_call" | custom-call | flops 10000000000 | bytes 50000000 | tf_op jit(solution)/shard_map/pallas_call | solution.py:275
  16.1 1.3 %collective-permute-start.5 = (f32[1,864]{1,0:T(1,128)S(1)}, f32[1,864]{1,0:T(1,128)S(1)}, u32[]{:S(2)}, u32[]{:S(2)}) collective-permute-start(f32[1,864]{1,0:T(1,128)S(1)} %get-tuple-element.15), channel_id=1, source_target_pairs={{0,8},{8,0},{16,24},{24,16},{1,9},{9,1},{17,25},{25,17},{2,10},{10... | collective-permute-start | bytes 10376 | tf_op jit(solution)/shard_map/ppermute | solution.py:270
  17.4 1.5 %collective-permute-done.5.rest_1_ = f32[1,864]{1,0:T(1,128)S(1)} collective-permute-done((f32[1,864]{1,0:T(1,128)S(1)}, f32[1,864]{1,0:T(1,128)S(1)}, u32[]{:S(2)}, u32[]{:S(2)}) %collective-permute-start.5) | collective-permute-done | bytes 3488 | tf_op jit(solution)/shard_map/ppermute | solution.py:270
  18.9 1.2 %collective-permute-start.6 = (f32[1,864]{1,0:T(1,128)S(1)}, f32[1,864]{1,0:T(1,128)S(1)}, u32[]{:S(2)}, u32[]{:S(2)}) collective-permute-start(f32[1,864]{1,0:T(1,128)S(1)} %get-tuple-element.16), channel_id=1, source_target_pairs={{0,16},{8,24},{16,0},{24,8},{1,17},{9,25},{17,1},{25,9},{2,18},{10... | collective-permute-start | bytes 10376 | tf_op jit(solution)/shard_map/ppermute | solution.py:270
  20.2 1.5 %collective-permute-done.6.rest_2_ = f32[1,864]{1,0:T(1,128)S(1)} collective-permute-done((f32[1,864]{1,0:T(1,128)S(1)}, f32[1,864]{1,0:T(1,128)S(1)}, u32[]{:S(2)}, u32[]{:S(2)}) %collective-permute-start.6) | collective-permute-done | bytes 3488 | tf_op jit(solution)/shard_map/ppermute | solution.py:270
  21.7 2.2 %collective-permute-start.7 = (f32[1,864]{1,0:T(1,128)S(1)}, f32[1,864]{1,0:T(1,128)S(1)}, u32[]{:S(2)}, u32[]{:S(2)}) collective-permute-start(f32[1,864]{1,0:T(1,128)S(1)} %get-tuple-element.17), channel_id=1, source_target_pairs={{0,24},{8,16},{16,8},{24,0},{1,25},{9,17},{17,9},{25,1},{2,26},{10... | collective-permute-start | bytes 10376 | tf_op jit(solution)/shard_map/ppermute | solution.py:270
  23.9 1.2 %collective-permute-done.7.rest_3_ = f32[1,864]{1,0:T(1,128)S(1)} collective-permute-done((f32[1,864]{1,0:T(1,128)S(1)}, f32[1,864]{1,0:T(1,128)S(1)}, u32[]{:S(2)}, u32[]{:S(2)}) %collective-permute-start.7) | collective-permute-done | bytes 3488 | tf_op jit(solution)/shard_map/ppermute | solution.py:270
  25.0 9.1 %collective-permute-start.14 = (bf16[128,1152]{1,0:T(8,128)(2,1)S(1)}, bf16[128,1152]{1,0:T(8,128)(2,1)S(1)}, u32[]{:S(2)}, u32[]{:S(2)}) collective-permute-start(bf16[128,1152]{1,0:T(8,128)(2,1)S(1)} %collective-permute-done.ours), channel_id=1, source_target_pairs={{0,1},{1,0},{2,3},{3,2},{4,5},{5,4},{6,7},{7,6},{8,9},{9,8},{10,11... | collective-permute-start | bytes 884744 | tf_op jit(solution)/shard_map/ppermute | solution.py:318
  34.1 0.0 collective-permute-done.4.partner
  34.1 0.0 collective-permute-start.13
  34.1 0.0 collective-permute-done.1.ours
  34.1 0.7 %collective-permute-start.2 = (bf16[128,1152]{1,0:T(8,128)(2,1)S(1)}, bf16[128,1152]{1,0:T(8,128)(2,1)S(1)}, u32[]{:S(2)}, u32[]{:S(2)}) collective-permute-start(bf16[128,1152]{1,0:T(8,128)(2,1)S(1)} %collective-permute-done.1.ours), channel_id=1, source_target_pairs={{4,6},{3,1},{12,14},{11,9},{20,22},{19,17},{28,30},{27,25}} | collective-permute-start | bytes 884744 | tf_op jit(solution)/shard_map/ppermute | solution.py:317
  34.8 0.0 slice-done
  34.8 0.0 slice-done.1
  34.8 0.0 copy-done
  34.8 0.0 copy-start.1
  34.9 2.1 %shard_map.66 = (bf16[256,640]{1,0:T(8,128)(2,1)S(1)}, bf16[256,1280]{1,0:T(8,128)(2,1)S(1)}, f32[1,3456]{1,0:T(1,128)S(1)}) custom-call(bf16[128,1152]{1,0:T(8,128)(2,1)S(1)} %bitcast.8, bf16[128,1152]{1,0:T(8,128)(2,1)S(1)} %collective-permute-done.4.partner, f32[1,864]{1,0:T(1,128)S(1)} %get-tuple-element.14.rest_0_, ...), custom_call_target="tpu_custom_call" | custom-call | flops 2000000000 | bytes 10000000 | tf_op jit(solution)/shard_map/pallas_call | solution.py:275
  36.9 0.0 collective-permute-done.15.theirs
  36.9 1.2 %collective-permute-start.12 = (bf16[128,1152]{1,0:T(8,128)(2,1)S(1)}, bf16[128,1152]{1,0:T(8,128)(2,1)S(1)}, u32[]{:S(2)}, u32[]{:S(2)}) collective-permute-start(bf16[128,1152]{1,0:T(8,128)(2,1)S(1)} %collective-permute-done.1.ours), channel_id=1, source_target_pairs={{0,1},{1,0},{2,3},{3,2},{4,5},{5,4},{6,7},{7,6},{8,9},{9,8},{10,11... | collective-permute-start | bytes 884744 | tf_op jit(solution)/shard_map/ppermute | solution.py:318
  38.1 0.0 copy-done.1
  38.1 2.0 %shard_map.67.before = bf16[1024,1280]{1,0:T(8,128)(2,1)S(1)} custom-call(bf16[128,1152]{1,0:T(8,128)(2,1)S(1)} %collective-permute-done.8.ours.mine, bf16[128,1152]{1,0:T(8,128)(2,1)S(1)} %collective-permute-done.15.theirs, f32[1,3456]{1,0:T(1,128)S(1)} %get-tuple-element.18.row, s32[1,8]{1,0:T(1,128)S(1)} %copy-done.1, ...), custom_call_target="tpu_custom_call" | custom-call | flops 1000000000 | bytes 5000000 | tf_op jit(solution)/shard_map/pallas_call | solution.py:275
  40.2 0.0 collective-permute-done.10.ours
  40.2 0.1 collective-permute-start.11
  40.3 2.2 %shard_map.72.near = f32[256,640]{1,0:T(8,128)S(1)} custom-call(bf16[128,1152]{1,0:T(8,128)(2,1)S(1)} %collective-permute-done.8.ours.mine, bf16[128,1152]{1,0:T(8,128)(2,1)S(1)} %collective-permute-done.15.theirs, f32[1,3456]{1,0:T(1,128)S(1)} %get-tuple-element.18.row, bf16[256,640]{1,0:T(8,128)(2,1)S(1)} %get-tuple-element.19.query, ...), custom_call_target="tpu_custom_call" | custom-call | flops 1000000000 | bytes 5000000 | tf_op jit(solution)/shard_map/pallas_call | solution.py:275
  42.5 0.0 collective-permute-done.2.ours
  42.5 0.5 %collective-permute-start.3 = (bf16[128,1152]{1,0:T(8,128)(2,1)S(1)}, bf16[128,1152]{1,0:T(8,128)(2,1)S(1)}, u32[]{:S(2)}, u32[]{:S(2)}) collective-permute-start(bf16[128,1152]{1,0:T(8,128)(2,1)S(1)} %collective-permute-done.2.ours), channel_id=1, source_target_pairs={{0,1},{1,0},{2,3},{3,2},{4,5},{5,4},{6,7},{7,6},{8,9},{9,8},{10,11... | collective-permute-start | bytes 884744 | tf_op jit(solution)/shard_map/ppermute | solution.py:318
  43.0 0.0 collective-permute-done.14.theirs
  43.0 2.0 %shard_map.68.before = bf16[1024,1280]{1,0:T(8,128)(2,1)S(1)} custom-call(bf16[128,1152]{1,0:T(8,128)(2,1)S(1)} %collective-permute-done.ours, bf16[128,1152]{1,0:T(8,128)(2,1)S(1)} %collective-permute-done.14.theirs, f32[1,3456]{1,0:T(1,128)S(1)} %get-tuple-element.18.row, s32[1,8]{1,0:T(1,128)S(1)} %copy-done.1, ...), custom_call_target="tpu_custom_call", output_to_operand_aliasing={{}: (4, {})} | custom-call | flops 1000000000 | bytes 5000000 | tf_op jit(solution)/shard_map/pallas_call | solution.py:275
  45.0 0.0 collective-permute-done.13.theirs
  45.0 1.1 %shard_map.69.before = bf16[1024,1280]{1,0:T(8,128)(2,1)S(1)} custom-call(bf16[128,1152]{1,0:T(8,128)(2,1)S(1)} %collective-permute-done.9.ours, bf16[128,1152]{1,0:T(8,128)(2,1)S(1)} %collective-permute-done.13.theirs, f32[1,3456]{1,0:T(1,128)S(1)} %get-tuple-element.18.row, s32[1,8]{1,0:T(1,128)S(1)} %copy-done.1, ...), custom_call_target="tpu_custom_call", output_to_operand_aliasing={{}: (4, {})} | custom-call | flops 1000000000 | bytes 5000000 | tf_op jit(solution)/shard_map/pallas_call | solution.py:275
  46.2 0.0 collective-permute-done.12.theirs
  46.2 1.1 %shard_map.70.before = bf16[1024,1280]{1,0:T(8,128)(2,1)S(1)} custom-call(bf16[128,1152]{1,0:T(8,128)(2,1)S(1)} %collective-permute-done.1.ours, bf16[128,1152]{1,0:T(8,128)(2,1)S(1)} %collective-permute-done.12.theirs, f32[1,3456]{1,0:T(1,128)S(1)} %get-tuple-element.18.row, s32[1,8]{1,0:T(1,128)S(1)} %copy-done.1, ...), custom_call_target="tpu_custom_call", output_to_operand_aliasing={{}: (4, {})} | custom-call | flops 1000000000 | bytes 5000000 | tf_op jit(solution)/shard_map/pallas_call | solution.py:275
  47.3 0.0 collective-permute-done.11.theirs
  47.3 0.4 shard_map.71.before
  47.7 0.0 copy-start.2
  47.7 0.0 collective-permute-done.3.theirs
  47.7 3.8 %shard_map.73 = (bf16[1024,1280]{1,0:T(8,128)(2,1)S(1)}, bf16[128,640]{1,0:T(8,128)(2,1)S(1)}, bf16[128,640]{1,0:T(8,128)(2,1)S(1)}) custom-call(bf16[128,1152]{1,0:T(8,128)(2,1)S(1)} %collective-permute-done.2.ours, bf16[128,1152]{1,0:T(8,128)(2,1)S(1)} %collective-permute-done.3.theirs, ...), custom_call_target="tpu_custom_call", output_to_operand_aliasing={{0}: (5, {})} | custom-call | flops 1000000000 | bytes 5000000 | tf_op jit(solution)/shard_map/pallas_call | solution.py:275
  51.5 0.1 collective-permute-start.16
  51.6 1.3 %collective-permute-done.16.got = bf16[128,640]{1,0:T(8,128)(2,1)S(1)} collective-permute-done((bf16[128,640]{1,0:T(8,128)(2,1)S(1)}, bf16[128,640]{1,0:T(8,128)(2,1)S(1)}, u32[]{:S(2)}, u32[]{:S(2)}) %collective-permute-start.16) | collective-permute-done | bytes 163872 | tf_op jit(solution)/shard_map/ppermute | solution.py:359
  53.0 0.0 copy-done.2
  53.0 1.3 %shard_map.74 = bf16[128,1152]{1,0:T(8,128)(2,1)} custom-call(bf16[128,1152]{1,0:T(8,128)(2,1)S(1)} %bitcast.9, bf16[128,640]{1,0:T(8,128)(2,1)S(1)} %get-tuple-element.21.keep, bf16[128,640]{1,0:T(8,128)(2,1)S(1)} %collective-permute-done.16.got, f32[1,3456]{1,0:T(1,128)S(1)} %get-tuple-element.18.row, bf16[1152,1152]{1,0:T(8,128)(2,1)S(1)} %copy-done.2), custom_call_target="tpu_custom_call" | custom-call | flops 1000000000 | bytes 5000000 | tf_op jit(solution)/shard_map/pallas_call | solution.py:275
  (2 shorter events, 0.0 us)
Async XLA Ops:
  0.0 15.4 %copy-start.3 = (bf16[1152,864]{0,1:T(8,128)(2,1)S(1)}, bf16[1152,864]{0,1:T(8,128)(2,1)}, u32[]{:S(2)}) copy-start(bf16[1152,864]{0,1:T(8,128)(2,1)} %param.8) | copy-start | bytes 5971972
  0.0 15.4 %copy-start.4 = (bf16[4,1152]{1,0:T(4,128)(2,1)S(1)}, bf16[4,1152]{1,0:T(4,128)(2,1)}, u32[]{:S(2)}) copy-start(bf16[4,1152]{1,0:T(4,128)(2,1)} %condition.1) | copy-start | bytes 27652
  0.0 8.7 %collective-permute-start.8 = (bf16[128,1152]{1,0:T(8,128)(2,1)}, bf16[128,1152]{1,0:T(8,128)(2,1)S(1)}, u32[]{:S(2)}, u32[]{:S(2)}) collective-permute-start(bf16[128,1152]{1,0:T(8,128)(2,1)} %bitcast.5), channel_id=1, source_target_pairs={{1,2},{3,4},{5,6},{2,1},{4,3},{6,5},{9,10},{11,12},{13,14},{10,9},... | collective-permute-start | bytes 884744 | tf_op jit(solution)/shard_map/ppermute | solution.py:307
  3.9 30.2 %collective-permute-start.4 = (bf16[128,1152]{1,0:T(8,128)(2,1)}, bf16[128,1152]{1,0:T(8,128)(2,1)S(1)}, u32[]{:S(2)}, u32[]{:S(2)}) collective-permute-start(bf16[128,1152]{1,0:T(8,128)(2,1)} %bitcast.6), channel_id=1, source_target_pairs={{0,1},{1,0},{2,3},{3,2},{4,5},{5,4},{6,7},{7,6},{8,9},{9,8},{10,11... | collective-permute-start | bytes 884744 | tf_op jit(solution)/shard_map/ppermute | solution.py:308
  4.0 9.1 %collective-permute-start = (bf16[128,1152]{1,0:T(8,128)(2,1)}, bf16[128,1152]{1,0:T(8,128)(2,1)S(1)}, u32[]{:S(2)}, u32[]{:S(2)}) collective-permute-start(bf16[128,1152]{1,0:T(8,128)(2,1)} %bitcast.7), channel_id=1, source_target_pairs={{0,2},{2,4},{4,6},{3,1},{5,3},{7,5},{8,10},{10,12},{12,14},{11,9},... | collective-permute-start | bytes 884744 | tf_op jit(solution)/shard_map/ppermute | solution.py:307
  8.7 6.1 %collective-permute-start.9 = (bf16[128,1152]{1,0:T(8,128)(2,1)S(1)}, bf16[128,1152]{1,0:T(8,128)(2,1)S(1)}, u32[]{:S(2)}, u32[]{:S(2)}) collective-permute-start(bf16[128,1152]{1,0:T(8,128)(2,1)S(1)} %collective-permute-done.8.ours.mine), channel_id=1, source_target_pairs={{2,4},{4,6},{3,1},{5,3},{10,12},{12,14},{11,9},{13,11},{18,20},{20... | collective-permute-start | bytes 884744 | tf_op jit(solution)/shard_map/ppermute | solution.py:317
  10.7 24.1 %slice-start = ((s8[7962624]{0:T(1024)(128)(4,1)}), s8[4194304]{0:T(1024)(128)(4,1)S(1)}, s32[]{:S(2)}) async-start(s8[7962624]{0:T(1024)(128)(4,1)} %bitcast.3), calls=%async_computation | async-start | bytes 8388608
  10.8 26.1 %collective-permute-start.15 = (bf16[128,1152]{1,0:T(8,128)(2,1)S(1)}, bf16[128,1152]{1,0:T(8,128)(2,1)S(1)}, u32[]{:S(2)}, u32[]{:S(2)}) collective-permute-start(bf16[128,1152]{1,0:T(8,128)(2,1)S(1)} %collective-permute-done.8.ours.mine), channel_id=1, source_target_pairs={{0,1},{1,0},{2,3},{3,2},{4,5},{5,4},{6,7},{7,6},{8,9},{9,8},{10,11... | collective-permute-start | bytes 884744 | tf_op jit(solution)/shard_map/ppermute | solution.py:318
  13.1 21.0 %collective-permute-start.1 = (bf16[128,1152]{1,0:T(8,128)(2,1)S(1)}, bf16[128,1152]{1,0:T(8,128)(2,1)S(1)}, u32[]{:S(2)}, u32[]{:S(2)}) collective-permute-start(bf16[128,1152]{1,0:T(8,128)(2,1)S(1)} %collective-permute-done.ours), channel_id=1, source_target_pairs={{2,4},{4,6},{3,1},{5,3},{10,12},{12,14},{11,9},{13,11},{18,20},{20... | collective-permute-start | bytes 884744 | tf_op jit(solution)/shard_map/ppermute | solution.py:317
  14.7 25.4 %collective-permute-start.10 = (bf16[128,1152]{1,0:T(8,128)(2,1)S(1)}, bf16[128,1152]{1,0:T(8,128)(2,1)S(1)}, u32[]{:S(2)}, u32[]{:S(2)}) collective-permute-start(bf16[128,1152]{1,0:T(8,128)(2,1)S(1)} %collective-permute-done.9.ours), channel_id=1, source_target_pairs={{4,6},{3,1},{12,14},{11,9},{20,22},{19,17},{28,30},{27,25}} | collective-permute-start | bytes 884744 | tf_op jit(solution)/shard_map/ppermute | solution.py:317
  15.4 19.4 %slice-start.1 = ((s8[7962624]{0:T(1024)(128)(4,1)}), s8[3768320]{0:T(1024)(128)(4,1)S(1)}, s32[]{:S(2)}) async-start(s8[7962624]{0:T(1024)(128)(4,1)} %bitcast.3), calls=%async_computation.1 | async-start | bytes 7536640
  15.5 19.4 %copy-start = (bf16[1,128,1152]{2,1,0:T(8,128)(2,1)S(1)}, bf16[1,128,1152]{2,1,0:T(8,128)(2,1)}, u32[]{:S(2)}) copy-start(bf16[1,128,1152]{2,1,0:T(8,128)(2,1)} %param.6) | copy-start | bytes 884740
  16.1 2.8 %collective-permute-start.5 = (f32[1,864]{1,0:T(1,128)S(1)}, f32[1,864]{1,0:T(1,128)S(1)}, u32[]{:S(2)}, u32[]{:S(2)}) collective-permute-start(f32[1,864]{1,0:T(1,128)S(1)} %get-tuple-element.15), channel_id=1, source_target_pairs={{0,8},{8,0},{16,24},{24,16},{1,9},{9,1},{17,25},{25,17},{2,10},{10... | collective-permute-start | bytes 10376 | tf_op jit(solution)/shard_map/ppermute | solution.py:270
  18.9 2.7 %collective-permute-start.6 = (f32[1,864]{1,0:T(1,128)S(1)}, f32[1,864]{1,0:T(1,128)S(1)}, u32[]{:S(2)}, u32[]{:S(2)}) collective-permute-start(f32[1,864]{1,0:T(1,128)S(1)} %get-tuple-element.16), channel_id=1, source_target_pairs={{0,16},{8,24},{16,0},{24,8},{1,17},{9,25},{17,1},{25,9},{2,18},{10... | collective-permute-start | bytes 10376 | tf_op jit(solution)/shard_map/ppermute | solution.py:270
  21.7 3.4 %collective-permute-start.7 = (f32[1,864]{1,0:T(1,128)S(1)}, f32[1,864]{1,0:T(1,128)S(1)}, u32[]{:S(2)}, u32[]{:S(2)}) collective-permute-start(f32[1,864]{1,0:T(1,128)S(1)} %get-tuple-element.17), channel_id=1, source_target_pairs={{0,24},{8,16},{16,8},{24,0},{1,25},{9,17},{17,9},{25,1},{2,26},{10... | collective-permute-start | bytes 10376 | tf_op jit(solution)/shard_map/ppermute | solution.py:270
  25.0 18.0 %collective-permute-start.14 = (bf16[128,1152]{1,0:T(8,128)(2,1)S(1)}, bf16[128,1152]{1,0:T(8,128)(2,1)S(1)}, u32[]{:S(2)}, u32[]{:S(2)}) collective-permute-start(bf16[128,1152]{1,0:T(8,128)(2,1)S(1)} %collective-permute-done.ours), channel_id=1, source_target_pairs={{0,1},{1,0},{2,3},{3,2},{4,5},{5,4},{6,7},{7,6},{8,9},{9,8},{10,11... | collective-permute-start | bytes 884744 | tf_op jit(solution)/shard_map/ppermute | solution.py:318
  34.1 10.9 %collective-permute-start.13 = (bf16[128,1152]{1,0:T(8,128)(2,1)S(1)}, bf16[128,1152]{1,0:T(8,128)(2,1)S(1)}, u32[]{:S(2)}, u32[]{:S(2)}) collective-permute-start(bf16[128,1152]{1,0:T(8,128)(2,1)S(1)} %collective-permute-done.9.ours), channel_id=1, source_target_pairs={{0,1},{1,0},{2,3},{3,2},{4,5},{5,4},{6,7},{7,6},{8,9},{9,8},{10,11... | collective-permute-start | bytes 884744 | tf_op jit(solution)/shard_map/ppermute | solution.py:318
  34.1 8.4 %collective-permute-start.2 = (bf16[128,1152]{1,0:T(8,128)(2,1)S(1)}, bf16[128,1152]{1,0:T(8,128)(2,1)S(1)}, u32[]{:S(2)}, u32[]{:S(2)}) collective-permute-start(bf16[128,1152]{1,0:T(8,128)(2,1)S(1)} %collective-permute-done.1.ours), channel_id=1, source_target_pairs={{4,6},{3,1},{12,14},{11,9},{20,22},{19,17},{28,30},{27,25}} | collective-permute-start | bytes 884744 | tf_op jit(solution)/shard_map/ppermute | solution.py:317
  34.8 3.3 %copy-start.1 = (s32[1,8]{1,0:T(1,128)S(1)}, s32[1,8]{1,0:T(1,128)}, u32[]{:S(2)}) copy-start(s32[1,8]{1,0:T(1,128)} %marks.11) | copy-start | bytes 100
  36.9 9.2 %collective-permute-start.12 = (bf16[128,1152]{1,0:T(8,128)(2,1)S(1)}, bf16[128,1152]{1,0:T(8,128)(2,1)S(1)}, u32[]{:S(2)}, u32[]{:S(2)}) collective-permute-start(bf16[128,1152]{1,0:T(8,128)(2,1)S(1)} %collective-permute-done.1.ours), channel_id=1, source_target_pairs={{0,1},{1,0},{2,3},{3,2},{4,5},{5,4},{6,7},{7,6},{8,9},{9,8},{10,11... | collective-permute-start | bytes 884744 | tf_op jit(solution)/shard_map/ppermute | solution.py:318
  40.2 7.1 %collective-permute-start.11 = (bf16[128,1152]{1,0:T(8,128)(2,1)S(1)}, bf16[128,1152]{1,0:T(8,128)(2,1)S(1)}, u32[]{:S(2)}, u32[]{:S(2)}) collective-permute-start(bf16[128,1152]{1,0:T(8,128)(2,1)S(1)} %collective-permute-done.10.ours), channel_id=1, source_target_pairs={{0,1},{1,0},{2,3},{3,2},{4,5},{5,4},{6,7},{7,6},{8,9},{9,8},{10,11... | collective-permute-start | bytes 884744 | tf_op jit(solution)/shard_map/ppermute | solution.py:318
  42.5 5.3 %collective-permute-start.3 = (bf16[128,1152]{1,0:T(8,128)(2,1)S(1)}, bf16[128,1152]{1,0:T(8,128)(2,1)S(1)}, u32[]{:S(2)}, u32[]{:S(2)}) collective-permute-start(bf16[128,1152]{1,0:T(8,128)(2,1)S(1)} %collective-permute-done.2.ours), channel_id=1, source_target_pairs={{0,1},{1,0},{2,3},{3,2},{4,5},{5,4},{6,7},{7,6},{8,9},{9,8},{10,11... | collective-permute-start | bytes 884744 | tf_op jit(solution)/shard_map/ppermute | solution.py:318
  47.7 5.2 %copy-start.2 = (bf16[1152,1152]{1,0:T(8,128)(2,1)S(1)}, bf16[1152,1152]{1,0:T(8,128)(2,1)}, u32[]{:S(2)}) copy-start(bf16[1152,1152]{1,0:T(8,128)(2,1)} %wo.1) | copy-start | bytes 7962628
  51.5 1.5 %collective-permute-start.16 = (bf16[128,640]{1,0:T(8,128)(2,1)S(1)}, bf16[128,640]{1,0:T(8,128)(2,1)S(1)}, u32[]{:S(2)}, u32[]{:S(2)}) collective-permute-start(bf16[128,640]{1,0:T(8,128)(2,1)S(1)} %get-tuple-element.22), channel_id=1, source_target_pairs={{0,1},{1,0},{2,3},{3,2},{4,5},{5,4},{6,7},{7,6},{8,9},{9,8},{10,11... | collective-permute-start | bytes 491528 | tf_op jit(solution)/shard_map/ppermute | solution.py:359
